TPU v7x, 32 devices: a whole 2x2x4 slice. The times are simulated.
32 devices in a mesh: groups: 2 (over y), pages: 4 (over z), heads: 4 (over x, core).
Axes of the slice: x: 2, y: 2, z: 4, core: 2. Of those that a mesh axis runs over, the one named last changes fastest.
Arguments:
- q_nope: bfloat16 [256, 16384], P(('groups', 'pages'), 'heads'), parts along dimension 0, may hold values from -6 to 6
- q_rope: bfloat16 [256, 8192], P(('groups', 'pages'), 'heads'), parts along dimension 0, may hold values from -16 to 16
- cache_tiles: bfloat16 [12288, 576], P(('groups', 'pages')), parts along dimension 0, may hold values from -8 to 8
- absorb_keys: bfloat16 [128, 128, 512], P('heads'), may hold values from -0.5 to 0.5
- absorb_values: bfloat16 [128, 512, 128], P('heads'), may hold values from -2 to 2
- page_counts: int32 [8], P('groups'), parts along dimension 0, may hold values from 1 to 24, as said below
- query_token: int32 [256], P('groups'), parts along dimension 0, may hold values from 0 to 127, each once
- query_offsets: int32 [256], P('groups'), parts along dimension 0, may hold values from 512 to 2048
Outputs:
- attention_out: bfloat16 [256, 16384], P(('groups', 'pages'), 'heads'), parts along dimension 0
There are 2 independent parts, one for each index of `groups`. A program takes and returns all parts, laid end to end along the dimension named above; an argument that names none is the same for every part. Nothing has to cross between parts.
Inputs may be any that keep to these rules, and one draw needn't show every extreme that they name: Member m's live pages are its first page_counts[m] page slots; the counts sum to 32. `query_token`: a permutation of the span's tokens. Token t attends to the live cache rows whose key_position is below query_offsets[t].
All inputs are finite; a program needn't handle non-finite values.
Results may differ from a plain program's by a relative error of at most 0.022.
Values may be sent and summed in bfloat16 or wider, within the bound.
No kernel may reach another device: no remote copies, remote signals or barrier semaphores. Data moves between devices by JAX's collectives and lax.ppermute only.
A program may use at most 64 MiB of HBM per device.

v0:
```python
import jax
import jax.numpy as jnp
from jax import lax
from jax.sharding import PartitionSpec as P

PAGE = 64
BLOCK_PAGES = 8


floor_score = -1e30


def on_device(
    q_nope, q_rope, cache_tiles, absorb_keys, absorb_values, page_counts, query_token, query_offsets
):
    member = lax.axis_index("pages")
    heads_here, nope_width, latent = absorb_keys.shape
    value_width = absorb_values.shape[2]
    local_rows = q_nope.shape[0]
    rope_width = q_rope.shape[1] // heads_here
    full_width = cache_tiles.shape[1]
    page_rows = PAGE
    slot_pages = cache_tiles.shape[0] // page_rows
    scale = (nope_width + rope_width) ** (-0.5)
    nope_local = q_nope.reshape(local_rows, heads_here, nope_width)
    rope_local = q_rope.reshape(local_rows, heads_here, rope_width)
    local_full = jnp.concatenate(
        [
            jnp.einsum(
                "qhn,hnl->qhl", nope_local, absorb_keys, preferred_element_type=jnp.float32
            ).astype(jnp.bfloat16),
            rope_local,
        ],
        axis=2,
    )
    gathered = lax.all_gather(local_full, "pages", axis=0, tiled=True)
    queries = gathered.shape[0]
    inverse = (
        jnp.zeros((queries,), jnp.int32).at[query_token].set(jnp.arange(queries, dtype=jnp.int32))
    )
    flat_queries = gathered[inverse].reshape(queries * heads_here, full_width)
    row_limits = jnp.repeat(query_offsets, heads_here)
    prefix = jnp.cumsum(page_counts) - page_counts
    pages_view = cache_tiles.reshape(slot_pages, page_rows, full_width)
    own_steps = jnp.arange(slot_pages, dtype=jnp.int32)
    logical = jnp.where(own_steps < page_counts[member], prefix[member] + own_steps, -1)
    live_pages = page_counts[member]
    block_pages = BLOCK_PAGES
    pool_pages = pages_view.shape[0]
    padded_length = -(-pool_pages // block_pages) * block_pages
    order_padded = jnp.concatenate([own_steps, jnp.zeros((padded_length - pool_pages,), jnp.int32)])
    block_count = (live_pages + block_pages - 1) // block_pages
    offsets_in_page = jnp.arange(page_rows, dtype=jnp.int32)
    far_away = jnp.int32(2**30)

    def attend(block, carry):
        running_max, running_sum, running_acc = carry
        chosen = lax.dynamic_slice_in_dim(order_padded, block * block_pages, block_pages)
        tiles = pages_view[chosen].reshape(block_pages * page_rows, full_width)
        usable = block * block_pages + jnp.arange(block_pages, dtype=jnp.int32) < live_pages
        positions = logical[chosen][:, None] * page_rows + offsets_in_page[None, :]
        positions = jnp.where(usable[:, None], positions, far_away).reshape(-1)
        scores = (
            lax.dot_general(
                flat_queries, tiles, (((1,), (1,)), ((), ())), preferred_element_type=jnp.float32
            )
            * scale
        )
        mask = positions[None, :] < row_limits[:, None]
        block_max = jnp.max(jnp.where(mask, scores, floor_score), axis=1)
        new_max = jnp.maximum(running_max, block_max)
        weights = jnp.where(mask, jnp.exp(scores - new_max[:, None]), 0.0)
        rescale = jnp.exp(running_max - new_max)
        new_sum = running_sum * rescale + jnp.sum(weights, axis=1)
        new_acc = running_acc * rescale[:, None] + jnp.dot(
            weights.astype(jnp.bfloat16), tiles[:, :latent], preferred_element_type=jnp.float32
        )
        return (new_max, new_sum, new_acc)

    rows_all = queries * heads_here
    initial = (
        jnp.full((rows_all,), floor_score, jnp.float32),
        jnp.zeros((rows_all,), jnp.float32),
        jnp.zeros((rows_all, latent), jnp.float32),
    )
    running_max, running_sum, running_acc = lax.fori_loop(0, block_count, attend, initial)
    local_max = running_max.reshape(queries, heads_here)
    global_max = lax.pmax(local_max, "pages")
    factor = jnp.exp(local_max - global_max)
    partial_den = running_sum.reshape(queries, heads_here) * factor
    partial_num = running_acc.reshape(queries, heads_here, latent) * factor[:, :, None]
    values_wide = absorb_values.astype(jnp.float32)
    projected = jnp.einsum(
        "qhl,hlv->qhv", partial_num, values_wide, precision=lax.Precision.HIGHEST
    )
    summed, totals = (
        lax.psum_scatter(
            projected.astype(jnp.bfloat16), "pages", scatter_dimension=0, tiled=True
        ).astype(jnp.float32),
        lax.psum_scatter(
            partial_den.astype(jnp.bfloat16), "pages", scatter_dimension=0, tiled=True
        ).astype(jnp.float32),
    )
    result = summed / totals[:, :, None]
    return result.reshape(local_rows, heads_here * value_width).astype(jnp.bfloat16)


def solution(mesh):
    in_specs = (
        P(("groups", "pages"), "heads"),
        P(("groups", "pages"), "heads"),
        P(("groups", "pages"), None),
        P("heads", None, None),
        P("heads", None, None),
        P("groups"),
        P("groups"),
        P("groups"),
    )
    out_specs = P(("groups", "pages"), "heads")
    return jax.shard_map(
        on_device, mesh=mesh, in_specs=in_specs, out_specs=out_specs, check_vma=False
    )
```

profile of v0, /device:TPU:0, one launch (start us, length us, event | category | flops | bytes accessed | tf_op | source)
XLA Modules:
  0.0 259.4 jit_solution(1545467615496081824)
XLA Ops:
  7.9 2.9 %fusion.24 = bf16[32,32,512]{2,0,1:T(8,128)(2,1)S(1)} fusion(bf16[32,128,512]{2,1,0:T(8,128)(2,1)} %param.13, bf16[32,4096]{1,0:T(8,128)(2,1)S(1)} %copy-done), kind=kOutput, calls=%fused_computation.38 | convolution fusion | flops 134742016 | bytes 5505024 | tf_op jit(solution)/shard_map/qhn,hnl->qhl/dot_general | solution.py:29
  14.1 2.7 %copy.12 = bf16[1536,576]{1,0:T(8,128)(2,1)S(1)} copy(bf16[1536,576]{0,1:T(8,128)(2,1)} %param.12) | data formatting | bytes 3538944 | tf_op args[2]
  17.9 95.1 %all-gather.2.cloned.1.call-done = bf16[128,32,576]{2,0,1:T(8,128)(2,1)} async-done(((bf16[32,32,576]{2,0,1:T(8,128)(2,1)}), bf16[128,32,576]{2,0,1:T(8,128)(2,1)}) %all-gather.2.cloned.1.call-update) | async-done | bytes 4718608 | tf_op jit(solution)/shard_map/all_gather | solution.py:36
  113.0 7.8 %copy.15 = bf16[128,32,576]{2,1,0:T(8,128)(2,1)} copy(bf16[128,32,576]{2,0,1:T(8,128)(2,1)} %all-gather.2.cloned.1.call-done) | data formatting | bytes 9437184 | tf_op jit(solution)/shard_map/all_gather | solution.py:36
  120.8 6.0 %gather_fusion.2 = bf16[128,32,576]{2,1,0:T(8,128)(2,1)} fusion(bf16[128,32,576]{2,1,0:T(8,128)(2,1)} %copy.15, s32[1024]{0:T(1024)S(1)} %pad_clamp_fusion.1), kind=kCustom, calls=%fused_computation.2 | custom fusion | bytes 9437696 | tf_op jit(solution)/shard_map/gather | solution.py:41
  126.8 4.3 %broadcast_in_dim.54 = f32[4096,512]{1,0:T(8,128)} broadcast(f32[]{:T(128)} %constant.52.clone.1), dimensions={} | broadcast | bytes 8388612 | tf_op jit(solution)/shard_map/broadcast_in_dim | solution.py:84
  131.1 57.0 %while.16 = (s32[]{:T(128)}, f32[4096]{0:T(1024)S(1)}, f32[4096]{0:T(1024)S(1)}, f32[4096,512]{1,0:T(8,128)}, s32[]{:T(128)}, /*index=5*/s32[]{:T(128)}, s32[24]...) while((s32[]{:T(128)}, f32[4096]{0:T(1024)S(1)}, ...), condition=%wide.region_5.6_spmd.clone.clone, body=%wide.region_2.5_spmd.clone.clone.sunk | while | flops 4596967424 | bytes 108053704 | solution.py:86
  134.8 5.8 %fusion.48 = (f32[4096]{0:T(1024)S(1)}, f32[512,4096]{1,0:T(8,128)S(1)}) fusion(s32[4096]{0:T(1024)S(1)} %lt.144, s32[512]{0:T(512)S(1)} %select_n.96, bf16[512,576]{1,0:T(8,128)(2,1)S(1)} %bitcast.57, bf16[4096,576]{1,0:T(8,128)(2,1)} %get-tuple-element.276), kind=kOutput, calls=%fused_computation.9.clone.1 | convolution fusion | flops 2424303616 | bytes 13731840 | tf_op jit(solution)/shard_map/while/body/dot_general | solution.py:64
  140.5 2.2 fusion.49
  142.8 4.1 %multiply_add_fusion.5 = f32[4096,512]{1,0:T(8,128)S(1)} fusion(f32[4096,512]{1,0:T(8,128)S(1)} %bitcast.55, f32[512,4096]{1,0:T(8,128)S(1)} %get-tuple-element.235, f32[4096]{0:T(1024)S(1)} %get-tuple-element.237, f32[4096]{0:T(1024)S(1)} %max.8, s32[4096]{0:T(1024)S(1)} %lt.144, s32[512]{0:T(512)S(1)} %select_n.96, bf16[512,576]{1,0:T(8,128)(2,1)S(1)} %bitcast.58), kind=kOutput, calls=%fused_computation.12.clone.1 | convolution fusion | flops 2162163712 | bytes 25741312 | tf_op jit(solution)/shard_map/while/body/dot_general | solution.py:75
  146.9 3.2 %copy-done.1 = f32[4096,512]{1,0:T(8,128)} copy-done((f32[4096,512]{1,0:T(8,128)}, f32[4096,512]{1,0:T(8,128)S(1)}, u32[]{:S(2)}) %copy-start.1) | copy-done | bytes 8388632 | tf_op jit(solution)/shard_map/while
  153.8 5.8 %fusion.48 = (f32[4096]{0:T(1024)S(1)}, f32[512,4096]{1,0:T(8,128)S(1)}) fusion(s32[4096]{0:T(1024)S(1)} %lt.144, s32[512]{0:T(512)S(1)} %select_n.96, bf16[512,576]{1,0:T(8,128)(2,1)S(1)} %bitcast.57, bf16[4096,576]{1,0:T(8,128)(2,1)} %get-tuple-element.276), kind=kOutput, calls=%fused_computation.9.clone.1 | convolution fusion | flops 2424303616 | bytes 13731840 | tf_op jit(solution)/shard_map/while/body/dot_general | solution.py:64
  159.6 2.2 fusion.49
  161.8 4.1 %multiply_add_fusion.5 = f32[4096,512]{1,0:T(8,128)S(1)} fusion(f32[4096,512]{1,0:T(8,128)S(1)} %bitcast.55, f32[512,4096]{1,0:T(8,128)S(1)} %get-tuple-element.235, f32[4096]{0:T(1024)S(1)} %get-tuple-element.237, f32[4096]{0:T(1024)S(1)} %max.8, s32[4096]{0:T(1024)S(1)} %lt.144, s32[512]{0:T(512)S(1)} %select_n.96, bf16[512,576]{1,0:T(8,128)(2,1)S(1)} %bitcast.58), kind=kOutput, calls=%fused_computation.12.clone.1 | convolution fusion | flops 2162163712 | bytes 25741312 | tf_op jit(solution)/shard_map/while/body/dot_general | solution.py:75
  165.9 3.2 %copy-done.1 = f32[4096,512]{1,0:T(8,128)} copy-done((f32[4096,512]{1,0:T(8,128)}, f32[4096,512]{1,0:T(8,128)S(1)}, u32[]{:S(2)}) %copy-start.1) | copy-done | bytes 8388632 | tf_op jit(solution)/shard_map/while
  172.8 5.8 %fusion.48 = (f32[4096]{0:T(1024)S(1)}, f32[512,4096]{1,0:T(8,128)S(1)}) fusion(s32[4096]{0:T(1024)S(1)} %lt.144, s32[512]{0:T(512)S(1)} %select_n.96, bf16[512,576]{1,0:T(8,128)(2,1)S(1)} %bitcast.57, bf16[4096,576]{1,0:T(8,128)(2,1)} %get-tuple-element.276), kind=kOutput, calls=%fused_computation.9.clone.1 | convolution fusion | flops 2424303616 | bytes 13731840 | tf_op jit(solution)/shard_map/while/body/dot_general | solution.py:64
  178.6 2.2 fusion.49
  180.8 4.1 %multiply_add_fusion.5 = f32[4096,512]{1,0:T(8,128)S(1)} fusion(f32[4096,512]{1,0:T(8,128)S(1)} %bitcast.55, f32[512,4096]{1,0:T(8,128)S(1)} %get-tuple-element.235, f32[4096]{0:T(1024)S(1)} %get-tuple-element.237, f32[4096]{0:T(1024)S(1)} %max.8, s32[4096]{0:T(1024)S(1)} %lt.144, s32[512]{0:T(512)S(1)} %select_n.96, bf16[512,576]{1,0:T(8,128)(2,1)S(1)} %bitcast.58), kind=kOutput, calls=%fused_computation.12.clone.1 | convolution fusion | flops 2162163712 | bytes 25741312 | tf_op jit(solution)/shard_map/while/body/dot_general | solution.py:75
  184.9 3.2 %copy-done.1 = f32[4096,512]{1,0:T(8,128)} copy-done((f32[4096,512]{1,0:T(8,128)}, f32[4096,512]{1,0:T(8,128)S(1)}, u32[]{:S(2)}) %copy-start.1) | copy-done | bytes 8388632 | tf_op jit(solution)/shard_map/while
  188.2 16.5 %pmax.7 = f32[128,32]{1,0:T(8,128)S(1)} all-reduce(f32[128,32]{1,0:T(8,128)S(1)} %reshape.98), channel_id=1, replica_groups=mesh['groups'=2,'pages'=4,'heads'=4] {'pages'}, use_global_device_ids=true, to_apply=%region_6.7 | all-reduce | flops 4096 | bytes 32768 | tf_op jit(solution)/shard_map/pmax | solution.py:88
  205.8 13.8 %fusion.23 = bf16[128,32,128]{2,0,1:T(8,128)(2,1)} fusion(bf16[32,512,128]{2,1,0:T(8,128)(2,1)} %param.14, f32[128,32,512]{2,1,0:T(8,128)} %bitcast.56, f32[128,32]{0,1:T(8,128)S(1)} %copy.16), kind=kOutput, calls=%fused_computation.37 | convolution fusion | flops 3223846912 | bytes 13647872 | tf_op jit(solution)/shard_map/qhl,hlv->qhv/dot_general | solution.py:93
  219.6 3.7 %reduce-scatter.5.cloned.1.call-done = bf16[32,32]{1,0:T(8,128)(2,1)} async-done(((bf16[128,32]{1,0:T(8,128)(2,1)}), bf16[32,32]{1,0:T(8,128)(2,1)}) %reduce-scatter.5.cloned.1.call-update) | async-done | bytes 2064 | tf_op jit(solution)/shard_map/reduce_scatter | solution.py:100
  224.1 27.0 %reduce-scatter.3.cloned.1.call-done = bf16[32,32,128]{2,0,1:T(8,128)(2,1)} async-done(((bf16[128,32,128]{2,0,1:T(8,128)(2,1)}), bf16[32,32,128]{2,0,1:T(8,128)(2,1)}) %reduce-scatter.3.cloned.1.call-update) | async-done | bytes 262160 | tf_op jit(solution)/shard_map/reduce_scatter | solution.py:97
  251.1 1.9 copy_bitcast_fusion
  (94 shorter events, 17.8 us)
Async XLA Ops:
  6.5 1.3 copy-start
  6.5 5.5 %copy-start.3 = (s32[4]{0:T(128)S(1)}, s32[4]{0:T(128)}, u32[]{:S(2)}) copy-start(s32[4]{0:T(128)} %param.15) | copy-start | bytes 52
  6.5 10.3 %copy-start.4 = (s32[128]{0:T(128)S(1)}, s32[128]{0:T(128)}, u32[]{:S(2)}) copy-start(s32[128]{0:T(128)} %param.16) | copy-start | bytes 1540
  6.5 106.5 %all-gather.2.cloned.1.call-start = ((), (), s32[]{:S(2)}) async-start(), calls=%async_computation.2 | async-start | bytes 6553600 | tf_op jit(solution)/shard_map/all_gather | solution.py:36
  12.0 211.3 %reduce-scatter.5.cloned.1.call-start = ((), (), s32[]{:S(2)}) async-start(), calls=%async_computation.4 | async-start | bytes 40960 | tf_op jit(solution)/shard_map/reduce_scatter | solution.py:100
  120.8 10.3 %copy-start.2 = (s32[128]{0:T(128)S(1)}, s32[128]{0:T(128)}, u32[]{:S(2)}) copy-start(s32[128]{0:T(128)} %param.17) | copy-start | bytes 1540
  134.7 8.0 %slice-start = ((s8[8388608]{0:T(1024)(128)(4,1)}), s8[4194304]{0:T(1024)(128)(4,1)S(1)}, s32[]{:S(2)}) async-start(s8[8388608]{0:T(1024)(128)(4,1)} %bitcast.54), calls=%async_computation.5 | async-start | bytes 8388608 | tf_op jit(solution)/shard_map/while
  134.7 8.0 %slice-start.1 = ((s8[8388608]{0:T(1024)(128)(4,1)}), s8[4194304]{0:T(1024)(128)(4,1)S(1)}, s32[]{:S(2)}) async-start(s8[8388608]{0:T(1024)(128)(4,1)} %bitcast.54), calls=%async_computation.6 | async-start | bytes 8388608 | tf_op jit(solution)/shard_map/while
  146.9 3.2 %copy-start.1 = (f32[4096,512]{1,0:T(8,128)}, f32[4096,512]{1,0:T(8,128)S(1)}, u32[]{:S(2)}) copy-start(f32[4096,512]{1,0:T(8,128)S(1)} %multiply_add_fusion.5) | copy-start | bytes 25165828 | tf_op jit(solution)/shard_map/while
  153.7 8.0 %slice-start = ((s8[8388608]{0:T(1024)(128)(4,1)}), s8[4194304]{0:T(1024)(128)(4,1)S(1)}, s32[]{:S(2)}) async-start(s8[8388608]{0:T(1024)(128)(4,1)} %bitcast.54), calls=%async_computation.5 | async-start | bytes 8388608 | tf_op jit(solution)/shard_map/while
  153.8 8.0 %slice-start.1 = ((s8[8388608]{0:T(1024)(128)(4,1)}), s8[4194304]{0:T(1024)(128)(4,1)S(1)}, s32[]{:S(2)}) async-start(s8[8388608]{0:T(1024)(128)(4,1)} %bitcast.54), calls=%async_computation.6 | async-start | bytes 8388608 | tf_op jit(solution)/shard_map/while
  165.9 3.2 %copy-start.1 = (f32[4096,512]{1,0:T(8,128)}, f32[4096,512]{1,0:T(8,128)S(1)}, u32[]{:S(2)}) copy-start(f32[4096,512]{1,0:T(8,128)S(1)} %multiply_add_fusion.5) | copy-start | bytes 25165828 | tf_op jit(solution)/shard_map/while
  172.8 8.0 %slice-start = ((s8[8388608]{0:T(1024)(128)(4,1)}), s8[4194304]{0:T(1024)(128)(4,1)S(1)}, s32[]{:S(2)}) async-start(s8[8388608]{0:T(1024)(128)(4,1)} %bitcast.54), calls=%async_computation.5 | async-start | bytes 8388608 | tf_op jit(solution)/shard_map/while
  172.8 8.0 %slice-start.1 = ((s8[8388608]{0:T(1024)(128)(4,1)}), s8[4194304]{0:T(1024)(128)(4,1)S(1)}, s32[]{:S(2)}) async-start(s8[8388608]{0:T(1024)(128)(4,1)} %bitcast.54), calls=%async_computation.6 | async-start | bytes 8388608 | tf_op jit(solution)/shard_map/while
  184.9 3.2 %copy-start.1 = (f32[4096,512]{1,0:T(8,128)}, f32[4096,512]{1,0:T(8,128)S(1)}, u32[]{:S(2)}) copy-start(f32[4096,512]{1,0:T(8,128)S(1)} %multiply_add_fusion.5) | copy-start | bytes 25165828 | tf_op jit(solution)/shard_map/while
  205.5 45.6 %reduce-scatter.3.cloned.1.call-start = ((), (), s32[]{:S(2)}) async-start(), calls=%async_computation.3 | async-start | bytes 1310720 | tf_op jit(solution)/shard_map/reduce_scatter | solution.py:97
Sparse Core Ops, SparseCore 0:
  12.1 100.8 all-gather.1
  205.6 17.6 reduce-scatter.4
  225.6 25.3 reduce-scatter.2
where the time goes:
time: 260 us; the launch traced here: 259 us
  waiting for transfers between devices  126 us (48%)
  matrix products  46.3 us (18%)
  local copies, waits for them, and re-layouts  39.7 us (15%)
  other arithmetic  16.6 us (6%)
  blocking collectives  16.5 us (6%)
  between operations  13.9 us (5%)
    all_gather x1, waiting for transfers between devices, on_device(): gathered = lax.all_gather(local_full, 'pages', axis=0, tiled=True)  95.1 us
    reduce_scatter x1, waiting for transfers between devices, on_device(): lax.psum_scatter(projected.astype(jnp.bfloat16), 'pages', scatter_dimensi...  27 us
    dot_general x3, matrix products, attend(): lax.dot_general(flat_queries, tiles, (((1,), (1,)), ((), ())), preferred_...  17.3 us
    pmax x1, blocking collectives, on_device(): global_max = lax.pmax(local_max, 'pages')  16.5 us
    dot_general x1, matrix products, on_device(): jnp.einsum('qhl,hlv->qhv', partial_num, values_wide, precision=lax.Precis...  13.8 us
    dot_general x3, matrix products, attend(): jnp.dot(weights.astype(jnp.bfloat16), tiles[:, :latent], preferred_elemen...  12.3 us
    while x21, local copies, waits for them, and re-layouts  9.66 us
    all_gather x1, local copies, waits for them, and re-layouts, on_device(): gathered = lax.all_gather(local_full, 'pages', axis=0, tiled=True)  7.78 us
  transfers between devices with their start and end apart: 3, of which 3 were waited for; matrix products, arithmetic and copies ran while one was open for 8% of the time, Pallas kernels for 0%

commit v1 on v0

v1 whole, which is shorter than its diff:
```python
import functools

import jax
import jax.numpy as jnp
from jax import lax
from jax.experimental import pallas as pl
from jax.experimental.pallas import tpu as pltpu
from jax.sharding import PartitionSpec as P

PAGE = 64
GROUP = 2
LANES = 4
BLOCK_PAGES = 8
HEADS_STEP = 4

FLOOR = -1e30
FAR = 2**30
LOG2E = 1.4426950408889634


def attend_kernel(
    dims,
    scal_ref,
    q_ref,
    tok_ref,
    lim_ref,
    own_ref,
    part0_ref,
    part1_ref,
    part2_ref,
    part3_ref,
    keys_ref,
    values_ref,
    out_ref,
    qs,
    mx,
    den,
    acc,
    lse,
):
    hh, hb, nope, rope, latent, vhead, rows = dims
    step = pl.program_id(0)
    steps = hh // hb
    block = BLOCK_PAGES * PAGE
    scale2 = (nope + rope) ** (-0.5) * LOG2E
    nt = (((1,), (1,)), ((), ()))

    @pl.when(step == 0)
    def _():
        lse[...] = jnp.zeros_like(lse)

    for h in range(hb):
        lat = jnp.dot(q_ref[:, pl.ds(pl.multiple_of((step * hb + h) * nope, nope), nope)], keys_ref[h],
                      preferred_element_type=jnp.float32)
        qs[h * rows:(h + 1) * rows, :latent] = lat.astype(jnp.bfloat16)
    for pair in range(hb // 2):
        both = q_ref[:, pl.ds(pl.multiple_of(hh * nope + (step * hb // 2 + pair) * 2 * rope, 2 * rope), 2 * rope)]
        for e in range(2):
            h = 2 * pair + e
            qs[h * rows:(h + 1) * rows, latent:] = both[:, e * rope:(e + 1) * rope]

    mx[...] = jnp.full_like(mx, FLOOR)
    den[...] = jnp.zeros_like(den)
    acc[...] = jnp.zeros_like(acc)
    limit = jnp.concatenate([lim_ref[...]] * hb, axis=0)

    def attend(tiles, positions):
        scores = lax.dot_general(qs[...], tiles, nt, preferred_element_type=jnp.float32)
        mask = positions < limit
        scores = jnp.where(mask, scores, FLOOR)
        old = mx[...]
        new = jnp.maximum(old, jnp.max(scores, axis=1, keepdims=True))
        weights = jnp.where(mask, jnp.exp2((scores - new) * scale2), 0.0)
        keep = jnp.exp2((old - new) * scale2)
        mx[...] = new
        den[...] = den[...] * keep + jnp.sum(weights, axis=1, keepdims=True)
        acc[...] = acc[...] * keep + jnp.dot(
            weights.astype(jnp.bfloat16), tiles[:, :latent], preferred_element_type=jnp.float32
        )

    lane = lax.broadcasted_iota(jnp.int32, (1, block), 1)

    def own_block(j, _):
        live = scal_ref[0]
        tiles = own_ref[pl.ds(pl.multiple_of(j * block, block), block), :]
        page = j * BLOCK_PAGES + lane // PAGE
        positions = scal_ref[1] * PAGE + j * block + lane
        attend(tiles, jnp.where(page < live, positions, FAR))
        return 0

    lax.fori_loop(0, (scal_ref[0] + BLOCK_PAGES - 1) // BLOCK_PAGES, own_block, 0)

    sub = PAGE // LANES
    width = BLOCK_PAGES * sub

    def partner_block(j, _):
        live = scal_ref[2]
        refs = (part0_ref, part1_ref, part2_ref, part3_ref)
        tiles = jnp.concatenate([r[pl.ds(pl.multiple_of(j * width, width), width), :] for r in refs], axis=0)
        piece, inner = lane // width, lane % width
        quarter = jnp.where(piece == 0, scal_ref[5], jnp.where(piece == 1, scal_ref[6],
                            jnp.where(piece == 2, scal_ref[7], scal_ref[8])))
        page = j * BLOCK_PAGES + inner // sub
        positions = (scal_ref[3] + page) * PAGE + quarter * sub + inner % sub
        attend(tiles, jnp.where(page < live, positions, FAR))
        return 0

    lax.fori_loop(0, (scal_ref[2] + BLOCK_PAGES - 1) // BLOCK_PAGES, partner_block, 0)

    order = (tok_ref[...] == lax.broadcasted_iota(jnp.int32, (rows, rows), 0)).astype(jnp.bfloat16)
    total = den[...]
    seen = total > 0.0
    latent_out = (acc[...] * jnp.where(seen, 1.0 / jnp.where(seen, total, 1.0), 0.0)).astype(jnp.bfloat16)
    logs = jnp.where(seen, mx[...] * scale2 + jnp.log2(jnp.where(seen, total, 1.0)), FLOOR)
    column = lax.broadcasted_iota(jnp.int32, (rows, 128), 1)
    for h in range(hb):
        part = slice(h * rows, (h + 1) * rows)
        value = jnp.dot(latent_out[part], values_ref[h], preferred_element_type=jnp.float32).astype(jnp.bfloat16)
        value = jnp.dot(order, value, preferred_element_type=jnp.float32).astype(jnp.bfloat16)
        out_ref[:, pl.ds(pl.multiple_of((step * hb + h) * vhead, vhead), vhead)] = value
        full = logs[part]
        high = full.astype(jnp.bfloat16).astype(jnp.float32)
        middle = (full - high).astype(jnp.bfloat16).astype(jnp.float32)
        low = full - high - middle
        head = step * hb + h
        lse[...] = jnp.where(column == head, high, jnp.where(column == hh + head, middle,
                             jnp.where(column == 2 * hh + head, low, lse[...])))

    @pl.when(step == steps - 1)
    def _():
        ordered = jnp.dot(order, lse[...].astype(jnp.bfloat16), preferred_element_type=jnp.float32)
        out_ref[:, hh * vhead:] = ordered.astype(jnp.bfloat16)


def merge_kernel(dims, scal_ref, *refs):
    hh, vhead, count = dims
    out_ref = refs[-1]
    for parity in range(GROUP):
        blocks = [refs[s] for s in range(count) if s % GROUP == parity]
        logs = []
        for b in blocks:
            packed = b[:, hh * vhead:].astype(jnp.float32)
            logs.append(packed[:, :hh] + packed[:, hh:2 * hh] + packed[:, 2 * hh:3 * hh])
        top = functools.reduce(jnp.maximum, logs)
        weights = [jnp.exp2(v - top) for v in logs]
        total = sum(weights[1:], weights[0])
        weights = [w / total for w in weights]
        base = scal_ref[parity] * (hh * vhead)
        for h in range(hh):
            cols = slice(h * vhead, (h + 1) * vhead)
            value = sum(w[:, h:h + 1] * b[:, cols].astype(jnp.float32) for w, b in zip(weights, blocks))
            out_ref[:, pl.ds(pl.multiple_of(base + h * vhead, vhead), vhead)] = value.astype(jnp.bfloat16)


def on_device(
    q_nope, q_rope, cache_tiles, absorb_keys, absorb_values, page_counts, query_token, query_offsets, members, devices
):
    member = lax.axis_index("pages")
    lane = lax.axis_index("heads") % LANES
    heads_here, nope, latent = absorb_keys.shape
    vhead = absorb_values.shape[2]
    local_rows = q_nope.shape[0]
    rope = q_rope.shape[1] // heads_here
    full = cache_tiles.shape[1]
    slots = cache_tiles.shape[0] // PAGE
    rows = local_rows * members
    hh = heads_here // GROUP
    hb = min(HEADS_STEP, hh)
    mine = member % GROUP

    def over_pages(x, shift):
        return lax.ppermute(x, "pages", [(i, (i + shift) % members) for i in range(members)])

    def over_heads(x, bit):
        return lax.ppermute(x, "heads", [(i, i ^ bit) for i in range(devices)])

    sub = PAGE // LANES
    quarter = lax.dynamic_slice_in_dim(cache_tiles.reshape(slots, LANES, sub, full), lane, 1, axis=1)
    quarter = quarter.reshape(slots * sub, full)
    part0 = lax.ppermute(quarter, "pages", [(i, i ^ 1) for i in range(members)])
    part1 = over_heads(part0, 2)
    part2 = over_heads(part0, 1)
    part3 = over_heads(part1, 1)

    def share(which):
        return jnp.concatenate(
            [
                lax.dynamic_slice_in_dim(q_nope, which * hh * nope, hh * nope, axis=1),
                lax.dynamic_slice_in_dim(q_rope, which * hh * rope, hh * rope, axis=1),
            ],
            axis=1,
        )

    shares = [share((mine + s) % GROUP) for s in range(GROUP)]
    blocks = [shares[0]] + [over_pages(shares[s % GROUP], s) for s in range(1, members)]
    queries = jnp.concatenate(blocks, axis=0)
    sources = (member - jnp.arange(members)) % members
    row_token = query_token.reshape(members, local_rows)[sources].reshape(rows)
    limits = query_offsets[row_token]

    prefix = jnp.cumsum(page_counts) - page_counts
    partner = member ^ 1
    scalars = jnp.stack(
        [page_counts[member], prefix[member], page_counts[partner], prefix[partner], mine]
        + [lane, lane ^ 2, lane ^ 1, lane ^ 3]
    ).astype(jnp.int32)

    whole = lambda *shape: pl.BlockSpec(shape, lambda i, s: (0,) * len(shape))
    packed = hh * vhead + 128
    out = pl.pallas_call(
        functools.partial(attend_kernel, (hh, hb, nope, rope, latent, vhead, rows)),
        out_shape=jax.ShapeDtypeStruct((rows, packed), jnp.bfloat16),
        grid_spec=pltpu.PrefetchScalarGridSpec(
            num_scalar_prefetch=1,
            grid=(hh // hb,),
            in_specs=[
                whole(rows, hh * (nope + rope)),
                whole(1, rows),
                whole(rows, 1),
                whole(slots * PAGE, full),
                whole(slots * sub, full),
                whole(slots * sub, full),
                whole(slots * sub, full),
                whole(slots * sub, full),
                pl.BlockSpec((hb, nope, latent), lambda i, s: (s[4] * (hh // hb) + i, 0, 0)),
                pl.BlockSpec((hb, latent, vhead), lambda i, s: (s[4] * (hh // hb) + i, 0, 0)),
            ],
            out_specs=whole(rows, packed),
            scratch_shapes=[
                pltpu.VMEM((hb * rows, full), jnp.bfloat16),
                pltpu.VMEM((hb * rows, 1), jnp.float32),
                pltpu.VMEM((hb * rows, 1), jnp.float32),
                pltpu.VMEM((hb * rows, latent), jnp.float32),
                pltpu.VMEM((rows, 128), jnp.float32),
            ],
        ),
        compiler_params=pltpu.CompilerParams(dimension_semantics=("arbitrary",), vmem_limit_bytes=48 << 20),
        name="attend",
    )(scalars, queries, row_token[None, :], limits[:, None], cache_tiles, part0, part1, part2, part3,
      absorb_keys, absorb_values)

    def to_owner(shift):
        return lax.dynamic_slice_in_dim(out, ((member + shift) % members) * local_rows, local_rows, axis=0)

    arrived = [to_owner(0)] + [over_pages(to_owner(s), s) for s in range(1, members)]
    homes = jnp.stack([(mine + s) % GROUP for s in range(GROUP)]).astype(jnp.int32)
    return pl.pallas_call(
        functools.partial(merge_kernel, (hh, vhead, members)),
        out_shape=jax.ShapeDtypeStruct((local_rows, heads_here * vhead), jnp.bfloat16),
        grid_spec=pltpu.PrefetchScalarGridSpec(
            num_scalar_prefetch=1,
            grid=(1,),
            in_specs=[whole(local_rows, packed)] * members,
            out_specs=whole(local_rows, heads_here * vhead),
        ),
        name="merge",
    )(homes, *arrived)


def solution(mesh):
    in_specs = (
        P(("groups", "pages"), "heads"),
        P(("groups", "pages"), "heads"),
        P(("groups", "pages"), None),
        P("heads", None, None),
        P("heads", None, None),
        P("groups"),
        P("groups"),
        P("groups"),
    )
    body = functools.partial(on_device, members=mesh.shape["pages"], devices=mesh.shape["heads"])
    return jax.shard_map(
        body, mesh=mesh, in_specs=in_specs, out_specs=P(("groups", "pages"), "heads"), check_vma=False
    )
```

time: 260 us -> 97.9 us (0.38)
  waiting for transfers between devices: 126 us -> 34.5 us
  matrix products: 46.3 us -> 0 us
  Pallas kernels: 0 us -> 33.4 us
  local copies, waits for them, and re-layouts: 39.7 us -> 11.5 us
  blocking collectives: 16.5 us -> 0 us
  starting transfers between devices: 0.31 us -> 14.9 us
  between operations: 13.9 us -> 0.19 us
  other arithmetic: 16.6 us -> 3.5 us
    all_gather x1 -> x0, waiting for transfers between devices: 95.1 us -> none  [on_device(): gathered = lax.all_gather(local_full, 'pages', axis=0, tiled=True)]
    dot_general x8 -> x0, matrix products: 46.3 us -> none  [the longest x3 17.3 us: attend(): lax.dot_general(flat_queries, tiles, (((1,), (1,)), ((), ())), preferred_...]
    ppermute x0 -> x10, waiting for transfers between devices: none -> 34.5 us  [the longest x1 14.6 us: on_device(): part0 = lax.ppermute(quarter, 'pages', [(i, i ^ 1) for i in range(members)])]
    pallas_call x0 -> x2, Pallas kernels: none -> 33.4 us  [the longest x1 30.3 us: on_device(): pl.pallas_call(functools.partial(attend_kernel, (hh, hb, nope, rope, late...]
    reduce_scatter x2 -> x0, waiting for transfers between devices: 30.6 us -> none  [the longest x1 27 us: on_device(): lax.psum_scatter(projected.astype(jnp.bfloat16), 'pages', scatter_dimensi...]
    pmax x1 -> x0, blocking collectives: 16.5 us -> none  [on_device(): global_max = lax.pmax(local_max, 'pages')]
    ppermute x0 -> x10, starting transfers between devices: none -> 14.9 us  [the longest x6 13.3 us: over_pages(): lax.ppermute(x, 'pages', [(i, (i + shift) % members) for i in range(membe...]
    while x21 -> x0, local copies, waits for them, and re-layouts: 9.66 us -> none
  transfers between devices with their start and end apart: 3 -> 10, of which waited for: 3 -> 4; matrix products, arithmetic and copies ran while one was open for 8% -> 11% of each run, Pallas kernels for 0% -> 0%
where the time goes in v1:
time: 97.9 us
  waiting for transfers between devices  34.5 us (35%)
  Pallas kernels  33.4 us (34%)
  starting transfers between devices  14.9 us (15%)
  local copies, waits for them, and re-layouts  11.5 us (12%)
  other arithmetic  3.5 us (4%)
    pallas_call x1, Pallas kernels, on_device(): pl.pallas_call(functools.partial(attend_kernel, (hh, hb, nope, rope, late...  30.3 us
    ppermute x1, waiting for transfers between devices, on_device(): part0 = lax.ppermute(quarter, 'pages', [(i, i ^ 1) for i in range(members)])  14.6 us
    ppermute x6, starting transfers between devices, over_pages(): lax.ppermute(x, 'pages', [(i, (i + shift) % members) for i in range(membe...  13.3 us
    ppermute x3, waiting for transfers between devices, over_heads(): return lax.ppermute(x, 'heads', [(i, i ^ bit) for i in range(devices)])  10.9 us
    ppermute x6, waiting for transfers between devices, over_pages(): lax.ppermute(x, 'pages', [(i, (i + shift) % members) for i in range(membe...  9.03 us
    unnamed x17, local copies, waits for them, and re-layouts  3.48 us
    pallas_call x1, Pallas kernels, on_device(): pl.pallas_call(functools.partial(merge_kernel, (hh, vhead, members)), out...  3.1 us
    another operation x1, local copies, waits for them, and re-layouts, on_device(): jnp.stack([page_counts[member], prefix[member], page_counts[partner], pre...  2.51 us
  transfers between devices with their start and end apart: 10, of which 4 were waited for; matrix products, arithmetic and copies ran while one was open for 11% of the time, Pallas kernels for 0%

profile of v1, /device:TPU:0, one launch (start us, length us, event | category | flops | bytes accessed | tf_op | source)
XLA Modules:
  0.0 97.9 jit_solution(15253505300643014074)
XLA Ops:
  0.0 0.9 constant_dynamic-slice_fusion.7
  0.9 1.0 %constant_dynamic-slice_fusion.8 = (bf16[32,2048]{1,0:T(8,128)(2,1)S(1)}, bf16[32,2048]{1,0:T(8,128)(2,1)S(1)}) fusion(bf16[32,4096]{1,0:T(8,128)(2,1)} %param.8, s32[]{:T(128)S(6)} %select_n.113, s32[]{:T(128)S(6)} %select_n.115), kind=kLoop, calls=%fused_computation.17 | loop fusion | bytes 524296 | tf_op jit(solution)/shard_map/dynamic_slice | solution.py:188
  1.9 0.7 pad_maximum_fusion.2
  2.6 5.1 %collective-permute-start.2 = (bf16[32,3072]{1,0:T(8,128)(2,1)}, bf16[32,3072]{1,0:T(8,128)(2,1)}, u32[]{:S(2)}, u32[]{:S(2)}) collective-permute-start(bf16[32,3072]{1,0:T(8,128)(2,1)} %pad_maximum_fusion.2), channel_id=1, source_target_pairs={{0,12},{4,0},{8,4},{12,8},{1,13},{5,1},{9,5},{13,9},{2,14},{6,2},{... | collective-permute-start | bytes 589832 | tf_op jit(solution)/shard_map/ppermute | solution.py:172
  7.7 2.8 %copy.14.own_ref = bf16[1536,576]{1,0:T(8,128)(2,1)S(1)} copy(bf16[1536,576]{0,1:T(8,128)(2,1)} %param.10) | data formatting | bytes 3538944 | tf_op args[2]
  10.7 0.7 pad_maximum_fusion.1
  11.4 4.4 %collective-permute-start.1 = (bf16[32,3072]{1,0:T(8,128)(2,1)}, bf16[32,3072]{1,0:T(8,128)(2,1)}, u32[]{:S(2)}, u32[]{:S(2)}) collective-permute-start(bf16[32,3072]{1,0:T(8,128)(2,1)} %pad_maximum_fusion.1), channel_id=1, source_target_pairs={{0,8},{4,12},{8,0},{12,4},{1,9},{5,13},{9,1},{13,5},{2,10},{6,14},... | collective-permute-start | bytes 589832 | tf_op jit(solution)/shard_map/ppermute | solution.py:172
  15.7 0.2 reduce-window.9
  16.0 0.6 gather_fusion
  16.7 14.6 %collective-permute-done.3.part0_ref = bf16[384,576]{1,0:T(8,128)(2,1)S(1)} collective-permute-done((bf16[384,576]{1,0:T(8,128)(2,1)S(1)}, bf16[384,576]{1,0:T(8,128)(2,1)S(1)}, u32[]{:S(2)}, u32[]{:S(2)}) %collective-permute-start.3) | collective-permute-done | bytes 442400 | tf_op jit(solution)/shard_map/ppermute | solution.py:180
  31.3 1.5 %collective-permute-start.4 = (bf16[384,576]{1,0:T(8,128)(2,1)S(1)}, bf16[384,576]{1,0:T(8,128)(2,1)S(1)}, u32[]{:S(2)}, u32[]{:S(2)}) collective-permute-start(bf16[384,576]{1,0:T(8,128)(2,1)S(1)} %collective-permute-done.3.part0_ref), channel_id=1, source_target_pairs={{0,2},{1,3},{2,0},{3,1},{4,6},{5,7},{6,4},{7,5},{8,10},{9,11},{10,... | collective-permute-start | bytes 1327112 | tf_op jit(solution)/shard_map/ppermute | solution.py:175
  32.9 10.9 %collective-permute-done.4.part1_ref = bf16[384,576]{1,0:T(8,128)(2,1)S(1)} collective-permute-done((bf16[384,576]{1,0:T(8,128)(2,1)S(1)}, bf16[384,576]{1,0:T(8,128)(2,1)S(1)}, u32[]{:S(2)}, u32[]{:S(2)}) %collective-permute-start.4) | collective-permute-done | bytes 442400 | tf_op jit(solution)/shard_map/ppermute | solution.py:175
  43.8 1.2 %gather_fusion.1 = s32[128]{0:T(128)S(1)} fusion(s32[128]{0:T(128)S(1)} %copy-done, s32[1024]{0:T(1024)S(1)} %pad_clamp_fusion), kind=kCustom, calls=%fused_computation.1 | custom fusion | bytes 1536 | tf_op jit(solution)/shard_map/gather | solution.py:199
  45.2 0.7 fusion.3
  45.9 2.5 %stack.35.scal_ref = s32[9]{0:T(128)S(1)} concatenate(s32[1]{0:T(128)} %get-tuple-element.17, s32[1]{0:T(128)} %get-tuple-element.14, s32[1]{0:T(128)} %get-tuple-element.18, s32[1]{0:T(128)} %get-tuple-element.13, s32[1]{0:T(128)} %bitcast.4, s32[1]{0:T(128)} %bitcast.5, s32[1]{0:T(128)} %bitcast.6, s32[1]{0:T(128)} %bitcast.7, s32[1]{0:T(128)} %bitcast.8), dimensions={0} | concatenate | bytes 72 | tf_op jit(solution)/shard_map/stack | solution.py:203
  48.4 1.3 %pad_maximum_fusion.q_ref = bf16[128,3072]{1,0:T(8,128)(2,1)S(1)} fusion(bf16[32,3072]{1,0:T(8,128)(2,1)} %collective-permute-done.2, bf16[32,3072]{1,0:T(8,128)(2,1)} %collective-permute-done.1, bf16[32,3072]{1,0:T(8,128)(2,1)} %collective-permute-done, bf16[32,1024]{1,0:T(8,128)(2,1)} %copy-done.2, bf16[32,2048]{1,0:T(8,128)(2,1)} %copy-done.1), kind=kLoop, calls=%fused_computation.2 | loop fusion | flops 3932160 | bytes 1572864 | tf_op jit(solution)/shard_map/concatenate | solution.py:196
  49.7 30.3 %attend.1 = bf16[128,2176]{1,0:T(8,128)(2,1)S(1)} custom-call(s32[9]{0:T(128)S(1)} %stack.35.scal_ref, bf16[128,3072]{1,0:T(8,128)(2,1)S(1)} %pad_maximum_fusion.q_ref, s32[1,128]{1,0:T(1,128)S(1)} %broadcast_in_dim_reshape.3.tok_ref, s32[128,1]{1,0:T(8,128)S(1)} %copy.13.lim_ref, bf16[1536,576]{1,0:T(8,128)(2,1)S(1)} %copy.14.own_ref, ...), custom_call_target="tpu_custom_call" | custom-call | tf_op jit(solution)/shard_map/attend/pallas_call | solution.py:210
  79.9 0.7 constant_dynamic-slice_fusion
  80.7 3.8 %collective-permute-start.9 = (bf16[32,2176]{1,0:T(8,128)(2,1)S(1)}, bf16[32,2176]{1,0:T(8,128)(2,1)S(1)}, u32[]{:S(2)}, u32[]{:S(2)}) collective-permute-start(bf16[32,2176]{1,0:T(8,128)(2,1)S(1)} %get-tuple-element.5), channel_id=1, source_target_pairs={{0,12},{4,0},{8,4},{12,8},{1,13},{5,1},{9,5},{13,9},{2,14},{6,2},{... | collective-permute-start | bytes 417800 | tf_op jit(solution)/shard_map/ppermute | solution.py:172
  84.5 0.6 pad_add_fusion.scal_ref
  85.1 4.0 %collective-permute-done.7.refs_1_ = bf16[32,2176]{1,0:T(8,128)(2,1)S(1)} collective-permute-done((bf16[32,2176]{1,0:T(8,128)(2,1)S(1)}, bf16[32,2176]{1,0:T(8,128)(2,1)S(1)}, u32[]{:S(2)}, u32[]{:S(2)}) %collective-permute-start.7) | collective-permute-done | bytes 139296 | tf_op jit(solution)/shard_map/ppermute | solution.py:172
  89.1 5.0 %collective-permute-done.8.refs_2_ = bf16[32,2176]{1,0:T(8,128)(2,1)S(1)} collective-permute-done((bf16[32,2176]{1,0:T(8,128)(2,1)S(1)}, bf16[32,2176]{1,0:T(8,128)(2,1)S(1)}, u32[]{:S(2)}, u32[]{:S(2)}) %collective-permute-start.8) | collective-permute-done | bytes 139296 | tf_op jit(solution)/shard_map/ppermute | solution.py:172
  94.1 0.6 copy-done.4
  94.8 3.1 %merge.1 = bf16[32,4096]{1,0:T(8,128)(2,1)} custom-call(s32[2]{0:T(128)} %pad_add_fusion.scal_ref, bf16[32,2176]{1,0:T(8,128)(2,1)} %get-tuple-element.8.refs_0_, bf16[32,2176]{1,0:T(8,128)(2,1)} %copy-done.3, bf16[32,2176]{1,0:T(8,128)(2,1)} %copy-done.4, bf16[32,2176]{1,0:T(8,128)(2,1)} %copy-done.5), custom_call_target="tpu_custom_call" | custom-call | tf_op jit(solution)/shard_map/merge/pallas_call | solution.py:247
  (37 shorter events, 0.7 us)
Async XLA Ops:
  0.0 43.8 %copy-start = (s32[128]{0:T(128)S(1)}, s32[128]{0:T(128)}, u32[]{:S(2)}) copy-start(s32[128]{0:T(128)} %param.15) | copy-start | bytes 1540
  0.9 9.7 %copy-start.2 = (bf16[32,1024]{1,0:T(8,128)(2,1)}, bf16[32,1024]{1,0:T(8,128)(2,1)S(1)}, u32[]{:S(2)}) copy-start(bf16[32,1024]{1,0:T(8,128)(2,1)S(1)} %get-tuple-element.11) | copy-start | bytes 196612
  1.9 8.7 %copy-start.1 = (bf16[32,2048]{1,0:T(8,128)(2,1)}, bf16[32,2048]{1,0:T(8,128)(2,1)S(1)}, u32[]{:S(2)}) copy-start(bf16[32,2048]{1,0:T(8,128)(2,1)S(1)} %get-tuple-element.9) | copy-start | bytes 393220
  2.6 45.7 %collective-permute-start.2 = (bf16[32,3072]{1,0:T(8,128)(2,1)}, bf16[32,3072]{1,0:T(8,128)(2,1)}, u32[]{:S(2)}, u32[]{:S(2)}) collective-permute-start(bf16[32,3072]{1,0:T(8,128)(2,1)} %pad_maximum_fusion.2), channel_id=1, source_target_pairs={{0,12},{4,0},{8,4},{12,8},{1,13},{5,1},{9,5},{13,9},{2,14},{6,2},{... | collective-permute-start | bytes 589832 | tf_op jit(solution)/shard_map/ppermute | solution.py:172
  7.7 40.7 %collective-permute-start = (bf16[32,3072]{1,0:T(8,128)(2,1)}, bf16[32,3072]{1,0:T(8,128)(2,1)}, u32[]{:S(2)}, u32[]{:S(2)}) collective-permute-start(bf16[32,3072]{1,0:T(8,128)(2,1)} %pad_maximum_fusion.2), channel_id=1, source_target_pairs={{0,4},{4,8},{8,12},{12,0},{1,5},{5,9},{9,13},{13,1},{2,6},{6,10},{... | collective-permute-start | bytes 589832 | tf_op jit(solution)/shard_map/ppermute | solution.py:172
  7.7 8.0 %copy-start.6 = (s32[4]{0:T(128)S(1)}, s32[4]{0:T(128)}, u32[]{:S(2)}) copy-start(s32[4]{0:T(128)} %param.13) | copy-start | bytes 52
  7.7 8.2 %copy-start.7 = (s32[128]{0:T(128)S(1)}, s32[128]{0:T(128)}, u32[]{:S(2)}) copy-start(s32[128]{0:T(128)} %param.14) | copy-start | bytes 1540
  10.6 20.7 %collective-permute-start.3 = (bf16[384,576]{1,0:T(8,128)(2,1)S(1)}, bf16[384,576]{1,0:T(8,128)(2,1)S(1)}, u32[]{:S(2)}, u32[]{:S(2)}) collective-permute-start(bf16[384,576]{1,0:T(8,128)(2,1)S(1)} %bitcast.18), channel_id=1, source_target_pairs={{0,4},{4,0},{8,12},{12,8},{1,5},{5,1},{9,13},{13,9},{2,6},{6,2},{1... | collective-permute-start | bytes 1327112 | tf_op jit(solution)/shard_map/ppermute | solution.py:180
  11.4 37.0 %collective-permute-start.1 = (bf16[32,3072]{1,0:T(8,128)(2,1)}, bf16[32,3072]{1,0:T(8,128)(2,1)}, u32[]{:S(2)}, u32[]{:S(2)}) collective-permute-start(bf16[32,3072]{1,0:T(8,128)(2,1)} %pad_maximum_fusion.1), channel_id=1, source_target_pairs={{0,8},{4,12},{8,0},{12,4},{1,9},{5,13},{9,1},{13,5},{2,10},{6,14},... | collective-permute-start | bytes 589832 | tf_op jit(solution)/shard_map/ppermute | solution.py:172
  31.3 12.5 %collective-permute-start.4 = (bf16[384,576]{1,0:T(8,128)(2,1)S(1)}, bf16[384,576]{1,0:T(8,128)(2,1)S(1)}, u32[]{:S(2)}, u32[]{:S(2)}) collective-permute-start(bf16[384,576]{1,0:T(8,128)(2,1)S(1)} %collective-permute-done.3.part0_ref), channel_id=1, source_target_pairs={{0,2},{1,3},{2,0},{3,1},{4,6},{5,7},{6,4},{7,5},{8,10},{9,11},{10,... | collective-permute-start | bytes 1327112 | tf_op jit(solution)/shard_map/ppermute | solution.py:175
  32.9 16.8 %collective-permute-start.5 = (bf16[384,576]{1,0:T(8,128)(2,1)S(1)}, bf16[384,576]{1,0:T(8,128)(2,1)S(1)}, u32[]{:S(2)}, u32[]{:S(2)}) collective-permute-start(bf16[384,576]{1,0:T(8,128)(2,1)S(1)} %collective-permute-done.3.part0_ref), channel_id=1, source_target_pairs={{0,1},{1,0},{2,3},{3,2},{4,5},{5,4},{6,7},{7,6},{8,9},{9,8},{10,11... | collective-permute-start | bytes 1327112 | tf_op jit(solution)/shard_map/ppermute | solution.py:175
  43.8 5.9 %collective-permute-start.6 = (bf16[384,576]{1,0:T(8,128)(2,1)S(1)}, bf16[384,576]{1,0:T(8,128)(2,1)}, u32[]{:S(2)}, u32[]{:S(2)}) collective-permute-start(bf16[384,576]{1,0:T(8,128)(2,1)S(1)} %collective-permute-done.4.part1_ref), channel_id=1, source_target_pairs={{0,1},{1,0},{2,3},{3,2},{4,5},{5,4},{6,7},{7,6},{8,9},{9,8},{10,11... | collective-permute-start | bytes 1327112 | tf_op jit(solution)/shard_map/ppermute | solution.py:175
  80.6 8.5 %collective-permute-start.7 = (bf16[32,2176]{1,0:T(8,128)(2,1)S(1)}, bf16[32,2176]{1,0:T(8,128)(2,1)S(1)}, u32[]{:S(2)}, u32[]{:S(2)}) collective-permute-start(bf16[32,2176]{1,0:T(8,128)(2,1)S(1)} %get-tuple-element.7), channel_id=1, source_target_pairs={{0,4},{4,8},{8,12},{12,0},{1,5},{5,9},{9,13},{13,1},{2,6},{6,10},{... | collective-permute-start | bytes 417800 | tf_op jit(solution)/shard_map/ppermute | solution.py:172
  80.7 13.5 %collective-permute-start.8 = (bf16[32,2176]{1,0:T(8,128)(2,1)S(1)}, bf16[32,2176]{1,0:T(8,128)(2,1)S(1)}, u32[]{:S(2)}, u32[]{:S(2)}) collective-permute-start(bf16[32,2176]{1,0:T(8,128)(2,1)S(1)} %get-tuple-element.6), channel_id=1, source_target_pairs={{0,8},{4,12},{8,0},{12,4},{1,9},{5,13},{9,1},{13,5},{2,10},{6,14},... | collective-permute-start | bytes 417800 | tf_op jit(solution)/shard_map/ppermute | solution.py:172
  80.7 13.5 %collective-permute-start.9 = (bf16[32,2176]{1,0:T(8,128)(2,1)S(1)}, bf16[32,2176]{1,0:T(8,128)(2,1)S(1)}, u32[]{:S(2)}, u32[]{:S(2)}) collective-permute-start(bf16[32,2176]{1,0:T(8,128)(2,1)S(1)} %get-tuple-element.5), channel_id=1, source_target_pairs={{0,12},{4,0},{8,4},{12,8},{1,13},{5,1},{9,5},{13,9},{2,14},{6,2},{... | collective-permute-start | bytes 417800 | tf_op jit(solution)/shard_map/ppermute | solution.py:172
  89.1 5.0 %copy-start.3 = (bf16[32,2176]{1,0:T(8,128)(2,1)}, bf16[32,2176]{1,0:T(8,128)(2,1)S(1)}, u32[]{:S(2)}) copy-start(bf16[32,2176]{1,0:T(8,128)(2,1)S(1)} %collective-permute-done.7.refs_1_) | copy-start | bytes 417796
  94.1 0.6 copy-start.4
  94.1 0.7 copy-start.5

commit v2 on v0

v2 whole, which is shorter than its diff:
```python
import functools

import jax
import jax.numpy as jnp
from jax import lax
from jax.experimental import pallas as pl
from jax.experimental.pallas import tpu as pltpu
from jax.sharding import PartitionSpec as P

PAGE = 64
GROUP = 2
LANES = 4
BLOCK_PAGES = 8
HEADS_STEP = 4
CHUNKS = 2

FLOOR = -1e30
FAR = 2**30
LOG2E = 1.4426950408889634


def pack_kernel(dims, nope_ref, rope_ref, cache_ref, share0_ref, share1_ref, quarter_ref, sems):
    nope_width, rope_width, quarter_cols = dims
    mine = lax.axis_index("pages") % GROUP
    lane = lax.axis_index("heads") % LANES
    copies = [
        pltpu.make_async_copy(
            cache_ref.at[:, pl.ds(pl.multiple_of(lane * quarter_cols, 128), quarter_cols)], quarter_ref, sems.at[0]
        )
    ]
    for e, share in enumerate((share0_ref, share1_ref)):
        which = (mine + e) % GROUP
        for j, (ref, width, at) in enumerate(((nope_ref, nope_width, 0), (rope_ref, rope_width, nope_width))):
            copies.append(
                pltpu.make_async_copy(
                    ref.at[:, pl.ds(pl.multiple_of(which * width, 128), width)],
                    share.at[:, pl.ds(at, width)],
                    sems.at[1 + 2 * e + j],
                )
            )
    for c in copies:
        c.start()
    for c in copies:
        c.wait()


def attend_kernel(dims, counts_ref, tok_ref, off_ref, *refs):
    members, first, hc, hh, hb, nope, rope, latent, vhead, rows, slots = dims
    q_refs, refs = refs[:members], refs[members:]
    part_refs, refs = refs[:LANES], refs[LANES:]
    own_ref, keys_hbm, values_hbm = refs[:3]
    out_refs, refs = refs[3:3 + members], refs[3 + members:]
    tiles, wk, wv, bias, qs, sbuf, mx, den, acc, lse, sems = refs
    local_rows = rows // members
    block = BLOCK_PAGES * PAGE
    cols = slots * PAGE
    scale2 = (nope + rope) ** (-0.5) * LOG2E
    steps = hc // hb
    member = lax.axis_index("pages")
    lane_id = lax.axis_index("heads") % LANES
    partner = member ^ 1
    mine = member % GROUP

    own_copy = pltpu.make_async_copy(own_ref, tiles.at[:, pl.ds(0, cols)], sems.at[0])
    own_copy.start()
    weight_copies = []
    for g in range(steps):
        at = pl.ds(mine * hh + first + g * hb, hb)
        pair = (
            pltpu.make_async_copy(keys_hbm.at[at], wk.at[pl.ds(g * hb, hb)], sems.at[1 + 2 * g]),
            pltpu.make_async_copy(values_hbm.at[at], wv.at[pl.ds(g * hb, hb)], sems.at[2 + 2 * g]),
        )
        for c in pair:
            c.start()
        weight_copies.append(pair)

    token = pltpu.roll(
        jnp.broadcast_to(tok_ref[...], (8, rows)), lax.rem(rows - member * local_rows, rows), axis=1
    )[:1]
    token_down = jnp.transpose(jnp.broadcast_to(token, (rows, rows)).astype(jnp.float32)).astype(jnp.int32)
    across = lax.broadcasted_iota(jnp.int32, (rows, rows), 1)
    down = lax.broadcasted_iota(jnp.int32, (rows, rows), 0)
    limit = jnp.max(jnp.where(token_down == across, off_ref[...], 0), axis=1, keepdims=True)
    owner = lax.rem(member - down // local_rows + members, members)
    order = (jnp.broadcast_to(token, (rows, rows)) == owner * local_rows + lax.rem(down, local_rows)).astype(
        jnp.bfloat16
    )

    quarter_cols = cols // LANES
    for ref, flip in zip(part_refs, (0, 2, 1, 3)):
        at = pl.multiple_of(cols + (lane_id ^ flip) * quarter_cols, 128)
        tiles[:, pl.ds(at, quarter_cols)] = ref[...]
    before = lambda who: lax.fori_loop(0, who, lambda i, total: total + counts_ref[i], jnp.int32(0))
    own_live, part_live = counts_ref[member], counts_ref[partner]
    own_base, part_base = before(member) * PAGE, before(partner) * PAGE
    own_blocks = (own_live + BLOCK_PAGES - 1) // BLOCK_PAGES
    blocks = own_blocks + (part_live + BLOCK_PAGES - 1) // BLOCK_PAGES

    def column(b):
        return pl.multiple_of(jnp.where(b < own_blocks, b * block, cols + (b - own_blocks) * block), 128)

    spot = lax.broadcasted_iota(jnp.int32, (1, block), 1)

    def fill_bias(b, carry):
        own = b < own_blocks
        inside = jnp.where(own, b, b - own_blocks) * block + spot
        live = jnp.where(own, own_live, part_live) * PAGE
        positions = jnp.where(inside < live, jnp.where(own, own_base, part_base) + inside, FAR)
        bias[:, pl.ds(pl.multiple_of(b * block, 128), block)] = jnp.where(positions < limit, 0.0, FLOOR)
        return carry

    lax.fori_loop(0, blocks, fill_bias, 0)
    lse[...] = jnp.zeros_like(lse)
    queries = [jnp.concatenate([q[:, (first + h) * nope:(first + h + 1) * nope] for q in q_refs], axis=0)
               for h in range(hc)]
    own_copy.wait()

    def absorb(g):
        slot = g % 2
        weight_copies[g][0].wait()
        for e in range(hb):
            h = g * hb + e
            lat = jnp.dot(queries[h], wk[h], preferred_element_type=jnp.float32)
            qs[slot, e * rows:(e + 1) * rows, :latent] = lat.astype(jnp.bfloat16)
        for e in range(0, hb, 2):
            at = hh * nope + (first + g * hb + e) * rope
            both = jnp.concatenate([q[:, at:at + 2 * rope] for q in q_refs], axis=0)
            for i in range(2):
                qs[slot, (e + i) * rows:(e + i + 1) * rows, latent:] = both[:, i * rope:(i + 1) * rope]
        mx[slot] = jnp.full(mx.shape[1:], FLOOR, jnp.float32)

    def score(g, b):
        slot = g % 2
        scores = jnp.dot(qs[slot], tiles[:, pl.ds(column(b), block)], preferred_element_type=jnp.float32)
        at = pl.multiple_of(b * block, 128)
        shut = bias[:, pl.ds(at, block)]
        for e in range(hb):
            part = slice(e * rows, (e + 1) * rows)
            value = scores[part] + shut
            sbuf[slot, part, pl.ds(at, block)] = value
            top = functools.reduce(jnp.maximum, [value[:, i:i + 128] for i in range(0, block, 128)])
            mx[slot, part] = jnp.maximum(mx[slot, part], top)

    def gather(g, b, top):
        slot = g % 2
        at = pl.multiple_of(b * block, 128)
        weights = jnp.exp2((sbuf[slot, :, pl.ds(at, block)] - top) * scale2)
        den[...] += functools.reduce(jnp.add, [weights[:, i:i + 128] for i in range(0, block, 128)])
        acc[...] += lax.dot_general(
            weights.astype(jnp.bfloat16),
            tiles[:latent, pl.ds(column(b), block)],
            (((1,), (1,)), ((), ())),
            preferred_element_type=jnp.float32,
        )

    lane = lax.broadcasted_iota(jnp.int32, (rows, 128), 1)

    def finish(g, top):
        weight_copies[g][1].wait()
        total = jnp.sum(den[...], axis=1, keepdims=True)
        seen = top > 0.5 * FLOOR
        total = jnp.where(seen, total, 1.0)
        latent_out = (acc[...] * jnp.where(seen, 1.0 / total, 0.0)).astype(jnp.bfloat16)
        logs = jnp.where(seen, top * scale2 + jnp.log2(total), FLOOR)
        for e in range(hb):
            h = g * hb + e
            part = slice(e * rows, (e + 1) * rows)
            value = jnp.dot(latent_out[part], wv[h], preferred_element_type=jnp.float32).astype(jnp.bfloat16)
            value = jnp.dot(order, value, preferred_element_type=jnp.float32).astype(jnp.bfloat16)
            for s in range(members):
                out_refs[s][:, h * vhead:(h + 1) * vhead] = value[s * local_rows:(s + 1) * local_rows]
            full = logs[part]
            high = full.astype(jnp.bfloat16).astype(jnp.float32)
            middle = (full - high).astype(jnp.bfloat16).astype(jnp.float32)
            low = full - high - middle
            lse[...] = jnp.where(lane == h, high, jnp.where(lane == hc + h, middle,
                                 jnp.where(lane == 2 * hc + h, low, lse[...])))

    top = None
    for g in range(steps + 1):
        if g < steps:
            absorb(g)
        if g > 0:
            den[...] = jnp.zeros_like(den)
            acc[...] = jnp.zeros_like(acc)

        def body(b, carry, g=g, top=top):
            if g < steps:
                score(g, b)
            if g > 0:
                gather(g - 1, b, top)
            return carry

        lax.fori_loop(0, blocks, body, 0)
        if g > 0:
            finish(g - 1, top)
        if g < steps:
            top = jnp.max(mx[g % 2], axis=1, keepdims=True)

    ordered = jnp.dot(order, lse[...].astype(jnp.bfloat16), preferred_element_type=jnp.float32).astype(jnp.bfloat16)
    for s in range(members):
        out_refs[s][:, hc * vhead:] = ordered[s * local_rows:(s + 1) * local_rows]


def merge_kernel(dims, *refs):
    hc, vhead, members, chunks = dims
    out_ref = refs[-1]
    mine = lax.axis_index("pages") % GROUP
    for c in range(chunks):
        for parity in range(GROUP):
            parts = [refs[c * members + s] for s in range(members) if s % GROUP == parity]
            logs = []
            for b in parts:
                packed = b[:, hc * vhead:].astype(jnp.float32)
                logs.append(packed[:, :hc] + packed[:, hc:2 * hc] + packed[:, 2 * hc:3 * hc])
            top = functools.reduce(jnp.maximum, logs)
            weights = [jnp.exp2(v - top) for v in logs]
            total = functools.reduce(jnp.add, weights)
            weights = [w / total for w in weights]
            base = (lax.rem(mine + parity, GROUP) * chunks + c) * (hc * vhead)
            for h in range(hc):
                cols = slice(h * vhead, (h + 1) * vhead)
                value = functools.reduce(
                    jnp.add, [w[:, h:h + 1] * b[:, cols].astype(jnp.float32) for w, b in zip(weights, parts)]
                )
                out_ref[:, pl.ds(pl.multiple_of(base + h * vhead, 128), vhead)] = value.astype(jnp.bfloat16)


def on_device(
    q_nope, q_rope, cache_tiles, absorb_keys, absorb_values, page_counts, query_token, query_offsets, members, devices
):
    heads_here, nope, latent = absorb_keys.shape
    vhead = absorb_values.shape[2]
    local_rows = q_nope.shape[0]
    rope = q_rope.shape[1] // heads_here
    full = cache_tiles.shape[1]
    slots = cache_tiles.shape[0] // PAGE
    cols = slots * PAGE
    rows = local_rows * members
    hh = heads_here // GROUP
    chunks = min(CHUNKS, hh // 2)
    hc = hh // chunks
    hb = min(HEADS_STEP, hc)
    hbm = pl.BlockSpec(memory_space=pltpu.HBM)
    vmem = pl.BlockSpec(memory_space=pltpu.VMEM)
    bf16 = jnp.bfloat16

    def over_pages(x, s):
        return lax.ppermute(x, "pages", [(i, (i - s) % members) for i in range(members)])

    def over_heads(x, bit):
        return lax.ppermute(x, "heads", [(i, i ^ bit) for i in range(devices)])

    turned = cache_tiles.T
    share0, share1, quarter = pl.pallas_call(
        functools.partial(pack_kernel, (hh * nope, hh * rope, cols // LANES)),
        out_shape=[jax.ShapeDtypeStruct((local_rows, hh * (nope + rope)), bf16)] * 2
        + [jax.ShapeDtypeStruct((full, cols // LANES), bf16)],
        in_specs=[hbm] * 3,
        out_specs=[vmem] * 3,
        scratch_shapes=[pltpu.SemaphoreType.DMA((5,))],
        name="pack",
    )(q_nope, q_rope, turned)

    part0 = lax.ppermute(quarter, "pages", [(i, i ^ 1) for i in range(members)])
    shares = (share0, share1)
    queries = [share0] + [over_pages(shares[s % GROUP], s) for s in range(1, members)]
    part1 = over_heads(part0, 2)
    part2 = over_heads(part0, 1)
    part3 = over_heads(part1, 1)

    packed = hc * vhead + 128
    block = BLOCK_PAGES * PAGE
    most = 2 * (-(-cols // block))
    arrived = []
    for c in range(chunks):
        outs = pl.pallas_call(
            functools.partial(
                attend_kernel, (members, c * hc, hc, hh, hb, nope, rope, latent, vhead, rows, slots)
            ),
            out_shape=[jax.ShapeDtypeStruct((local_rows, packed), bf16)] * members,
            in_specs=[pl.BlockSpec(memory_space=pltpu.SMEM)] + [vmem] * (2 + members + LANES) + [hbm] * 3,
            out_specs=[vmem] * members,
            scratch_shapes=[
                pltpu.VMEM((full, 2 * cols), bf16),
                pltpu.VMEM((hc, nope, latent), bf16),
                pltpu.VMEM((hc, latent, vhead), bf16),
                pltpu.VMEM((rows, most * block), jnp.float32),
                pltpu.VMEM((2, hb * rows, full), bf16),
                pltpu.VMEM((2, hb * rows, most * block), jnp.float32),
                pltpu.VMEM((2, hb * rows, 128), jnp.float32),
                pltpu.VMEM((hb * rows, 128), jnp.float32),
                pltpu.VMEM((hb * rows, latent), jnp.float32),
                pltpu.VMEM((rows, 128), jnp.float32),
                pltpu.SemaphoreType.DMA((1 + 2 * (hc // hb),)),
            ],
            compiler_params=pltpu.CompilerParams(vmem_limit_bytes=56 << 20),
            cost_estimate=pl.CostEstimate(flops=8 * 10**9 // chunks, bytes_accessed=8 * 10**6, transcendentals=0),
            name=f"attend{c}",
        )(page_counts, query_token[None, :], query_offsets[None, :], *queries, part0, part1, part2, part3,
          turned, absorb_keys, absorb_values)
        arrived += [outs[0]] + [over_pages(outs[s], s) for s in range(1, members)]

    return pl.pallas_call(
        functools.partial(merge_kernel, (hc, vhead, members, chunks)),
        out_shape=jax.ShapeDtypeStruct((local_rows, heads_here * vhead), bf16),
        in_specs=[vmem] * (members * chunks),
        out_specs=vmem,
        name="merge",
    )(*arrived)


def solution(mesh):
    in_specs = (
        P(("groups", "pages"), "heads"),
        P(("groups", "pages"), "heads"),
        P(("groups", "pages"), None),
        P("heads", None, None),
        P("heads", None, None),
        P("groups"),
        P("groups"),
        P("groups"),
    )
    body = functools.partial(on_device, members=mesh.shape["pages"], devices=mesh.shape["heads"])
    return jax.shard_map(
        body, mesh=mesh, in_specs=in_specs, out_specs=P(("groups", "pages"), "heads"), check_vma=False
    )
```

time: 260 us -> 94.1 us (0.36)
  waiting for transfers between devices: 126 us -> 40.2 us
  matrix products: 46.3 us -> 0 us
  local copies, waits for them, and re-layouts: 39.7 us -> 1.64 us
  Pallas kernels: 0 us -> 33.9 us
  other arithmetic: 16.6 us -> 0 us
  blocking collectives: 16.5 us -> 0 us
  starting transfers between devices: 0.31 us -> 16.8 us
  between operations: 13.9 us -> 0.14 us
    all_gather x1 -> x0, waiting for transfers between devices: 95.1 us -> none  [on_device(): gathered = lax.all_gather(local_full, 'pages', axis=0, tiled=True)]
    dot_general x8 -> x0, matrix products: 46.3 us -> none  [the longest x3 17.3 us: attend(): lax.dot_general(flat_queries, tiles, (((1,), (1,)), ((), ())), preferred_...]
    ppermute x0 -> x13, waiting for transfers between devices: none -> 40.2 us  [the longest x9 20.1 us: over_pages(): lax.ppermute(x, 'pages', [(i, (i - s) % members) for i in range(members)])]
    pallas_call x0 -> x4, Pallas kernels: none -> 33.9 us  [the longest x2 29.2 us: on_device(): pl.pallas_call(functools.partial(attend_kernel, (members, c * hc, hc, hh,...]
    reduce_scatter x2 -> x0, waiting for transfers between devices: 30.6 us -> none  [the longest x1 27 us: on_device(): lax.psum_scatter(projected.astype(jnp.bfloat16), 'pages', scatter_dimensi...]
    ppermute x0 -> x13, starting transfers between devices: none -> 16.8 us  [the longest x9 12 us: over_pages(): lax.ppermute(x, 'pages', [(i, (i - s) % members) for i in range(members)])]
    pmax x1 -> x0, blocking collectives: 16.5 us -> none  [on_device(): global_max = lax.pmax(local_max, 'pages')]
    gather x7 -> x0, local copies, waits for them, and re-layouts: 9.97 us -> none  [the longest x1 6.02 us: on_device(): flat_queries = gathered[inverse].reshape(queries * heads_here, full_width)]
  transfers between devices with their start and end apart: 3 -> 13, of which waited for: 3 -> 6; matrix products, arithmetic and copies ran while one was open for 8% -> 0% of each run, Pallas kernels for 0% -> 16%
where the time goes in v2:
time: 94.1 us; the launch traced here: 92.7 us
  waiting for transfers between devices  40.2 us (43%)
  Pallas kernels  33.9 us (36%)
  starting transfers between devices  16.8 us (18%)
  local copies, waits for them, and re-layouts  1.64 us (2%)
    pallas_call x2, Pallas kernels, on_device(): pl.pallas_call(functools.partial(attend_kernel, (members, c * hc, hc, hh,...  29.2 us
    ppermute x9, waiting for transfers between devices, over_pages(): lax.ppermute(x, 'pages', [(i, (i - s) % members) for i in range(members)])  20.1 us
    ppermute x9, starting transfers between devices, over_pages(): lax.ppermute(x, 'pages', [(i, (i - s) % members) for i in range(members)])  12 us
    ppermute x1, waiting for transfers between devices, on_device(): part0 = lax.ppermute(quarter, 'pages', [(i, i ^ 1) for i in range(members)])  10.4 us
    ppermute x3, waiting for transfers between devices, over_heads(): return lax.ppermute(x, 'heads', [(i, i ^ bit) for i in range(devices)])  9.68 us
    ppermute x1, starting transfers between devices, on_device(): part0 = lax.ppermute(quarter, 'pages', [(i, i ^ 1) for i in range(members)])  3.12 us
    pallas_call x1, Pallas kernels, on_device(): pl.pallas_call(functools.partial(merge_kernel, (hc, vhead, members, chunk...  2.62 us
    pallas_call x1, Pallas kernels, on_device(): pl.pallas_call(functools.partial(pack_kernel, (hh * nope, hh * rope, cols...  2.07 us
  transfers between devices with their start and end apart: 13, of which 6 were waited for; matrix products, arithmetic and copies ran while one was open for 0% of the time, Pallas kernels for 16%

profile of v2, /device:TPU:0, one launch (start us, length us, event | category | flops | bytes accessed | tf_op | source)
XLA Modules:
  0.0 92.7 jit_solution(13189594152207374188)
XLA Ops:
  0.0 2.1 %pack.1 = (bf16[32,3072]{1,0:T(8,128)(2,1)}, bf16[32,3072]{1,0:T(8,128)(2,1)}, bf16[576,384]{1,0:T(8,128)(2,1)}) custom-call(bf16[32,4096]{1,0:T(8,128)(2,1)} %nope_ref.1, bf16[32,2048]{1,0:T(8,128)(2,1)} %rope_ref.1, bf16[576,1536]{1,0:T(8,128)(2,1)} %bitcast.3), custom_call_target="tpu_custom_call" | custom-call | tf_op jit(solution)/shard_map/pack/pallas_call | solution.py:255
  2.1 3.1 %collective-permute-start.3 = (bf16[576,384]{1,0:T(8,128)(2,1)}, bf16[576,384]{1,0:T(8,128)(2,1)S(1)}, u32[]{:S(2)}, u32[]{:S(2)}) collective-permute-start(bf16[576,384]{1,0:T(8,128)(2,1)} %get-tuple-element.18), channel_id=1, source_target_pairs={{0,4},{4,0},{8,12},{12,8},{1,5},{5,1},{9,13},{13,9},{2,6},{6,2},{1... | collective-permute-start | bytes 1327112 | tf_op jit(solution)/shard_map/ppermute | solution.py:265
  5.2 10.4 %collective-permute-done.3.refs_4_ = bf16[576,384]{1,0:T(8,128)(2,1)S(1)} collective-permute-done((bf16[576,384]{1,0:T(8,128)(2,1)}, bf16[576,384]{1,0:T(8,128)(2,1)S(1)}, u32[]{:S(2)}, u32[]{:S(2)}) %collective-permute-start.3) | collective-permute-done | bytes 442400 | tf_op jit(solution)/shard_map/ppermute | solution.py:265
  15.6 1.7 %collective-permute-start.4 = (bf16[576,384]{1,0:T(8,128)(2,1)S(1)}, bf16[576,384]{1,0:T(8,128)(2,1)S(1)}, u32[]{:S(2)}, u32[]{:S(2)}) collective-permute-start(bf16[576,384]{1,0:T(8,128)(2,1)S(1)} %collective-permute-done.3.refs_4_), channel_id=1, source_target_pairs={{0,2},{1,3},{2,0},{3,1},{4,6},{5,7},{6,4},{7,5},{8,10},{9,11},{10,... | collective-permute-start | bytes 1327112 | tf_op jit(solution)/shard_map/ppermute | solution.py:252
  17.2 9.7 %collective-permute-done.4.refs_5_ = bf16[576,384]{1,0:T(8,128)(2,1)S(1)} collective-permute-done((bf16[576,384]{1,0:T(8,128)(2,1)S(1)}, bf16[576,384]{1,0:T(8,128)(2,1)S(1)}, u32[]{:S(2)}, u32[]{:S(2)}) %collective-permute-start.4) | collective-permute-done | bytes 442400 | tf_op jit(solution)/shard_map/ppermute | solution.py:252
  26.9 2.5 %collective-permute-start.1 = (bf16[32,3072]{1,0:T(8,128)(2,1)}, bf16[32,3072]{1,0:T(8,128)(2,1)S(1)}, u32[]{:S(2)}, u32[]{:S(2)}) collective-permute-start(bf16[32,3072]{1,0:T(8,128)(2,1)} %get-tuple-element.16.refs_0_), channel_id=1, source_target_pairs={{0,8},{4,12},{8,0},{12,4},{1,9},{5,13},{9,1},{13,5},{2,10},{6,14},... | collective-permute-start | bytes 589832 | tf_op jit(solution)/shard_map/ppermute | solution.py:249
  29.4 1.3 %collective-permute-start = (bf16[32,3072]{1,0:T(8,128)(2,1)}, bf16[32,3072]{1,0:T(8,128)(2,1)S(1)}, u32[]{:S(2)}, u32[]{:S(2)}) collective-permute-start(bf16[32,3072]{1,0:T(8,128)(2,1)} %get-tuple-element.17), channel_id=1, source_target_pairs={{0,12},{4,0},{8,4},{12,8},{1,13},{5,1},{9,5},{13,9},{2,14},{6,2},{... | collective-permute-start | bytes 589832 | tf_op jit(solution)/shard_map/ppermute | solution.py:249
  30.7 0.7 collective-permute-start.2
  31.4 8.7 %collective-permute-done.1.refs_2_ = bf16[32,3072]{1,0:T(8,128)(2,1)S(1)} collective-permute-done((bf16[32,3072]{1,0:T(8,128)(2,1)}, bf16[32,3072]{1,0:T(8,128)(2,1)S(1)}, u32[]{:S(2)}, u32[]{:S(2)}) %collective-permute-start.1) | collective-permute-done | bytes 196640 | tf_op jit(solution)/shard_map/ppermute | solution.py:249
  40.1 4.7 %collective-permute-done.2.refs_3_ = bf16[32,3072]{1,0:T(8,128)(2,1)S(1)} collective-permute-done((bf16[32,3072]{1,0:T(8,128)(2,1)}, bf16[32,3072]{1,0:T(8,128)(2,1)S(1)}, u32[]{:S(2)}, u32[]{:S(2)}) %collective-permute-start.2) | collective-permute-done | bytes 196640 | tf_op jit(solution)/shard_map/ppermute | solution.py:249
  44.9 0.6 copy-done.12
  45.5 0.2 copy-done.8
  45.7 0.2 copy-done.9
  45.9 14.6 %attend1.1 = (bf16[32,1152]{1,0:T(8,128)(2,1)}, bf16[32,1152]{1,0:T(8,128)(2,1)}, bf16[32,1152]{1,0:T(8,128)(2,1)}, bf16[32,1152]{1,0:T(8,128)(2,1)}) custom-call(s32[4]{0:T(128)} %counts_ref.3, s32[1,128]{1,0:T(1,128)} %bitcast.6, s32[1,128]{1,0:T(1,128)} %bitcast.8, bf16[32,3072]{1,0:T(8,128)(2,1)} %get-tuple-element.16.refs_0_, ...), custom_call_target="tpu_custom_call" | custom-call | flops 4000000000 | bytes 8000000 | tf_op jit(solution)/shard_map/attend1/pallas_call | solution.py:277
  60.5 0.1 collective-permute-start.10
  60.5 5.3 %collective-permute-start.11 = (bf16[32,1152]{1,0:T(8,128)(2,1)}, bf16[32,1152]{1,0:T(8,128)(2,1)S(1)}, u32[]{:S(2)}, u32[]{:S(2)}) collective-permute-start(bf16[32,1152]{1,0:T(8,128)(2,1)} %get-tuple-element.25), channel_id=1, source_target_pairs={{0,8},{4,12},{8,0},{12,4},{1,9},{5,13},{9,1},{13,5},{2,10},{6,14},... | collective-permute-start | bytes 221192 | tf_op jit(solution)/shard_map/ppermute | solution.py:249
  65.9 14.6 %attend0.1 = (bf16[32,1152]{1,0:T(8,128)(2,1)}, bf16[32,1152]{1,0:T(8,128)(2,1)}, bf16[32,1152]{1,0:T(8,128)(2,1)}, bf16[32,1152]{1,0:T(8,128)(2,1)}) custom-call(s32[4]{0:T(128)} %counts_ref.3, s32[1,128]{1,0:T(1,128)} %bitcast.7, s32[1,128]{1,0:T(1,128)} %bitcast.9, bf16[32,3072]{1,0:T(8,128)(2,1)} %get-tuple-element.16.refs_0_, ...), custom_call_target="tpu_custom_call" | custom-call | flops 4000000000 | bytes 8000000 | tf_op jit(solution)/shard_map/attend0/pallas_call | solution.py:277
  80.5 0.1 collective-permute-start.7
  80.6 2.0 %collective-permute-start.8 = (bf16[32,1152]{1,0:T(8,128)(2,1)}, bf16[32,1152]{1,0:T(8,128)(2,1)S(1)}, u32[]{:S(2)}, u32[]{:S(2)}) collective-permute-start(bf16[32,1152]{1,0:T(8,128)(2,1)} %get-tuple-element.21), channel_id=1, source_target_pairs={{0,8},{4,12},{8,0},{12,4},{1,9},{5,13},{9,1},{13,5},{2,10},{6,14},... | collective-permute-start | bytes 221192 | tf_op jit(solution)/shard_map/ppermute | solution.py:249
  82.6 0.1 collective-permute-start.9
  82.7 2.8 %collective-permute-done.7.refs_1_ = bf16[32,1152]{1,0:T(8,128)(2,1)S(1)} collective-permute-done((bf16[32,1152]{1,0:T(8,128)(2,1)}, bf16[32,1152]{1,0:T(8,128)(2,1)S(1)}, u32[]{:S(2)}, u32[]{:S(2)}) %collective-permute-start.7) | collective-permute-done | bytes 73760 | tf_op jit(solution)/shard_map/ppermute | solution.py:249
  85.4 3.9 %collective-permute-done.8.refs_2_ = bf16[32,1152]{1,0:T(8,128)(2,1)S(1)} collective-permute-done((bf16[32,1152]{1,0:T(8,128)(2,1)}, bf16[32,1152]{1,0:T(8,128)(2,1)S(1)}, u32[]{:S(2)}, u32[]{:S(2)}) %collective-permute-start.8) | collective-permute-done | bytes 73760 | tf_op jit(solution)/shard_map/ppermute | solution.py:249
  89.4 0.6 copy-done.4
  90.1 2.6 %merge.1 = bf16[32,4096]{1,0:T(8,128)(2,1)} custom-call(bf16[32,1152]{1,0:T(8,128)(2,1)} %get-tuple-element.19.refs_0_, bf16[32,1152]{1,0:T(8,128)(2,1)} %copy-done.3, bf16[32,1152]{1,0:T(8,128)(2,1)} %copy-done.4, bf16[32,1152]{1,0:T(8,128)(2,1)} %copy-done.5, bf16[32,1152]{1,0:T(8,128)(2,1)} %get-tuple-element.23.refs_4_, bf16[32,1152]{1,0:T(8,128)(2,1)} %copy-done, ...), custom_call_target="tpu_custom_call" | custom-call | tf_op jit(solution)/shard_map/merge/pallas_call | solution.py:304
  (32 shorter events, 0.1 us)
Async XLA Ops:
  2.1 13.5 %collective-permute-start.3 = (bf16[576,384]{1,0:T(8,128)(2,1)}, bf16[576,384]{1,0:T(8,128)(2,1)S(1)}, u32[]{:S(2)}, u32[]{:S(2)}) collective-permute-start(bf16[576,384]{1,0:T(8,128)(2,1)} %get-tuple-element.18), channel_id=1, source_target_pairs={{0,4},{4,0},{8,12},{12,8},{1,5},{5,1},{9,13},{13,9},{2,6},{6,2},{1... | collective-permute-start | bytes 1327112 | tf_op jit(solution)/shard_map/ppermute | solution.py:265
  15.6 29.3 %copy-start.6 = (bf16[576,384]{1,0:T(8,128)(2,1)}, bf16[576,384]{1,0:T(8,128)(2,1)S(1)}, u32[]{:S(2)}) copy-start(bf16[576,384]{1,0:T(8,128)(2,1)S(1)} %collective-permute-done.3.refs_4_) | copy-start | bytes 1327108
  15.6 11.3 %collective-permute-start.4 = (bf16[576,384]{1,0:T(8,128)(2,1)S(1)}, bf16[576,384]{1,0:T(8,128)(2,1)S(1)}, u32[]{:S(2)}, u32[]{:S(2)}) collective-permute-start(bf16[576,384]{1,0:T(8,128)(2,1)S(1)} %collective-permute-done.3.refs_4_), channel_id=1, source_target_pairs={{0,2},{1,3},{2,0},{3,1},{4,6},{5,7},{6,4},{7,5},{8,10},{9,11},{10,... | collective-permute-start | bytes 1327112 | tf_op jit(solution)/shard_map/ppermute | solution.py:252
  17.2 27.6 %collective-permute-start.5 = (bf16[576,384]{1,0:T(8,128)(2,1)S(1)}, bf16[576,384]{1,0:T(8,128)(2,1)S(1)}, u32[]{:S(2)}, u32[]{:S(2)}) collective-permute-start(bf16[576,384]{1,0:T(8,128)(2,1)S(1)} %collective-permute-done.3.refs_4_), channel_id=1, source_target_pairs={{0,1},{1,0},{2,3},{3,2},{4,5},{5,4},{6,7},{7,6},{8,9},{9,8},{10,11... | collective-permute-start | bytes 1327112 | tf_op jit(solution)/shard_map/ppermute | solution.py:252
  26.9 17.9 %copy-start.7 = (bf16[576,384]{1,0:T(8,128)(2,1)}, bf16[576,384]{1,0:T(8,128)(2,1)S(1)}, u32[]{:S(2)}) copy-start(bf16[576,384]{1,0:T(8,128)(2,1)S(1)} %collective-permute-done.4.refs_5_) | copy-start | bytes 1327108
  26.9 17.9 %collective-permute-start.6 = (bf16[576,384]{1,0:T(8,128)(2,1)S(1)}, bf16[576,384]{1,0:T(8,128)(2,1)S(1)}, u32[]{:S(2)}, u32[]{:S(2)}) collective-permute-start(bf16[576,384]{1,0:T(8,128)(2,1)S(1)} %collective-permute-done.4.refs_5_), channel_id=1, source_target_pairs={{0,1},{1,0},{2,3},{3,2},{4,5},{5,4},{6,7},{7,6},{8,9},{9,8},{10,11... | collective-permute-start | bytes 1327112 | tf_op jit(solution)/shard_map/ppermute | solution.py:252
  26.9 13.2 %collective-permute-start.1 = (bf16[32,3072]{1,0:T(8,128)(2,1)}, bf16[32,3072]{1,0:T(8,128)(2,1)S(1)}, u32[]{:S(2)}, u32[]{:S(2)}) collective-permute-start(bf16[32,3072]{1,0:T(8,128)(2,1)} %get-tuple-element.16.refs_0_), channel_id=1, source_target_pairs={{0,8},{4,12},{8,0},{12,4},{1,9},{5,13},{9,1},{13,5},{2,10},{6,14},... | collective-permute-start | bytes 589832 | tf_op jit(solution)/shard_map/ppermute | solution.py:249
  29.4 10.7 %collective-permute-start = (bf16[32,3072]{1,0:T(8,128)(2,1)}, bf16[32,3072]{1,0:T(8,128)(2,1)S(1)}, u32[]{:S(2)}, u32[]{:S(2)}) collective-permute-start(bf16[32,3072]{1,0:T(8,128)(2,1)} %get-tuple-element.17), channel_id=1, source_target_pairs={{0,12},{4,0},{8,4},{12,8},{1,13},{5,1},{9,5},{13,9},{2,14},{6,2},{... | collective-permute-start | bytes 589832 | tf_op jit(solution)/shard_map/ppermute | solution.py:249
  30.7 14.1 %collective-permute-start.2 = (bf16[32,3072]{1,0:T(8,128)(2,1)}, bf16[32,3072]{1,0:T(8,128)(2,1)S(1)}, u32[]{:S(2)}, u32[]{:S(2)}) collective-permute-start(bf16[32,3072]{1,0:T(8,128)(2,1)} %get-tuple-element.17), channel_id=1, source_target_pairs={{0,4},{4,8},{8,12},{12,0},{1,5},{5,9},{9,13},{13,1},{2,6},{6,10},{... | collective-permute-start | bytes 589832 | tf_op jit(solution)/shard_map/ppermute | solution.py:249
  40.1 4.8 %copy-start.10 = (bf16[32,3072]{1,0:T(8,128)(2,1)}, bf16[32,3072]{1,0:T(8,128)(2,1)S(1)}, u32[]{:S(2)}) copy-start(bf16[32,3072]{1,0:T(8,128)(2,1)S(1)} %collective-permute-done.1.refs_2_) | copy-start | bytes 589828
  40.1 4.8 %copy-start.11 = (bf16[32,3072]{1,0:T(8,128)(2,1)}, bf16[32,3072]{1,0:T(8,128)(2,1)S(1)}, u32[]{:S(2)}) copy-start(bf16[32,3072]{1,0:T(8,128)(2,1)S(1)} %collective-permute-done.refs_1_) | copy-start | bytes 589828
  44.8 0.7 copy-start.12
  44.8 0.9 copy-start.8
  44.8 1.0 %copy-start.9 = (bf16[576,384]{1,0:T(8,128)(2,1)}, bf16[576,384]{1,0:T(8,128)(2,1)S(1)}, u32[]{:S(2)}) copy-start(bf16[576,384]{1,0:T(8,128)(2,1)S(1)} %collective-permute-done.6.refs_7_) | copy-start | bytes 1327108
  60.5 22.1 %collective-permute-start.10 = (bf16[32,1152]{1,0:T(8,128)(2,1)}, bf16[32,1152]{1,0:T(8,128)(2,1)S(1)}, u32[]{:S(2)}, u32[]{:S(2)}) collective-permute-start(bf16[32,1152]{1,0:T(8,128)(2,1)} %get-tuple-element.24), channel_id=1, source_target_pairs={{0,12},{4,0},{8,4},{12,8},{1,13},{5,1},{9,5},{13,9},{2,14},{6,2},{... | collective-permute-start | bytes 221192 | tf_op jit(solution)/shard_map/ppermute | solution.py:249
  60.5 22.1 %collective-permute-start.11 = (bf16[32,1152]{1,0:T(8,128)(2,1)}, bf16[32,1152]{1,0:T(8,128)(2,1)S(1)}, u32[]{:S(2)}, u32[]{:S(2)}) collective-permute-start(bf16[32,1152]{1,0:T(8,128)(2,1)} %get-tuple-element.25), channel_id=1, source_target_pairs={{0,8},{4,12},{8,0},{12,4},{1,9},{5,13},{9,1},{13,5},{2,10},{6,14},... | collective-permute-start | bytes 221192 | tf_op jit(solution)/shard_map/ppermute | solution.py:249
  65.9 16.8 %collective-permute-start.12 = (bf16[32,1152]{1,0:T(8,128)(2,1)}, bf16[32,1152]{1,0:T(8,128)(2,1)S(1)}, u32[]{:S(2)}, u32[]{:S(2)}) collective-permute-start(bf16[32,1152]{1,0:T(8,128)(2,1)} %get-tuple-element.26), channel_id=1, source_target_pairs={{0,4},{4,8},{8,12},{12,0},{1,5},{5,9},{9,13},{13,1},{2,6},{6,10},{... | collective-permute-start | bytes 221192 | tf_op jit(solution)/shard_map/ppermute | solution.py:249
  80.5 4.9 %collective-permute-start.7 = (bf16[32,1152]{1,0:T(8,128)(2,1)}, bf16[32,1152]{1,0:T(8,128)(2,1)S(1)}, u32[]{:S(2)}, u32[]{:S(2)}) collective-permute-start(bf16[32,1152]{1,0:T(8,128)(2,1)} %get-tuple-element.20), channel_id=1, source_target_pairs={{0,12},{4,0},{8,4},{12,8},{1,13},{5,1},{9,5},{13,9},{2,14},{6,2},{... | collective-permute-start | bytes 221192 | tf_op jit(solution)/shard_map/ppermute | solution.py:249
  80.6 8.8 %collective-permute-start.8 = (bf16[32,1152]{1,0:T(8,128)(2,1)}, bf16[32,1152]{1,0:T(8,128)(2,1)S(1)}, u32[]{:S(2)}, u32[]{:S(2)}) collective-permute-start(bf16[32,1152]{1,0:T(8,128)(2,1)} %get-tuple-element.21), channel_id=1, source_target_pairs={{0,8},{4,12},{8,0},{12,4},{1,9},{5,13},{9,1},{13,5},{2,10},{6,14},... | collective-permute-start | bytes 221192 | tf_op jit(solution)/shard_map/ppermute | solution.py:249
  82.6 6.8 %copy-start = (bf16[32,1152]{1,0:T(8,128)(2,1)}, bf16[32,1152]{1,0:T(8,128)(2,1)S(1)}, u32[]{:S(2)}) copy-start(bf16[32,1152]{1,0:T(8,128)(2,1)S(1)} %collective-permute-done.10.refs_5_) | copy-start | bytes 221188
  82.6 6.8 %collective-permute-start.9 = (bf16[32,1152]{1,0:T(8,128)(2,1)}, bf16[32,1152]{1,0:T(8,128)(2,1)S(1)}, u32[]{:S(2)}, u32[]{:S(2)}) collective-permute-start(bf16[32,1152]{1,0:T(8,128)(2,1)} %get-tuple-element.22), channel_id=1, source_target_pairs={{0,4},{4,8},{8,12},{12,0},{1,5},{5,9},{9,13},{13,1},{2,6},{6,10},{... | collective-permute-start | bytes 221192 | tf_op jit(solution)/shard_map/ppermute | solution.py:249
  82.7 6.7 %copy-start.1 = (bf16[32,1152]{1,0:T(8,128)(2,1)}, bf16[32,1152]{1,0:T(8,128)(2,1)S(1)}, u32[]{:S(2)}) copy-start(bf16[32,1152]{1,0:T(8,128)(2,1)S(1)} %collective-permute-done.11.refs_6_) | copy-start | bytes 221188
  82.7 6.7 %copy-start.2 = (bf16[32,1152]{1,0:T(8,128)(2,1)}, bf16[32,1152]{1,0:T(8,128)(2,1)S(1)}, u32[]{:S(2)}) copy-start(bf16[32,1152]{1,0:T(8,128)(2,1)S(1)} %collective-permute-done.12.refs_7_) | copy-start | bytes 221188
  85.4 4.0 %copy-start.3 = (bf16[32,1152]{1,0:T(8,128)(2,1)}, bf16[32,1152]{1,0:T(8,128)(2,1)S(1)}, u32[]{:S(2)}) copy-start(bf16[32,1152]{1,0:T(8,128)(2,1)S(1)} %collective-permute-done.7.refs_1_) | copy-start | bytes 221188
  (2 other events, 1.3 us)

commit v3 on v2

--- a/solution.py
+++ b/solution.py
@@ -7,6 +7,7 @@
 from jax.experimental.pallas import tpu as pltpu
 from jax.sharding import PartitionSpec as P
 
+
 PAGE = 64
 GROUP = 2
 LANES = 4
@@ -14,66 +15,43 @@
 HEADS_STEP = 4
 CHUNKS = 2
 
+
 FLOOR = -1e30
 FAR = 2**30
 LOG2E = 1.4426950408889634
 
 
-def pack_kernel(dims, nope_ref, rope_ref, cache_ref, share0_ref, share1_ref, quarter_ref, sems):
-    nope_width, rope_width, quarter_cols = dims
+def pack_kernel(dims, nope_ref, rope_ref, cache_ref, *refs):
+    nope_width, rope_width, quarter_cols, chunks = dims
+    outs, sems = refs[:-1], refs[-1]
     mine = lax.axis_index("pages") % GROUP
     lane = lax.axis_index("heads") % LANES
     copies = [
         pltpu.make_async_copy(
-            cache_ref.at[:, pl.ds(pl.multiple_of(lane * quarter_cols, 128), quarter_cols)], quarter_ref, sems.at[0]
+            cache_ref.at[:, pl.ds(pl.multiple_of(lane * quarter_cols, 128), quarter_cols)], outs[0], sems.at[0]
         )
     ]
-    for e, share in enumerate((share0_ref, share1_ref)):
-        which = (mine + e) % GROUP
-        for j, (ref, width, at) in enumerate(((nope_ref, nope_width, 0), (rope_ref, rope_width, nope_width))):
-            copies.append(
-                pltpu.make_async_copy(
-                    ref.at[:, pl.ds(pl.multiple_of(which * width, 128), width)],
-                    share.at[:, pl.ds(at, width)],
-                    sems.at[1 + 2 * e + j],
+    for c in range(chunks):
+        for e in range(GROUP):
+            which = ((mine + e) % GROUP) * chunks + c
+            for ref, width, at in ((nope_ref, nope_width, 0), (rope_ref, rope_width, nope_width)):
+                copies.append(
+                    pltpu.make_async_copy(
+                        ref.at[:, pl.ds(pl.multiple_of(which * width, 128), width)],
+                        outs[1 + c * GROUP + e].at[:, pl.ds(at, width)],
+                        sems.at[len(copies)],
+                    )
                 )
-            )
     for c in copies:
         c.start()
     for c in copies:
         c.wait()
 
 
-def attend_kernel(dims, counts_ref, tok_ref, off_ref, *refs):
-    members, first, hc, hh, hb, nope, rope, latent, vhead, rows, slots = dims
-    q_refs, refs = refs[:members], refs[members:]
-    part_refs, refs = refs[:LANES], refs[LANES:]
-    own_ref, keys_hbm, values_hbm = refs[:3]
-    out_refs, refs = refs[3:3 + members], refs[3 + members:]
-    tiles, wk, wv, bias, qs, sbuf, mx, den, acc, lse, sems = refs
+def prepare_kernel(dims, tok_ref, off_ref, limit_ref, order_ref):
+    members, rows = dims
     local_rows = rows // members
-    block = BLOCK_PAGES * PAGE
-    cols = slots * PAGE
-    scale2 = (nope + rope) ** (-0.5) * LOG2E
-    steps = hc // hb
     member = lax.axis_index("pages")
-    lane_id = lax.axis_index("heads") % LANES
-    partner = member ^ 1
-    mine = member % GROUP
-
-    own_copy = pltpu.make_async_copy(own_ref, tiles.at[:, pl.ds(0, cols)], sems.at[0])
-    own_copy.start()
-    weight_copies = []
-    for g in range(steps):
-        at = pl.ds(mine * hh + first + g * hb, hb)
-        pair = (
-            pltpu.make_async_copy(keys_hbm.at[at], wk.at[pl.ds(g * hb, hb)], sems.at[1 + 2 * g]),
-            pltpu.make_async_copy(values_hbm.at[at], wv.at[pl.ds(g * hb, hb)], sems.at[2 + 2 * g]),
-        )
-        for c in pair:
-            c.start()
-        weight_copies.append(pair)
-
     token = pltpu.roll(
         jnp.broadcast_to(tok_ref[...], (8, rows)), lax.rem(rows - member * local_rows, rows), axis=1
     )[:1]
@@ -81,16 +59,53 @@
     across = lax.broadcasted_iota(jnp.int32, (rows, rows), 1)
     down = lax.broadcasted_iota(jnp.int32, (rows, rows), 0)
     limit = jnp.max(jnp.where(token_down == across, off_ref[...], 0), axis=1, keepdims=True)
+    limit_ref[...] = jnp.broadcast_to(limit, limit_ref.shape)
     owner = lax.rem(member - down // local_rows + members, members)
-    order = (jnp.broadcast_to(token, (rows, rows)) == owner * local_rows + lax.rem(down, local_rows)).astype(
-        jnp.bfloat16
-    )
-
+    order_ref[...] = (
+        jnp.broadcast_to(token, (rows, rows)) == owner * local_rows + lax.rem(down, local_rows)
+    ).astype(jnp.bfloat16)
+
+
+def attend_kernel(dims, counts_ref, limit_ref, order_ref, *refs):
+    members, first, hc, hh, hb, nope, rope, latent, vhead, rows, slots = dims
+    q_refs, refs = refs[:members], refs[members:]
+    part_refs, refs = refs[:LANES], refs[LANES:]
+    own_ref, keys_hbm, values_hbm = refs[:3]
+    out_refs, refs = refs[3:3 + members], refs[3 + members:]
+    tiles, wk, wv, bias, qs, sbuf, mx, den, acc, lse, sems, tile_sems = refs
+    local_rows = rows // members
+    block = BLOCK_PAGES * PAGE
+    cols = slots * PAGE
     quarter_cols = cols // LANES
-    for ref, flip in zip(part_refs, (0, 2, 1, 3)):
+    scale2 = (nope + rope) ** (-0.5) * LOG2E
+    steps = hc // hb
+    member = lax.axis_index("pages")
+    lane_id = lax.axis_index("heads") % LANES
+    partner = member ^ 1
+    mine = member % GROUP
+
+    weight_copies = []
+    for g in range(steps):
+        at = pl.ds(mine * hh + first + g * hb, hb)
+        weight_copies.append((
+            pltpu.make_async_copy(keys_hbm.at[at], wk.at[pl.ds(g * hb, hb)], sems.at[2 * g]),
+            pltpu.make_async_copy(values_hbm.at[at], wv.at[pl.ds(g * hb, hb)], sems.at[1 + 2 * g]),
+        ))
+    tile_copies = [pltpu.make_async_copy(own_ref, tiles.at[:, pl.ds(0, cols)], tile_sems.at[0])]
+    for i, (ref, flip) in enumerate(zip(part_refs, (0, 2, 1, 3))):
         at = pl.multiple_of(cols + (lane_id ^ flip) * quarter_cols, 128)
-        tiles[:, pl.ds(at, quarter_cols)] = ref[...]
+        tile_copies.append(pltpu.make_async_copy(ref, tiles.at[:, pl.ds(at, quarter_cols)], tile_sems.at[1 + i]))
+    weight_copies[0][0].start()
+    for c in tile_copies:
+        c.start()
+    weight_copies[0][1].start()
+    for pair in weight_copies[1:]:
+        for c in pair:
+            c.start()
+
     before = lambda who: lax.fori_loop(0, who, lambda i, total: total + counts_ref[i], jnp.int32(0))
+    limit = limit_ref[:, :1]
+    order = order_ref[...]
     own_live, part_live = counts_ref[member], counts_ref[partner]
     own_base, part_base = before(member) * PAGE, before(partner) * PAGE
     own_blocks = (own_live + BLOCK_PAGES - 1) // BLOCK_PAGES
@@ -111,19 +126,17 @@
 
     lax.fori_loop(0, blocks, fill_bias, 0)
     lse[...] = jnp.zeros_like(lse)
-    queries = [jnp.concatenate([q[:, (first + h) * nope:(first + h + 1) * nope] for q in q_refs], axis=0)
-               for h in range(hc)]
-    own_copy.wait()
 
     def absorb(g):
         slot = g % 2
         weight_copies[g][0].wait()
         for e in range(hb):
             h = g * hb + e
-            lat = jnp.dot(queries[h], wk[h], preferred_element_type=jnp.float32)
+            query = jnp.concatenate([q[:, h * nope:(h + 1) * nope] for q in q_refs], axis=0)
+            lat = jnp.dot(query, wk[h], preferred_element_type=jnp.float32)
             qs[slot, e * rows:(e + 1) * rows, :latent] = lat.astype(jnp.bfloat16)
         for e in range(0, hb, 2):
-            at = hh * nope + (first + g * hb + e) * rope
+            at = hc * nope + (g * hb + e) * rope
             both = jnp.concatenate([q[:, at:at + 2 * rope] for q in q_refs], axis=0)
             for i in range(2):
                 qs[slot, (e + i) * rows:(e + i + 1) * rows, latent:] = both[:, i * rope:(i + 1) * rope]
@@ -180,6 +193,9 @@
     for g in range(steps + 1):
         if g < steps:
             absorb(g)
+        if g == 0:
+            for c in tile_copies:
+                c.wait()
         if g > 0:
             den[...] = jnp.zeros_like(den)
             acc[...] = jnp.zeros_like(acc)
@@ -252,19 +268,31 @@
         return lax.ppermute(x, "heads", [(i, i ^ bit) for i in range(devices)])
 
     turned = cache_tiles.T
-    share0, share1, quarter = pl.pallas_call(
-        functools.partial(pack_kernel, (hh * nope, hh * rope, cols // LANES)),
-        out_shape=[jax.ShapeDtypeStruct((local_rows, hh * (nope + rope)), bf16)] * 2
-        + [jax.ShapeDtypeStruct((full, cols // LANES), bf16)],
+    quarter, *shares = pl.pallas_call(
+        functools.partial(pack_kernel, (hc * nope, hc * rope, cols // LANES, chunks)),
+        out_shape=[jax.ShapeDtypeStruct((full, cols // LANES), bf16)]
+        + [jax.ShapeDtypeStruct((local_rows, hc * (nope + rope)), bf16)] * (GROUP * chunks),
         in_specs=[hbm] * 3,
-        out_specs=[vmem] * 3,
-        scratch_shapes=[pltpu.SemaphoreType.DMA((5,))],
+        out_specs=[vmem] * (1 + GROUP * chunks),
+        scratch_shapes=[pltpu.SemaphoreType.DMA((1 + 2 * GROUP * chunks,))],
         name="pack",
     )(q_nope, q_rope, turned)
+    limits, order = pl.pallas_call(
+        functools.partial(prepare_kernel, (members, rows)),
+        out_shape=[jax.ShapeDtypeStruct((rows, 128), jnp.int32), jax.ShapeDtypeStruct((rows, rows), bf16)],
+        in_specs=[vmem] * 2,
+        out_specs=[vmem] * 2,
+        name="prepare",
+    )(query_token[None, :], query_offsets[None, :])
 
     part0 = lax.ppermute(quarter, "pages", [(i, i ^ 1) for i in range(members)])
-    shares = (share0, share1)
-    queries = [share0] + [over_pages(shares[s % GROUP], s) for s in range(1, members)]
+    queries = []
+    for c in range(chunks):
+        own, other = shares[c * GROUP:(c + 1) * GROUP]
+        sent = {}
+        for s in sorted(range(1, members), key=lambda s: s % GROUP):
+            sent[s] = over_pages((own, other)[s % GROUP], s)
+        queries.append([own] + [sent[s] for s in range(1, members)])
     part1 = over_heads(part0, 2)
     part2 = over_heads(part0, 1)
     part3 = over_heads(part1, 1)
@@ -279,7 +307,7 @@
                 attend_kernel, (members, c * hc, hc, hh, hb, nope, rope, latent, vhead, rows, slots)
             ),
             out_shape=[jax.ShapeDtypeStruct((local_rows, packed), bf16)] * members,
-            in_specs=[pl.BlockSpec(memory_space=pltpu.SMEM)] + [vmem] * (2 + members + LANES) + [hbm] * 3,
+            in_specs=[pl.BlockSpec(memory_space=pltpu.SMEM)] + [vmem] * (2 + members) + [hbm] * (LANES + 3),
             out_specs=[vmem] * members,
             scratch_shapes=[
                 pltpu.VMEM((full, 2 * cols), bf16),
@@ -292,14 +320,16 @@
                 pltpu.VMEM((hb * rows, 128), jnp.float32),
                 pltpu.VMEM((hb * rows, latent), jnp.float32),
                 pltpu.VMEM((rows, 128), jnp.float32),
-                pltpu.SemaphoreType.DMA((1 + 2 * (hc // hb),)),
+                pltpu.SemaphoreType.DMA((2 * (hc // hb),)),
+                pltpu.SemaphoreType.DMA((1 + LANES,)),
             ],
             compiler_params=pltpu.CompilerParams(vmem_limit_bytes=56 << 20),
             cost_estimate=pl.CostEstimate(flops=8 * 10**9 // chunks, bytes_accessed=8 * 10**6, transcendentals=0),
-            name=f"attend{c}",
-        )(page_counts, query_token[None, :], query_offsets[None, :], *queries, part0, part1, part2, part3,
+        )(page_counts, limits, order, *queries[c], part0, part1, part2, part3,
           turned, absorb_keys, absorb_values)
-        arrived += [outs[0]] + [over_pages(outs[s], s) for s in range(1, members)]
+        arrived.append(outs[0])
+        for s in range(1, members):
+            arrived.append(over_pages(outs[s], s))
 
     return pl.pallas_call(
         functools.partial(merge_kernel, (hc, vhead, members, chunks)),

time: 94.1 us -> 90.8 us (0.965); the launches traced: 92.7 us -> 90.5 us
  starting transfers between devices: 16.8 us -> 31.3 us
  waiting for transfers between devices: 40.2 us -> 28.8 us
  Pallas kernels: 33.9 us -> 27.5 us
  local copies, waits for them, and re-layouts: 1.64 us -> 2.76 us
    ppermute x9 -> x12, starting transfers between devices: 12 us -> 26.5 us  [over_pages(): lax.ppermute(x, 'pages', [(i, (i - s) % members) for i in range(members)])]
    ppermute x9 -> x12, waiting for transfers between devices: 20.1 us -> 8.72 us  [over_pages(): lax.ppermute(x, 'pages', [(i, (i - s) % members) for i in range(members)])]
    pallas_call x2, Pallas kernels: 29.2 us -> 21.2 us  [on_device(): pl.pallas_call(functools.partial(attend_kernel, (members, c * hc, hc, hh,...]
    pallas_call x1 -> x2, Pallas kernels: 2.07 us -> 3.68 us  [the longest x1 2.05 us: on_device(): pl.pallas_call(functools.partial(pack_kernel, (hc * nope, hc * rope, cols...]
    unnamed x26 -> x32, local copies, waits for them, and re-layouts: 1.64 us -> 2.76 us
  transfers between devices with their start and end apart: 13 -> 16, of which waited for: 6 -> 7; matrix products, arithmetic and copies ran while one was open for 0% -> 0% of each run, Pallas kernels for 16% -> 25%
where the time goes in v3:
time: 90.8 us; the launch traced here: 90.5 us
  starting transfers between devices  31.3 us (34%)
  waiting for transfers between devices  28.8 us (32%)
  Pallas kernels  27.5 us (30%)
  local copies, waits for them, and re-layouts  2.76 us (3%)
    ppermute x12, starting transfers between devices, over_pages(): lax.ppermute(x, 'pages', [(i, (i - s) % members) for i in range(members)])  26.5 us
    pallas_call x2, Pallas kernels, on_device(): pl.pallas_call(functools.partial(attend_kernel, (members, c * hc, hc, hh,...  21.2 us
    ppermute x1, waiting for transfers between devices, on_device(): part0 = lax.ppermute(quarter, 'pages', [(i, i ^ 1) for i in range(members)])  10.4 us
    ppermute x3, waiting for transfers between devices, over_heads(): return lax.ppermute(x, 'heads', [(i, i ^ bit) for i in range(devices)])  9.68 us
    ppermute x12, waiting for transfers between devices, over_pages(): lax.ppermute(x, 'pages', [(i, (i - s) % members) for i in range(members)])  8.72 us
    ppermute x1, starting transfers between devices, on_device(): part0 = lax.ppermute(quarter, 'pages', [(i, i ^ 1) for i in range(members)])  3.12 us
    unnamed x32, local copies, waits for them, and re-layouts  2.76 us
    pallas_call x1, Pallas kernels, on_device(): pl.pallas_call(functools.partial(merge_kernel, (hc, vhead, members, chunk...  2.62 us
  transfers between devices with their start and end apart: 16, of which 7 were waited for; matrix products, arithmetic and copies ran while one was open for 0% of the time, Pallas kernels for 25%

profile of v3, /device:TPU:0, one launch (start us, length us, event | category | flops | bytes accessed | tf_op | source)
XLA Modules:
  0.0 90.5 jit_solution(10929074815790874538)
XLA Ops:
  0.0 2.1 %pack.1 = (bf16[576,384]{1,0:T(8,128)(2,1)}, bf16[32,1536]{1,0:T(8,128)(2,1)}, bf16[32,1536]{1,0:T(8,128)(2,1)}, bf16[32,1536]{1,0:T(8,128)(2,1)}, bf16[32,1536]{1,0:T(8,128)(2,1)}) custom-call(bf16[32,4096]{1,0:T(8,128)(2,1)} %nope_ref.1, bf16[32,2048]{1,0:T(8,128)(2,1)} %rope_ref.1, bf16[576,1536]{1,0:T(8,128)(2,1)} %bitcast.3), custom_call_target="tpu_custom_call" | custom-call | tf_op jit(solution)/shard_map/pack/pallas_call | solution.py:271
  2.1 3.1 %collective-permute-start.3 = (bf16[576,384]{1,0:T(8,128)(2,1)}, bf16[576,384]{1,0:T(8,128)(2,1)S(1)}, u32[]{:S(2)}, u32[]{:S(2)}) collective-permute-start(bf16[576,384]{1,0:T(8,128)(2,1)} %get-tuple-element.24), channel_id=1, source_target_pairs={{0,4},{4,0},{8,12},{12,8},{1,5},{5,1},{9,13},{13,9},{2,6},{6,2},{1... | collective-permute-start | bytes 1327112 | tf_op jit(solution)/shard_map/ppermute | solution.py:288
  5.2 10.4 %collective-permute-done.3.refs_4_ = bf16[576,384]{1,0:T(8,128)(2,1)S(1)} collective-permute-done((bf16[576,384]{1,0:T(8,128)(2,1)}, bf16[576,384]{1,0:T(8,128)(2,1)S(1)}, u32[]{:S(2)}, u32[]{:S(2)}) %collective-permute-start.3) | collective-permute-done | bytes 442400 | tf_op jit(solution)/shard_map/ppermute | solution.py:288
  15.6 1.7 %collective-permute-start.4 = (bf16[576,384]{1,0:T(8,128)(2,1)S(1)}, bf16[576,384]{1,0:T(8,128)(2,1)S(1)}, u32[]{:S(2)}, u32[]{:S(2)}) collective-permute-start(bf16[576,384]{1,0:T(8,128)(2,1)S(1)} %collective-permute-done.3.refs_4_), channel_id=1, source_target_pairs={{0,2},{1,3},{2,0},{3,1},{4,6},{5,7},{6,4},{7,5},{8,10},{9,11},{10,... | collective-permute-start | bytes 1327112 | tf_op jit(solution)/shard_map/ppermute | solution.py:268
  17.2 9.7 %collective-permute-done.4.refs_5_ = bf16[576,384]{1,0:T(8,128)(2,1)S(1)} collective-permute-done((bf16[576,384]{1,0:T(8,128)(2,1)S(1)}, bf16[576,384]{1,0:T(8,128)(2,1)S(1)}, u32[]{:S(2)}, u32[]{:S(2)}) %collective-permute-start.4) | collective-permute-done | bytes 442400 | tf_op jit(solution)/shard_map/ppermute | solution.py:268
  26.9 3.5 %collective-permute-start.10 = (bf16[32,1536]{1,0:T(8,128)(2,1)}, bf16[32,1536]{1,0:T(8,128)(2,1)S(1)}, u32[]{:S(2)}, u32[]{:S(2)}) collective-permute-start(bf16[32,1536]{1,0:T(8,128)(2,1)} %get-tuple-element.30), channel_id=1, source_target_pairs={{0,12},{4,0},{8,4},{12,8},{1,13},{5,1},{9,5},{13,9},{2,14},{6,2},{... | collective-permute-start | bytes 294920 | tf_op jit(solution)/shard_map/ppermute | solution.py:265
  30.4 1.0 %collective-permute-start.12 = (bf16[32,1536]{1,0:T(8,128)(2,1)}, bf16[32,1536]{1,0:T(8,128)(2,1)S(1)}, u32[]{:S(2)}, u32[]{:S(2)}) collective-permute-start(bf16[32,1536]{1,0:T(8,128)(2,1)} %get-tuple-element.30), channel_id=1, source_target_pairs={{0,4},{4,8},{8,12},{12,0},{1,5},{5,9},{9,13},{13,1},{2,6},{6,10},{... | collective-permute-start | bytes 294920 | tf_op jit(solution)/shard_map/ppermute | solution.py:265
  31.4 1.6 %prepare.1 = (s32[128,128]{1,0:T(8,128)}, bf16[128,128]{1,0:T(8,128)(2,1)}) custom-call(s32[1,128]{1,0:T(1,128)} %bitcast.6, s32[1,128]{1,0:T(1,128)} %bitcast.7), custom_call_target="tpu_custom_call" | custom-call | tf_op jit(solution)/shard_map/prepare/pallas_call | solution.py:280
  33.0 0.9 collective-permute-done.10.refs_1_
  33.9 4.2 %collective-permute-start = (bf16[32,1536]{1,0:T(8,128)(2,1)}, bf16[32,1536]{1,0:T(8,128)(2,1)S(1)}, u32[]{:S(2)}, u32[]{:S(2)}) collective-permute-start(bf16[32,1536]{1,0:T(8,128)(2,1)} %get-tuple-element.23), channel_id=1, source_target_pairs={{0,12},{4,0},{8,4},{12,8},{1,13},{5,1},{9,5},{13,9},{2,14},{6,2},{... | collective-permute-start | bytes 294920 | tf_op jit(solution)/shard_map/ppermute | solution.py:265
  38.2 2.5 %collective-permute-done.11.refs_2_ = bf16[32,1536]{1,0:T(8,128)(2,1)S(1)} collective-permute-done((bf16[32,1536]{1,0:T(8,128)(2,1)}, bf16[32,1536]{1,0:T(8,128)(2,1)S(1)}, u32[]{:S(2)}, u32[]{:S(2)}) %collective-permute-start.11) | collective-permute-done | bytes 98336 | tf_op jit(solution)/shard_map/ppermute | solution.py:265
  40.7 4.3 %collective-permute-start.1 = (bf16[32,1536]{1,0:T(8,128)(2,1)}, bf16[32,1536]{1,0:T(8,128)(2,1)S(1)}, u32[]{:S(2)}, u32[]{:S(2)}) collective-permute-start(bf16[32,1536]{1,0:T(8,128)(2,1)} %get-tuple-element.22.refs_0_), channel_id=1, source_target_pairs={{0,8},{4,12},{8,0},{12,4},{1,9},{5,13},{9,1},{13,5},{2,10},{6,14},... | collective-permute-start | bytes 294920 | tf_op jit(solution)/shard_map/ppermute | solution.py:265
  45.1 0.7 copy-done.8
  46.0 10.6 %shard_map.83 = (bf16[32,1152]{1,0:T(8,128)(2,1)}, bf16[32,1152]{1,0:T(8,128)(2,1)}, bf16[32,1152]{1,0:T(8,128)(2,1)}, bf16[32,1152]{1,0:T(8,128)(2,1)}) custom-call(s32[4]{0:T(128)} %counts_ref.3, s32[128,128]{1,0:T(8,128)} %get-tuple-element.20.limit_ref, bf16[128,128]{1,0:T(8,128)(2,1)} %get-tuple-element.21.order_ref, ...), custom_call_target="tpu_custom_call" | custom-call | flops 4000000000 | bytes 8000000 | tf_op jit(solution)/shard_map/pallas_call | solution.py:305
  56.6 4.5 %collective-permute-start.13 = (bf16[32,1152]{1,0:T(8,128)(2,1)}, bf16[32,1152]{1,0:T(8,128)(2,1)S(1)}, u32[]{:S(2)}, u32[]{:S(2)}) collective-permute-start(bf16[32,1152]{1,0:T(8,128)(2,1)} %get-tuple-element.32), channel_id=1, source_target_pairs={{0,12},{4,0},{8,4},{12,8},{1,13},{5,1},{9,5},{13,9},{2,14},{6,2},{... | collective-permute-start | bytes 221192 | tf_op jit(solution)/shard_map/ppermute | solution.py:265
  61.1 1.5 %collective-permute-start.15 = (bf16[32,1152]{1,0:T(8,128)(2,1)}, bf16[32,1152]{1,0:T(8,128)(2,1)S(1)}, u32[]{:S(2)}, u32[]{:S(2)}) collective-permute-start(bf16[32,1152]{1,0:T(8,128)(2,1)} %get-tuple-element.34), channel_id=1, source_target_pairs={{0,4},{4,8},{8,12},{12,0},{1,5},{5,9},{9,13},{13,1},{2,6},{6,10},{... | collective-permute-start | bytes 221192 | tf_op jit(solution)/shard_map/ppermute | solution.py:265
  63.2 0.6 copy-done.11
  63.9 10.6 %shard_map.82 = (bf16[32,1152]{1,0:T(8,128)(2,1)}, bf16[32,1152]{1,0:T(8,128)(2,1)}, bf16[32,1152]{1,0:T(8,128)(2,1)}, bf16[32,1152]{1,0:T(8,128)(2,1)}) custom-call(s32[4]{0:T(128)} %counts_ref.3, s32[128,128]{1,0:T(8,128)} %get-tuple-element.20.limit_ref, bf16[128,128]{1,0:T(8,128)(2,1)} %get-tuple-element.21.order_ref, ...), custom_call_target="tpu_custom_call" | custom-call | flops 4000000000 | bytes 8000000 | tf_op jit(solution)/shard_map/pallas_call | solution.py:305
  74.5 6.3 %collective-permute-start.7 = (bf16[32,1152]{1,0:T(8,128)(2,1)}, bf16[32,1152]{1,0:T(8,128)(2,1)S(1)}, u32[]{:S(2)}, u32[]{:S(2)}) collective-permute-start(bf16[32,1152]{1,0:T(8,128)(2,1)} %get-tuple-element.26), channel_id=1, source_target_pairs={{0,12},{4,0},{8,4},{12,8},{1,13},{5,1},{9,5},{13,9},{2,14},{6,2},{... | collective-permute-start | bytes 221192 | tf_op jit(solution)/shard_map/ppermute | solution.py:265
  80.8 1.1 %collective-permute-start.9 = (bf16[32,1152]{1,0:T(8,128)(2,1)}, bf16[32,1152]{1,0:T(8,128)(2,1)S(1)}, u32[]{:S(2)}, u32[]{:S(2)}) collective-permute-start(bf16[32,1152]{1,0:T(8,128)(2,1)} %get-tuple-element.28), channel_id=1, source_target_pairs={{0,4},{4,8},{8,12},{12,0},{1,5},{5,9},{9,13},{13,1},{2,6},{6,10},{... | collective-permute-start | bytes 221192 | tf_op jit(solution)/shard_map/ppermute | solution.py:265
  81.9 1.2 %collective-permute-done.7.refs_1_ = bf16[32,1152]{1,0:T(8,128)(2,1)S(1)} collective-permute-done((bf16[32,1152]{1,0:T(8,128)(2,1)}, bf16[32,1152]{1,0:T(8,128)(2,1)S(1)}, u32[]{:S(2)}, u32[]{:S(2)}) %collective-permute-start.7) | collective-permute-done | bytes 73760 | tf_op jit(solution)/shard_map/ppermute | solution.py:265
  83.1 3.2 %collective-permute-done.8.refs_2_ = bf16[32,1152]{1,0:T(8,128)(2,1)S(1)} collective-permute-done((bf16[32,1152]{1,0:T(8,128)(2,1)}, bf16[32,1152]{1,0:T(8,128)(2,1)S(1)}, u32[]{:S(2)}, u32[]{:S(2)}) %collective-permute-start.8) | collective-permute-done | bytes 73760 | tf_op jit(solution)/shard_map/ppermute | solution.py:265
  86.3 1.0 %collective-permute-done.9.refs_3_ = bf16[32,1152]{1,0:T(8,128)(2,1)S(1)} collective-permute-done((bf16[32,1152]{1,0:T(8,128)(2,1)}, bf16[32,1152]{1,0:T(8,128)(2,1)S(1)}, u32[]{:S(2)}, u32[]{:S(2)}) %collective-permute-start.9) | collective-permute-done | bytes 73760 | tf_op jit(solution)/shard_map/ppermute | solution.py:265
  87.8 2.6 %merge.1 = bf16[32,4096]{1,0:T(8,128)(2,1)} custom-call(bf16[32,1152]{1,0:T(8,128)(2,1)} %get-tuple-element.25.refs_0_, bf16[32,1152]{1,0:T(8,128)(2,1)} %copy-done.3, bf16[32,1152]{1,0:T(8,128)(2,1)} %copy-done.4, bf16[32,1152]{1,0:T(8,128)(2,1)} %copy-done.5, bf16[32,1152]{1,0:T(8,128)(2,1)} %get-tuple-element.31.refs_4_, bf16[32,1152]{1,0:T(8,128)(2,1)} %copy-done, ...), custom_call_target="tpu_custom_call" | custom-call | tf_op jit(solution)/shard_map/merge/pallas_call | solution.py:334
  (45 shorter events, 1.4 us)
Async XLA Ops:
  2.1 13.5 %collective-permute-start.3 = (bf16[576,384]{1,0:T(8,128)(2,1)}, bf16[576,384]{1,0:T(8,128)(2,1)S(1)}, u32[]{:S(2)}, u32[]{:S(2)}) collective-permute-start(bf16[576,384]{1,0:T(8,128)(2,1)} %get-tuple-element.24), channel_id=1, source_target_pairs={{0,4},{4,0},{8,12},{12,8},{1,5},{5,1},{9,13},{13,9},{2,6},{6,2},{1... | collective-permute-start | bytes 1327112 | tf_op jit(solution)/shard_map/ppermute | solution.py:288
  15.6 29.5 %copy-start.6 = (bf16[576,384]{1,0:T(8,128)(2,1)}, bf16[576,384]{1,0:T(8,128)(2,1)S(1)}, u32[]{:S(2)}) copy-start(bf16[576,384]{1,0:T(8,128)(2,1)S(1)} %collective-permute-done.3.refs_4_) | copy-start | bytes 1327108
  15.6 11.3 %collective-permute-start.4 = (bf16[576,384]{1,0:T(8,128)(2,1)S(1)}, bf16[576,384]{1,0:T(8,128)(2,1)S(1)}, u32[]{:S(2)}, u32[]{:S(2)}) collective-permute-start(bf16[576,384]{1,0:T(8,128)(2,1)S(1)} %collective-permute-done.3.refs_4_), channel_id=1, source_target_pairs={{0,2},{1,3},{2,0},{3,1},{4,6},{5,7},{6,4},{7,5},{8,10},{9,11},{10,... | collective-permute-start | bytes 1327112 | tf_op jit(solution)/shard_map/ppermute | solution.py:268
  17.2 27.8 %collective-permute-start.5 = (bf16[576,384]{1,0:T(8,128)(2,1)S(1)}, bf16[576,384]{1,0:T(8,128)(2,1)S(1)}, u32[]{:S(2)}, u32[]{:S(2)}) collective-permute-start(bf16[576,384]{1,0:T(8,128)(2,1)S(1)} %collective-permute-done.3.refs_4_), channel_id=1, source_target_pairs={{0,1},{1,0},{2,3},{3,2},{4,5},{5,4},{6,7},{7,6},{8,9},{9,8},{10,11... | collective-permute-start | bytes 1327112 | tf_op jit(solution)/shard_map/ppermute | solution.py:268
  26.9 18.2 %copy-start.7 = (bf16[576,384]{1,0:T(8,128)(2,1)}, bf16[576,384]{1,0:T(8,128)(2,1)S(1)}, u32[]{:S(2)}) copy-start(bf16[576,384]{1,0:T(8,128)(2,1)S(1)} %collective-permute-done.4.refs_5_) | copy-start | bytes 1327108
  26.9 18.2 %collective-permute-start.6 = (bf16[576,384]{1,0:T(8,128)(2,1)S(1)}, bf16[576,384]{1,0:T(8,128)(2,1)S(1)}, u32[]{:S(2)}, u32[]{:S(2)}) collective-permute-start(bf16[576,384]{1,0:T(8,128)(2,1)S(1)} %collective-permute-done.4.refs_5_), channel_id=1, source_target_pairs={{0,1},{1,0},{2,3},{3,2},{4,5},{5,4},{6,7},{7,6},{8,9},{9,8},{10,11... | collective-permute-start | bytes 1327112 | tf_op jit(solution)/shard_map/ppermute | solution.py:268
  26.9 7.0 %collective-permute-start.10 = (bf16[32,1536]{1,0:T(8,128)(2,1)}, bf16[32,1536]{1,0:T(8,128)(2,1)S(1)}, u32[]{:S(2)}, u32[]{:S(2)}) collective-permute-start(bf16[32,1536]{1,0:T(8,128)(2,1)} %get-tuple-element.30), channel_id=1, source_target_pairs={{0,12},{4,0},{8,4},{12,8},{1,13},{5,1},{9,5},{13,9},{2,14},{6,2},{... | collective-permute-start | bytes 294920 | tf_op jit(solution)/shard_map/ppermute | solution.py:265
  30.4 10.3 %collective-permute-start.11 = (bf16[32,1536]{1,0:T(8,128)(2,1)}, bf16[32,1536]{1,0:T(8,128)(2,1)S(1)}, u32[]{:S(2)}, u32[]{:S(2)}) collective-permute-start(bf16[32,1536]{1,0:T(8,128)(2,1)} %get-tuple-element.29.refs_0_), channel_id=1, source_target_pairs={{0,8},{4,12},{8,0},{12,4},{1,9},{5,13},{9,1},{13,5},{2,10},{6,14},... | collective-permute-start | bytes 294920 | tf_op jit(solution)/shard_map/ppermute | solution.py:265
  30.4 10.3 %collective-permute-start.12 = (bf16[32,1536]{1,0:T(8,128)(2,1)}, bf16[32,1536]{1,0:T(8,128)(2,1)S(1)}, u32[]{:S(2)}, u32[]{:S(2)}) collective-permute-start(bf16[32,1536]{1,0:T(8,128)(2,1)} %get-tuple-element.30), channel_id=1, source_target_pairs={{0,4},{4,8},{8,12},{12,0},{1,5},{5,9},{9,13},{13,1},{2,6},{6,10},{... | collective-permute-start | bytes 294920 | tf_op jit(solution)/shard_map/ppermute | solution.py:265
  33.9 11.2 %copy-start.13 = (bf16[32,1536]{1,0:T(8,128)(2,1)}, bf16[32,1536]{1,0:T(8,128)(2,1)S(1)}, u32[]{:S(2)}) copy-start(bf16[32,1536]{1,0:T(8,128)(2,1)S(1)} %collective-permute-done.10.refs_1_) | copy-start | bytes 294916
  33.9 27.1 %collective-permute-start = (bf16[32,1536]{1,0:T(8,128)(2,1)}, bf16[32,1536]{1,0:T(8,128)(2,1)S(1)}, u32[]{:S(2)}, u32[]{:S(2)}) collective-permute-start(bf16[32,1536]{1,0:T(8,128)(2,1)} %get-tuple-element.23), channel_id=1, source_target_pairs={{0,12},{4,0},{8,4},{12,8},{1,13},{5,1},{9,5},{13,9},{2,14},{6,2},{... | collective-permute-start | bytes 294920 | tf_op jit(solution)/shard_map/ppermute | solution.py:265
  40.7 4.4 %copy-start.14 = (bf16[32,1536]{1,0:T(8,128)(2,1)}, bf16[32,1536]{1,0:T(8,128)(2,1)S(1)}, u32[]{:S(2)}) copy-start(bf16[32,1536]{1,0:T(8,128)(2,1)S(1)} %collective-permute-done.11.refs_2_) | copy-start | bytes 294916
  40.7 21.9 %collective-permute-start.2 = (bf16[32,1536]{1,0:T(8,128)(2,1)}, bf16[32,1536]{1,0:T(8,128)(2,1)S(1)}, u32[]{:S(2)}, u32[]{:S(2)}) collective-permute-start(bf16[32,1536]{1,0:T(8,128)(2,1)} %get-tuple-element.23), channel_id=1, source_target_pairs={{0,4},{4,8},{8,12},{12,0},{1,5},{5,9},{9,13},{13,1},{2,6},{6,10},{... | collective-permute-start | bytes 294920 | tf_op jit(solution)/shard_map/ppermute | solution.py:265
  40.7 4.4 %copy-start.15 = (bf16[32,1536]{1,0:T(8,128)(2,1)}, bf16[32,1536]{1,0:T(8,128)(2,1)S(1)}, u32[]{:S(2)}) copy-start(bf16[32,1536]{1,0:T(8,128)(2,1)S(1)} %collective-permute-done.12.refs_3_) | copy-start | bytes 294916
  40.7 21.9 %collective-permute-start.1 = (bf16[32,1536]{1,0:T(8,128)(2,1)}, bf16[32,1536]{1,0:T(8,128)(2,1)S(1)}, u32[]{:S(2)}, u32[]{:S(2)}) collective-permute-start(bf16[32,1536]{1,0:T(8,128)(2,1)} %get-tuple-element.22.refs_0_), channel_id=1, source_target_pairs={{0,8},{4,12},{8,0},{12,4},{1,9},{5,13},{9,1},{13,5},{2,10},{6,14},... | collective-permute-start | bytes 294920 | tf_op jit(solution)/shard_map/ppermute | solution.py:265
  56.6 24.2 %collective-permute-start.13 = (bf16[32,1152]{1,0:T(8,128)(2,1)}, bf16[32,1152]{1,0:T(8,128)(2,1)S(1)}, u32[]{:S(2)}, u32[]{:S(2)}) collective-permute-start(bf16[32,1152]{1,0:T(8,128)(2,1)} %get-tuple-element.32), channel_id=1, source_target_pairs={{0,12},{4,0},{8,4},{12,8},{1,13},{5,1},{9,5},{13,9},{2,14},{6,2},{... | collective-permute-start | bytes 221192 | tf_op jit(solution)/shard_map/ppermute | solution.py:265
  61.1 20.8 %collective-permute-start.14 = (bf16[32,1152]{1,0:T(8,128)(2,1)}, bf16[32,1152]{1,0:T(8,128)(2,1)S(1)}, u32[]{:S(2)}, u32[]{:S(2)}) collective-permute-start(bf16[32,1152]{1,0:T(8,128)(2,1)} %get-tuple-element.33), channel_id=1, source_target_pairs={{0,8},{4,12},{8,0},{12,4},{1,9},{5,13},{9,1},{13,5},{2,10},{6,14},... | collective-permute-start | bytes 221192 | tf_op jit(solution)/shard_map/ppermute | solution.py:265
  61.1 20.8 %collective-permute-start.15 = (bf16[32,1152]{1,0:T(8,128)(2,1)}, bf16[32,1152]{1,0:T(8,128)(2,1)S(1)}, u32[]{:S(2)}, u32[]{:S(2)}) collective-permute-start(bf16[32,1152]{1,0:T(8,128)(2,1)} %get-tuple-element.34), channel_id=1, source_target_pairs={{0,4},{4,8},{8,12},{12,0},{1,5},{5,9},{9,13},{13,1},{2,6},{6,10},{... | collective-permute-start | bytes 221192 | tf_op jit(solution)/shard_map/ppermute | solution.py:265
  74.5 8.6 %collective-permute-start.7 = (bf16[32,1152]{1,0:T(8,128)(2,1)}, bf16[32,1152]{1,0:T(8,128)(2,1)S(1)}, u32[]{:S(2)}, u32[]{:S(2)}) collective-permute-start(bf16[32,1152]{1,0:T(8,128)(2,1)} %get-tuple-element.26), channel_id=1, source_target_pairs={{0,12},{4,0},{8,4},{12,8},{1,13},{5,1},{9,5},{13,9},{2,14},{6,2},{... | collective-permute-start | bytes 221192 | tf_op jit(solution)/shard_map/ppermute | solution.py:265
  80.8 5.5 %collective-permute-start.8 = (bf16[32,1152]{1,0:T(8,128)(2,1)}, bf16[32,1152]{1,0:T(8,128)(2,1)S(1)}, u32[]{:S(2)}, u32[]{:S(2)}) collective-permute-start(bf16[32,1152]{1,0:T(8,128)(2,1)} %get-tuple-element.27), channel_id=1, source_target_pairs={{0,8},{4,12},{8,0},{12,4},{1,9},{5,13},{9,1},{13,5},{2,10},{6,14},... | collective-permute-start | bytes 221192 | tf_op jit(solution)/shard_map/ppermute | solution.py:265
  80.8 6.4 %copy-start = (bf16[32,1152]{1,0:T(8,128)(2,1)}, bf16[32,1152]{1,0:T(8,128)(2,1)S(1)}, u32[]{:S(2)}) copy-start(bf16[32,1152]{1,0:T(8,128)(2,1)S(1)} %collective-permute-done.13.refs_5_) | copy-start | bytes 221188
  80.8 6.4 %collective-permute-start.9 = (bf16[32,1152]{1,0:T(8,128)(2,1)}, bf16[32,1152]{1,0:T(8,128)(2,1)S(1)}, u32[]{:S(2)}, u32[]{:S(2)}) collective-permute-start(bf16[32,1152]{1,0:T(8,128)(2,1)} %get-tuple-element.28), channel_id=1, source_target_pairs={{0,4},{4,8},{8,12},{12,0},{1,5},{5,9},{9,13},{13,1},{2,6},{6,10},{... | collective-permute-start | bytes 221192 | tf_op jit(solution)/shard_map/ppermute | solution.py:265
  81.9 5.3 %copy-start.1 = (bf16[32,1152]{1,0:T(8,128)(2,1)}, bf16[32,1152]{1,0:T(8,128)(2,1)S(1)}, u32[]{:S(2)}) copy-start(bf16[32,1152]{1,0:T(8,128)(2,1)S(1)} %collective-permute-done.14.refs_6_) | copy-start | bytes 221188
  81.9 5.3 %copy-start.2 = (bf16[32,1152]{1,0:T(8,128)(2,1)}, bf16[32,1152]{1,0:T(8,128)(2,1)S(1)}, u32[]{:S(2)}) copy-start(bf16[32,1152]{1,0:T(8,128)(2,1)S(1)} %collective-permute-done.15.refs_7_) | copy-start | bytes 221188
  (8 other events, 10.3 us)

commit v4 on v3

v4 whole, which is shorter than its diff:
```python
import functools

import jax
import jax.numpy as jnp
from jax import lax
from jax.experimental import pallas as pl
from jax.experimental.pallas import tpu as pltpu
from jax.sharding import PartitionSpec as P


PAGE = 64
GROUP = 2
LANES = 4
BLOCK_PAGES = 8
HEADS_STEP = 4
PIECES = 2
CHUNKS = 2


FLOOR = -1e30
FAR = 2**30
LOG2E = 1.4426950408889634


def pack_kernel(dims, nope_ref, rope_ref, cache_ref, *refs):
    nope_width, rope_width, quarter_cols, chunks = dims
    outs, sems = refs[:-1], refs[-1]
    mine = lax.axis_index("pages") % GROUP
    lane = lax.axis_index("heads") % LANES
    depth = cache_ref.shape[0] // PIECES
    copies = []
    for p in range(PIECES):
        copies.append(
            pltpu.make_async_copy(
                cache_ref.at[pl.ds(p * depth, depth), pl.ds(pl.multiple_of(lane * quarter_cols, 128), quarter_cols)],
                outs[p],
                sems.at[p],
            )
        )
    for c in range(chunks):
        for e in range(GROUP):
            which = ((mine + e) % GROUP) * chunks + c
            for ref, width, at in ((nope_ref, nope_width, 0), (rope_ref, rope_width, nope_width)):
                copies.append(
                    pltpu.make_async_copy(
                        ref.at[:, pl.ds(pl.multiple_of(which * width, 128), width)],
                        outs[PIECES + c * GROUP + e].at[:, pl.ds(at, width)],
                        sems.at[len(copies)],
                    )
                )
    for c in copies:
        c.start()
    for c in copies:
        c.wait()


def absorb_kernel(dims, tok_ref, off_ref, *refs):
    members, first, hc, hh, nope, rope, latent = dims
    q_refs, keys_hbm, qs_ref, limit_ref, wk, sem = refs[:members], *refs[members:]
    rows = limit_ref.shape[0]
    local_rows = rows // members
    member = lax.axis_index("pages")
    mine = member % GROUP
    copy = pltpu.make_async_copy(keys_hbm.at[pl.ds(mine * hh + first, hc)], wk, sem)
    copy.start()
    token = pltpu.roll(
        jnp.broadcast_to(tok_ref[...], (8, rows)), lax.rem(rows - member * local_rows, rows), axis=1
    )[:1]
    across = lax.broadcasted_iota(jnp.int32, (rows, rows), 1)
    down = lax.broadcasted_iota(jnp.int32, (rows, rows), 0)
    wanted = lax.rem(member - down // local_rows + members, members) * local_rows + lax.rem(down, local_rows)
    order = (jnp.broadcast_to(token, (rows, rows)) == wanted).astype(jnp.bfloat16)
    limit = jnp.max(jnp.where(across == wanted, off_ref[...], 0), axis=1, keepdims=True)
    limit_ref[...] = jnp.broadcast_to(limit, limit_ref.shape)
    copy.wait()
    for h in range(hc):
        query = jnp.concatenate([q[:, h * nope:(h + 1) * nope] for q in q_refs], axis=0)
        query = jnp.dot(order, query, preferred_element_type=jnp.float32).astype(jnp.bfloat16)
        lat = jnp.dot(query, wk[h], preferred_element_type=jnp.float32)
        qs_ref[h * rows:(h + 1) * rows, :latent] = lat.astype(jnp.bfloat16)
    for h in range(0, hc, 2):
        at = hc * nope + h * rope
        both = jnp.concatenate([q[:, at:at + 2 * rope] for q in q_refs], axis=0)
        both = jnp.dot(order, both, preferred_element_type=jnp.float32).astype(jnp.bfloat16)
        for i in range(2):
            qs_ref[(h + i) * rows:(h + i + 1) * rows, latent:] = both[:, i * rope:(i + 1) * rope]


def attend_kernel(dims, counts_ref, limit_ref, qs_hbm, *refs):
    members, first, hc, hh, hb, nope, rope, latent, vhead, rows, slots = dims
    part_refs, refs = refs[:LANES * PIECES], refs[LANES * PIECES:]
    own_ref, values_hbm = refs[:2]
    out_refs, refs = refs[2:2 + members], refs[2 + members:]
    tiles, wv, bias, qs, sbuf, mx, den, acc, lse, sems, own_sems, part_sems = refs
    local_rows = rows // members
    block = BLOCK_PAGES * PAGE
    cols = slots * PAGE
    quarter_cols = cols // LANES
    depth = (latent + rope) // PIECES
    scale2 = (nope + rope) ** (-0.5) * LOG2E
    steps = hc // hb
    group_rows = hb * rows
    member = lax.axis_index("pages")
    lane_id = lax.axis_index("heads") % LANES
    partner = member ^ 1
    mine = member % GROUP
    own_live, part_live = counts_ref[member], counts_ref[partner]
    own_blocks = (own_live + BLOCK_PAGES - 1) // BLOCK_PAGES
    part_blocks = (part_live + BLOCK_PAGES - 1) // BLOCK_PAGES
    blocks = own_blocks + part_blocks

    query_copies = [
        pltpu.make_async_copy(
            qs_hbm.at[pl.ds(g * group_rows, group_rows)], qs.at[pl.ds(g * group_rows, group_rows)], sems.at[g]
        )
        for g in range(steps)
    ]
    value_copy = pltpu.make_async_copy(values_hbm.at[pl.ds(mine * hh + first, hc)], wv, sems.at[steps])
    tile_copies = []
    for b in range(-(-cols // block)):
        at = pl.ds(b * block, min(block, cols - b * block))
        tile_copies.append((b < own_blocks, pltpu.make_async_copy(own_ref.at[:, at], tiles.at[:, at], own_sems.at[b])))
    for i, flip in enumerate((0, 2, 1, 3)):
        quarter = lane_id ^ flip
        at = pl.multiple_of(cols + quarter * quarter_cols, 128)
        for p in range(PIECES):
            tile_copies.append((
                quarter * quarter_cols < part_blocks * block,
                pltpu.make_async_copy(
                    part_refs[i * PIECES + p],
                    tiles.at[pl.ds(p * depth, depth), pl.ds(at, quarter_cols)],
                    part_sems.at[i * PIECES + p],
                ),
            ))
    query_copies[0].start()
    for used, copy in tile_copies:
        pl.when(used)(copy.start)
    for copy in query_copies[1:] + [value_copy]:
        copy.start()

    before = lambda who: lax.fori_loop(0, who, lambda i, total: total + counts_ref[i], jnp.int32(0))
    limit = limit_ref[:, :1]
    own_base, part_base = before(member) * PAGE, before(partner) * PAGE

    def column(b):
        return pl.multiple_of(jnp.where(b < own_blocks, b * block, cols + (b - own_blocks) * block), 128)

    spot = lax.broadcasted_iota(jnp.int32, (1, block), 1)

    def fill_bias(b, carry):
        own = b < own_blocks
        inside = jnp.where(own, b, b - own_blocks) * block + spot
        live = jnp.where(own, own_live, part_live) * PAGE
        positions = jnp.where(inside < live, jnp.where(own, own_base, part_base) + inside, FAR)
        bias[:, pl.ds(pl.multiple_of(b * block, 128), block)] = jnp.where(positions < limit, 0.0, FLOOR)
        return carry

    lax.fori_loop(0, blocks, fill_bias, 0)
    lse[...] = jnp.zeros_like(lse)

    def score(g, b):
        slot = g % 2
        scores = jnp.dot(qs[g * group_rows:(g + 1) * group_rows], tiles[:, pl.ds(column(b), block)], preferred_element_type=jnp.float32)
        at = pl.multiple_of(b * block, 128)
        shut = bias[:, pl.ds(at, block)]
        for e in range(hb):
            part = slice(e * rows, (e + 1) * rows)
            value = scores[part] + shut
            sbuf[slot, part, pl.ds(at, block)] = value
            top = functools.reduce(jnp.maximum, [value[:, i:i + 128] for i in range(0, block, 128)])
            mx[slot, part] = jnp.maximum(mx[slot, part], top)

    def gather(g, b, top):
        slot = g % 2
        at = pl.multiple_of(b * block, 128)
        weights = jnp.exp2((sbuf[slot, :, pl.ds(at, block)] - top) * scale2)
        den[...] += functools.reduce(jnp.add, [weights[:, i:i + 128] for i in range(0, block, 128)])
        acc[...] += lax.dot_general(
            weights.astype(jnp.bfloat16),
            tiles[:latent, pl.ds(column(b), block)],
            (((1,), (1,)), ((), ())),
            preferred_element_type=jnp.float32,
        )

    lane = lax.broadcasted_iota(jnp.int32, (rows, 128), 1)

    def finish(g, top):
        total = jnp.sum(den[...], axis=1, keepdims=True)
        seen = top > 0.5 * FLOOR
        total = jnp.where(seen, total, 1.0)
        share = jnp.where(seen, 1.0 / total, 0.0)
        logs = jnp.where(seen, top * scale2 + jnp.log2(total), FLOOR)
        for e in range(hb):
            h = g * hb + e
            part = slice(e * rows, (e + 1) * rows)
            value = jnp.dot(acc[part].astype(jnp.bfloat16), wv[h], preferred_element_type=jnp.float32)
            value = (value * share[part]).astype(jnp.bfloat16)
            for s in range(members):
                out_refs[s][:, h * vhead:(h + 1) * vhead] = value[s * local_rows:(s + 1) * local_rows]
            full = logs[part]
            high = full.astype(jnp.bfloat16).astype(jnp.float32)
            middle = (full - high).astype(jnp.bfloat16).astype(jnp.float32)
            low = full - high - middle
            lse[...] = jnp.where(lane == h, high, jnp.where(lane == hc + h, middle,
                                 jnp.where(lane == 2 * hc + h, low, lse[...])))

    top = None
    for g in range(steps + 1):
        if g < steps:
            query_copies[g].wait()
            mx[g % 2] = jnp.full(mx.shape[1:], FLOOR, jnp.float32)
        if g == 0:
            for used, copy in tile_copies:
                pl.when(used)(copy.wait)
        if g == 1:
            value_copy.wait()
        if g > 0:
            den[...] = jnp.zeros_like(den)
            acc[...] = jnp.zeros_like(acc)

        def body(b, carry, g=g, top=top):
            if g < steps:
                score(g, b)
            if g > 0:
                gather(g - 1, b, top)
            return carry

        lax.fori_loop(0, blocks, body, 0)
        if g > 0:
            finish(g - 1, top)
        if g < steps:
            top = jnp.max(mx[g % 2], axis=1, keepdims=True)

    for s in range(members):
        out_refs[s][:, hc * vhead:] = lse[s * local_rows:(s + 1) * local_rows].astype(jnp.bfloat16)


def attend_call(members, first, hc, hh, hb, nope, rope, latent, vhead, rows, slots, chunks):
    hbm = pl.BlockSpec(memory_space=pltpu.HBM)
    vmem = pl.BlockSpec(memory_space=pltpu.VMEM)
    bf16 = jnp.bfloat16
    full = latent + rope
    cols = slots * PAGE
    local_rows = rows // members
    packed = hc * vhead + 128
    block = BLOCK_PAGES * PAGE
    most = 2 * (-(-cols // block))
    return pl.pallas_call(
        functools.partial(
            attend_kernel, (members, first, hc, hh, hb, nope, rope, latent, vhead, rows, slots)
        ),
        out_shape=[jax.ShapeDtypeStruct((local_rows, packed), bf16)] * members,
        in_specs=[pl.BlockSpec(memory_space=pltpu.SMEM), vmem] + [hbm] * (1 + LANES * PIECES + 2),
        out_specs=[vmem] * members,
        scratch_shapes=[
            pltpu.VMEM((full, 2 * cols), bf16),
            pltpu.VMEM((hc, latent, vhead), bf16),
            pltpu.VMEM((rows, most * block), jnp.float32),
            pltpu.VMEM((hc * rows, full), bf16),
            pltpu.VMEM((2, hb * rows, most * block), jnp.float32),
            pltpu.VMEM((2, hb * rows, 128), jnp.float32),
            pltpu.VMEM((hb * rows, 128), jnp.float32),
            pltpu.VMEM((hb * rows, latent), jnp.float32),
            pltpu.VMEM((rows, 128), jnp.float32),
            pltpu.SemaphoreType.DMA((1 + hc // hb,)),
            pltpu.SemaphoreType.DMA((most // 2,)),
            pltpu.SemaphoreType.DMA((LANES * PIECES,)),
        ],
        compiler_params=pltpu.CompilerParams(vmem_limit_bytes=56 << 20),
        cost_estimate=pl.CostEstimate(flops=8 * 10**9 // chunks, bytes_accessed=8 * 10**6, transcendentals=0),
    )


def merge_kernel(dims, *refs):
    hc, vhead, members, chunks = dims
    out_ref = refs[-1]
    mine = lax.axis_index("pages") % GROUP
    for c in range(chunks):
        for parity in range(GROUP):
            parts = [refs[c * members + s] for s in range(members) if s % GROUP == parity]
            logs = []
            for b in parts:
                packed = b[:, hc * vhead:].astype(jnp.float32)
                logs.append(packed[:, :hc] + packed[:, hc:2 * hc] + packed[:, 2 * hc:3 * hc])
            top = functools.reduce(jnp.maximum, logs)
            weights = [jnp.exp2(v - top) for v in logs]
            total = functools.reduce(jnp.add, weights)
            weights = [w / total for w in weights]
            base = (lax.rem(mine + parity, GROUP) * chunks + c) * (hc * vhead)
            for h in range(hc):
                cols = slice(h * vhead, (h + 1) * vhead)
                value = functools.reduce(
                    jnp.add, [w[:, h:h + 1] * b[:, cols].astype(jnp.float32) for w, b in zip(weights, parts)]
                )
                out_ref[:, pl.ds(pl.multiple_of(base + h * vhead, 128), vhead)] = value.astype(jnp.bfloat16)


def on_device(
    q_nope, q_rope, cache_tiles, absorb_keys, absorb_values, page_counts, query_token, query_offsets, members, devices
):
    heads_here, nope, latent = absorb_keys.shape
    vhead = absorb_values.shape[2]
    local_rows = q_nope.shape[0]
    rope = q_rope.shape[1] // heads_here
    full = cache_tiles.shape[1]
    slots = cache_tiles.shape[0] // PAGE
    cols = slots * PAGE
    rows = local_rows * members
    hh = heads_here // GROUP
    chunks = min(CHUNKS, hh // 2)
    hc = hh // chunks
    hb = min(HEADS_STEP, hc)
    hbm = pl.BlockSpec(memory_space=pltpu.HBM)
    vmem = pl.BlockSpec(memory_space=pltpu.VMEM)
    bf16 = jnp.bfloat16

    def over_pages(x, s):
        return lax.ppermute(x, "pages", [(i, (i - s) % members) for i in range(members)])

    def over_heads(x, bit):
        return lax.ppermute(x, "heads", [(i, i ^ bit) for i in range(devices)])

    turned = cache_tiles.T
    packed = pl.pallas_call(
        functools.partial(pack_kernel, (hc * nope, hc * rope, cols // LANES, chunks)),
        out_shape=[jax.ShapeDtypeStruct((full // PIECES, cols // LANES), bf16)] * PIECES
        + [jax.ShapeDtypeStruct((local_rows, hc * (nope + rope)), bf16)] * (GROUP * chunks),
        in_specs=[hbm] * 3,
        out_specs=[vmem] * (PIECES + GROUP * chunks),
        scratch_shapes=[pltpu.SemaphoreType.DMA((PIECES + 2 * GROUP * chunks,))],
        name="pack",
    )(q_nope, q_rope, turned)
    pieces, shares = packed[:PIECES], packed[PIECES:]

    parts = [[None] * PIECES for _ in range(LANES)]
    for p in range(PIECES):
        parts[0][p] = lax.ppermute(pieces[p], "pages", [(i, i ^ 1) for i in range(members)])
        parts[1][p] = over_heads(parts[0][p], 2)
        parts[2][p] = over_heads(parts[0][p], 1)
        parts[3][p] = over_heads(parts[1][p], 1)
    parts = [p for part in parts for p in part]
    absorbed = []
    for c in range(chunks):
        own, other = shares[c * GROUP:(c + 1) * GROUP]
        blocks = [own]
        for s in range(1, members):
            blocks.append(over_pages((own, other)[s % GROUP], s))
        absorbed.append(pl.pallas_call(
            functools.partial(absorb_kernel, (members, c * hc, hc, hh, nope, rope, latent)),
            out_shape=[
                jax.ShapeDtypeStruct((hc * rows, full), bf16),
                jax.ShapeDtypeStruct((rows, 128), jnp.int32),
            ],
            in_specs=[vmem] * (2 + members) + [hbm],
            out_specs=[vmem] * 2,
            scratch_shapes=[pltpu.VMEM((hc, nope, latent), bf16), pltpu.SemaphoreType.DMA(())],
        )(query_token[None, :], query_offsets[None, :], *blocks, absorb_keys))

    arrived = []
    for c in range(chunks):
        outs = attend_call(
            members, c * hc, hc, hh, hb, nope, rope, latent, vhead, rows, slots, chunks
        )(page_counts, absorbed[c][1], absorbed[c][0], *parts, turned, absorb_values)
        arrived.append(outs[0])
        for s in range(1, members):
            arrived.append(over_pages(outs[s], s))

    return pl.pallas_call(
        functools.partial(merge_kernel, (hc, vhead, members, chunks)),
        out_shape=jax.ShapeDtypeStruct((local_rows, heads_here * vhead), bf16),
        in_specs=[vmem] * (members * chunks),
        out_specs=vmem,
        name="merge",
    )(*arrived)


def solution(mesh):
    in_specs = (
        P(("groups", "pages"), "heads"),
        P(("groups", "pages"), "heads"),
        P(("groups", "pages"), None),
        P("heads", None, None),
        P("heads", None, None),
        P("groups"),
        P("groups"),
        P("groups"),
    )
    body = functools.partial(on_device, members=mesh.shape["pages"], devices=mesh.shape["heads"])
    return jax.shard_map(
        body, mesh=mesh, in_specs=in_specs, out_specs=P(("groups", "pages"), "heads"), check_vma=False
    )
```

time: 90.8 us -> 92.9 us (1.023)
  waiting for transfers between devices: 28.8 us -> 25 us
  Pallas kernels: 27.5 us -> 31 us
  starting transfers between devices: 31.3 us -> 34.1 us
    ppermute x3 -> x6, waiting for transfers between devices: 9.68 us -> 0.02 us  [over_heads(): return lax.ppermute(x, 'heads', [(i, i ^ bit) for i in range(devices)])]
    ppermute x12, waiting for transfers between devices: 8.72 us -> 16.6 us  [over_pages(): lax.ppermute(x, 'pages', [(i, (i - s) % members) for i in range(members)])]
    pallas_call x3 -> x4, Pallas kernels: 22.8 us -> 26.2 us  [the longest x2 16.2 us: on_device(): attend_call(members, c * hc, hc, hh, hb, nope, rope, latent, vhead, rows,...]
    ppermute x3 -> x6, starting transfers between devices: 1.66 us -> 4.6 us  [over_heads(): return lax.ppermute(x, 'heads', [(i, i ^ bit) for i in range(devices)])]
    ppermute x1 -> x2, waiting for transfers between devices: 10.4 us -> 8.36 us  [on_device(): lax.ppermute(pieces[p], 'pages', [(i, i ^ 1) for i in range(members)])]
    unnamed x32 -> x40, local copies, waits for them, and re-layouts: 2.76 us -> 2.11 us
    ppermute x1 -> x2, starting transfers between devices: 3.12 us -> 3.2 us  [on_device(): lax.ppermute(pieces[p], 'pages', [(i, i ^ 1) for i in range(members)])]
  transfers between devices with their start and end apart: 16 -> 20, of which waited for: 7 -> 9; matrix products, arithmetic and copies ran while one was open for 0% -> 0% of each run, Pallas kernels for 25% -> 20%
where the time goes in v4:
time: 92.9 us; the launch traced here: 92.4 us
  starting transfers between devices  34.1 us (37%)
  Pallas kernels  31 us (33%)
  waiting for transfers between devices  25 us (27%)
  local copies, waits for them, and re-layouts  2.11 us (2%)
    ppermute x12, starting transfers between devices, over_pages(): lax.ppermute(x, 'pages', [(i, (i - s) % members) for i in range(members)])  26.3 us
    ppermute x12, waiting for transfers between devices, over_pages(): lax.ppermute(x, 'pages', [(i, (i - s) % members) for i in range(members)])  16.6 us
    pallas_call x2, Pallas kernels, on_device(): attend_call(members, c * hc, hc, hh, hb, nope, rope, latent, vhead, rows,...  16.2 us
    pallas_call x2, Pallas kernels, on_device(): pl.pallas_call(functools.partial(absorb_kernel, (members, c * hc, hc, hh,...  10 us
    ppermute x2, waiting for transfers between devices, on_device(): lax.ppermute(pieces[p], 'pages', [(i, i ^ 1) for i in range(members)])  8.36 us
    ppermute x6, starting transfers between devices, over_heads(): return lax.ppermute(x, 'heads', [(i, i ^ bit) for i in range(devices)])  4.6 us
    ppermute x2, starting transfers between devices, on_device(): lax.ppermute(pieces[p], 'pages', [(i, i ^ 1) for i in range(members)])  3.2 us
    pallas_call x1, Pallas kernels, on_device(): pl.pallas_call(functools.partial(merge_kernel, (hc, vhead, members, chunk...  2.62 us
  transfers between devices with their start and end apart: 20, of which 9 were waited for; matrix products, arithmetic and copies ran while one was open for 0% of the time, Pallas kernels for 20%

profile of v4, /device:TPU:0, one launch (start us, length us, event | category | flops | bytes accessed | tf_op | source)
XLA Modules:
  0.0 92.4 jit_solution(14975785324801866262)
XLA Ops:
  0.0 2.2 %pack.1 = (bf16[288,384]{1,0:T(8,128)(2,1)}, bf16[288,384]{1,0:T(8,128)(2,1)}, bf16[32,1536]{1,0:T(8,128)(2,1)}, bf16[32,1536]{1,0:T(8,128)(2,1)}, bf16[32,1536]{1,0:T(8,128)(2,1)}, /*index=5*/bf16[32,1536]{1,0:T(8,128)(2,1)}) custom-call(bf16[32,4096]{1,0:T(8,128)(2,1)} %nope_ref.1, bf16[32,2048]{1,0:T(8,128)(2,1)} %rope_ref.1, bf16[576,1536]{1,0:T(8,128)(2,1)} %bitcast.3), custom_call_target="tpu_custom_call" | custom-call | tf_op jit(solution)/shard_map/pack/pallas_call | solution.py:324
  2.2 3.1 %collective-permute-start.4 = (bf16[288,384]{1,0:T(8,128)(2,1)}, bf16[288,384]{1,0:T(8,128)(2,1)S(1)}, u32[]{:S(2)}, u32[]{:S(2)}) collective-permute-start(bf16[288,384]{1,0:T(8,128)(2,1)} %get-tuple-element.28), channel_id=1, source_target_pairs={{0,4},{4,0},{8,12},{12,8},{1,5},{5,1},{9,13},{13,9},{2,6},{6,2},{1... | collective-permute-start | bytes 663560 | tf_op jit(solution)/shard_map/ppermute | solution.py:337
  5.4 6.4 %collective-permute-done.4.refs_1_ = bf16[288,384]{1,0:T(8,128)(2,1)S(1)} collective-permute-done((bf16[288,384]{1,0:T(8,128)(2,1)}, bf16[288,384]{1,0:T(8,128)(2,1)S(1)}, u32[]{:S(2)}, u32[]{:S(2)}) %collective-permute-start.4) | collective-permute-done | bytes 221216 | tf_op jit(solution)/shard_map/ppermute | solution.py:337
  11.8 1.9 %collective-permute-start.6 = (bf16[288,384]{1,0:T(8,128)(2,1)S(1)}, bf16[288,384]{1,0:T(8,128)(2,1)S(1)}, u32[]{:S(2)}, u32[]{:S(2)}) collective-permute-start(bf16[288,384]{1,0:T(8,128)(2,1)S(1)} %collective-permute-done.4.refs_1_), channel_id=1, source_target_pairs={{0,2},{1,3},{2,0},{3,1},{4,6},{5,7},{6,4},{7,5},{8,10},{9,11},{10,... | collective-permute-start | bytes 663560 | tf_op jit(solution)/shard_map/ppermute | solution.py:321
  13.7 2.0 %collective-permute-done.3.refs_0_ = bf16[288,384]{1,0:T(8,128)(2,1)S(1)} collective-permute-done((bf16[288,384]{1,0:T(8,128)(2,1)}, bf16[288,384]{1,0:T(8,128)(2,1)S(1)}, u32[]{:S(2)}, u32[]{:S(2)}) %collective-permute-start.3) | collective-permute-done | bytes 221216 | tf_op jit(solution)/shard_map/ppermute | solution.py:337
  15.7 1.7 %collective-permute-start.5 = (bf16[288,384]{1,0:T(8,128)(2,1)S(1)}, bf16[288,384]{1,0:T(8,128)(2,1)S(1)}, u32[]{:S(2)}, u32[]{:S(2)}) collective-permute-start(bf16[288,384]{1,0:T(8,128)(2,1)S(1)} %collective-permute-done.3.refs_0_), channel_id=1, source_target_pairs={{0,2},{1,3},{2,0},{3,1},{4,6},{5,7},{6,4},{7,5},{8,10},{9,11},{10,... | collective-permute-start | bytes 663560 | tf_op jit(solution)/shard_map/ppermute | solution.py:321
  17.3 3.6 %collective-permute-start.14 = (bf16[32,1536]{1,0:T(8,128)(2,1)}, bf16[32,1536]{1,0:T(8,128)(2,1)S(1)}, u32[]{:S(2)}, u32[]{:S(2)}) collective-permute-start(bf16[32,1536]{1,0:T(8,128)(2,1)} %get-tuple-element.34), channel_id=1, source_target_pairs={{0,12},{4,0},{8,4},{12,8},{1,13},{5,1},{9,5},{13,9},{2,14},{6,2},{... | collective-permute-start | bytes 294920 | tf_op jit(solution)/shard_map/ppermute | solution.py:318
  21.9 2.4 %collective-permute-done.14.refs_1_ = bf16[32,1536]{1,0:T(8,128)(2,1)S(1)} collective-permute-done((bf16[32,1536]{1,0:T(8,128)(2,1)}, bf16[32,1536]{1,0:T(8,128)(2,1)S(1)}, u32[]{:S(2)}, u32[]{:S(2)}) %collective-permute-start.14) | collective-permute-done | bytes 98336 | tf_op jit(solution)/shard_map/ppermute | solution.py:318
  24.3 4.2 %collective-permute-start = (bf16[32,1536]{1,0:T(8,128)(2,1)}, bf16[32,1536]{1,0:T(8,128)(2,1)S(1)}, u32[]{:S(2)}, u32[]{:S(2)}) collective-permute-start(bf16[32,1536]{1,0:T(8,128)(2,1)} %get-tuple-element.24), channel_id=1, source_target_pairs={{0,12},{4,0},{8,4},{12,8},{1,13},{5,1},{9,5},{13,9},{2,14},{6,2},{... | collective-permute-start | bytes 294920 | tf_op jit(solution)/shard_map/ppermute | solution.py:318
  28.5 1.8 %collective-permute-done.15.refs_2_ = bf16[32,1536]{1,0:T(8,128)(2,1)S(1)} collective-permute-done((bf16[32,1536]{1,0:T(8,128)(2,1)}, bf16[32,1536]{1,0:T(8,128)(2,1)S(1)}, u32[]{:S(2)}, u32[]{:S(2)}) %collective-permute-start.15) | collective-permute-done | bytes 98336 | tf_op jit(solution)/shard_map/ppermute | solution.py:318
  31.3 1.4 %collective-permute-start.1 = (bf16[32,1536]{1,0:T(8,128)(2,1)}, bf16[32,1536]{1,0:T(8,128)(2,1)S(1)}, u32[]{:S(2)}, u32[]{:S(2)}) collective-permute-start(bf16[32,1536]{1,0:T(8,128)(2,1)} %get-tuple-element.23.refs_0_), channel_id=1, source_target_pairs={{0,8},{4,12},{8,0},{12,4},{1,9},{5,13},{9,1},{13,5},{2,10},{6,14},... | collective-permute-start | bytes 294920 | tf_op jit(solution)/shard_map/ppermute | solution.py:318
  32.7 6.0 %collective-permute-done.1.refs_2_ = bf16[32,1536]{1,0:T(8,128)(2,1)S(1)} collective-permute-done((bf16[32,1536]{1,0:T(8,128)(2,1)}, bf16[32,1536]{1,0:T(8,128)(2,1)S(1)}, u32[]{:S(2)}, u32[]{:S(2)}) %collective-permute-start.1) | collective-permute-done | bytes 98336 | tf_op jit(solution)/shard_map/ppermute | solution.py:318
  38.9 5.0 %shard_map.84 = (bf16[1024,576]{1,0:T(8,128)(2,1)}, s32[128,128]{1,0:T(8,128)}) custom-call(s32[1,128]{1,0:T(1,128)} %bitcast.6, s32[1,128]{1,0:T(1,128)} %bitcast.8, bf16[32,1536]{1,0:T(8,128)(2,1)} %get-tuple-element.33.refs_0_, bf16[32,1536]{1,0:T(8,128)(2,1)} %copy-done, bf16[32,1536]{1,0:T(8,128)(2,1)} %copy-done.1, bf16[32,1536]{1,0:T(8,128)(2,1)} %copy-done.3, ...), custom_call_target="tpu_custom_call" | custom-call | tf_op jit(solution)/shard_map/pallas_call | solution.py:348
  43.9 1.4 %collective-permute-done.2.refs_3_ = bf16[32,1536]{1,0:T(8,128)(2,1)S(1)} collective-permute-done((bf16[32,1536]{1,0:T(8,128)(2,1)}, bf16[32,1536]{1,0:T(8,128)(2,1)S(1)}, u32[]{:S(2)}, u32[]{:S(2)}) %collective-permute-start.2) | collective-permute-done | bytes 98336 | tf_op jit(solution)/shard_map/ppermute | solution.py:318
  45.9 5.0 %shard_map.82 = (bf16[1024,576]{1,0:T(8,128)(2,1)}, s32[128,128]{1,0:T(8,128)}) custom-call(s32[1,128]{1,0:T(1,128)} %bitcast.7, s32[1,128]{1,0:T(1,128)} %bitcast.9, bf16[32,1536]{1,0:T(8,128)(2,1)} %get-tuple-element.23.refs_0_, bf16[32,1536]{1,0:T(8,128)(2,1)} %copy-done.2, bf16[32,1536]{1,0:T(8,128)(2,1)} %copy-done.4, bf16[32,1536]{1,0:T(8,128)(2,1)} %copy-done.5, ...), custom_call_target="tpu_custom_call" | custom-call | tf_op jit(solution)/shard_map/pallas_call | solution.py:348
  51.9 8.1 %shard_map.85 = (bf16[32,1152]{1,0:T(8,128)(2,1)}, bf16[32,1152]{1,0:T(8,128)(2,1)}, bf16[32,1152]{1,0:T(8,128)(2,1)}, bf16[32,1152]{1,0:T(8,128)(2,1)}) custom-call(s32[4]{0:T(128)} %counts_ref.3, s32[128,128]{1,0:T(8,128)} %get-tuple-element.35.limit_ref, bf16[1024,576]{1,0:T(8,128)(2,1)} %get-tuple-element.36.qs_hbm, bf16[288,384]{1,0:T(8,128)(2,1)} %copy-done.13, ...), custom_call_target="tpu_custom_call" | custom-call | flops 4000000000 | bytes 8000000 | tf_op jit(solution)/shard_map/pallas_call | solution.py:361
  60.0 6.6 %collective-permute-start.17 = (bf16[32,1152]{1,0:T(8,128)(2,1)}, bf16[32,1152]{1,0:T(8,128)(2,1)S(1)}, u32[]{:S(2)}, u32[]{:S(2)}) collective-permute-start(bf16[32,1152]{1,0:T(8,128)(2,1)} %get-tuple-element.38), channel_id=1, source_target_pairs={{0,12},{4,0},{8,4},{12,8},{1,13},{5,1},{9,5},{13,9},{2,14},{6,2},{... | collective-permute-start | bytes 221192 | tf_op jit(solution)/shard_map/ppermute | solution.py:318
  66.5 1.1 %collective-permute-start.19 = (bf16[32,1152]{1,0:T(8,128)(2,1)}, bf16[32,1152]{1,0:T(8,128)(2,1)S(1)}, u32[]{:S(2)}, u32[]{:S(2)}) collective-permute-start(bf16[32,1152]{1,0:T(8,128)(2,1)} %get-tuple-element.40), channel_id=1, source_target_pairs={{0,4},{4,8},{8,12},{12,0},{1,5},{5,9},{9,13},{13,1},{2,6},{6,10},{... | collective-permute-start | bytes 221192 | tf_op jit(solution)/shard_map/ppermute | solution.py:318
  67.6 8.1 %shard_map.83 = (bf16[32,1152]{1,0:T(8,128)(2,1)}, bf16[32,1152]{1,0:T(8,128)(2,1)}, bf16[32,1152]{1,0:T(8,128)(2,1)}, bf16[32,1152]{1,0:T(8,128)(2,1)}) custom-call(s32[4]{0:T(128)} %counts_ref.3, s32[128,128]{1,0:T(8,128)} %get-tuple-element.25.limit_ref, bf16[1024,576]{1,0:T(8,128)(2,1)} %get-tuple-element.26.qs_hbm, bf16[288,384]{1,0:T(8,128)(2,1)} %copy-done.13, ...), custom_call_target="tpu_custom_call" | custom-call | flops 4000000000 | bytes 8000000 | tf_op jit(solution)/shard_map/pallas_call | solution.py:361
  75.7 7.0 %collective-permute-start.11 = (bf16[32,1152]{1,0:T(8,128)(2,1)}, bf16[32,1152]{1,0:T(8,128)(2,1)S(1)}, u32[]{:S(2)}, u32[]{:S(2)}) collective-permute-start(bf16[32,1152]{1,0:T(8,128)(2,1)} %get-tuple-element.30), channel_id=1, source_target_pairs={{0,12},{4,0},{8,4},{12,8},{1,13},{5,1},{9,5},{13,9},{2,14},{6,2},{... | collective-permute-start | bytes 221192 | tf_op jit(solution)/shard_map/ppermute | solution.py:318
  82.8 1.2 %collective-permute-start.13 = (bf16[32,1152]{1,0:T(8,128)(2,1)}, bf16[32,1152]{1,0:T(8,128)(2,1)S(1)}, u32[]{:S(2)}, u32[]{:S(2)}) collective-permute-start(bf16[32,1152]{1,0:T(8,128)(2,1)} %get-tuple-element.32), channel_id=1, source_target_pairs={{0,4},{4,8},{8,12},{12,0},{1,5},{5,9},{9,13},{13,1},{2,6},{6,10},{... | collective-permute-start | bytes 221192 | tf_op jit(solution)/shard_map/ppermute | solution.py:318
  84.0 1.0 %collective-permute-done.11.refs_1_ = bf16[32,1152]{1,0:T(8,128)(2,1)S(1)} collective-permute-done((bf16[32,1152]{1,0:T(8,128)(2,1)}, bf16[32,1152]{1,0:T(8,128)(2,1)S(1)}, u32[]{:S(2)}, u32[]{:S(2)}) %collective-permute-start.11) | collective-permute-done | bytes 73760 | tf_op jit(solution)/shard_map/ppermute | solution.py:318
  85.0 3.2 %collective-permute-done.12.refs_2_ = bf16[32,1152]{1,0:T(8,128)(2,1)S(1)} collective-permute-done((bf16[32,1152]{1,0:T(8,128)(2,1)}, bf16[32,1152]{1,0:T(8,128)(2,1)S(1)}, u32[]{:S(2)}, u32[]{:S(2)}) %collective-permute-start.12) | collective-permute-done | bytes 73760 | tf_op jit(solution)/shard_map/ppermute | solution.py:318
  89.8 2.6 %merge.1 = bf16[32,4096]{1,0:T(8,128)(2,1)} custom-call(bf16[32,1152]{1,0:T(8,128)(2,1)} %get-tuple-element.29.refs_0_, bf16[32,1152]{1,0:T(8,128)(2,1)} %copy-done.9, bf16[32,1152]{1,0:T(8,128)(2,1)} %copy-done.10, bf16[32,1152]{1,0:T(8,128)(2,1)} %copy-done.11, bf16[32,1152]{1,0:T(8,128)(2,1)} %get-tuple-element.37.refs_4_, bf16[32,1152]{1,0:T(8,128)(2,1)} %copy-done.6, ...), custom_call_target="tpu_custom_call" | custom-call | tf_op jit(solution)/shard_map/merge/pallas_call | solution.py:368
  (62 shorter events, 5.4 us)
Async XLA Ops:
  2.2 9.6 %collective-permute-start.4 = (bf16[288,384]{1,0:T(8,128)(2,1)}, bf16[288,384]{1,0:T(8,128)(2,1)S(1)}, u32[]{:S(2)}, u32[]{:S(2)}) collective-permute-start(bf16[288,384]{1,0:T(8,128)(2,1)} %get-tuple-element.28), channel_id=1, source_target_pairs={{0,4},{4,0},{8,12},{12,8},{1,5},{5,1},{9,13},{13,9},{2,6},{6,2},{1... | collective-permute-start | bytes 663560 | tf_op jit(solution)/shard_map/ppermute | solution.py:337
  5.3 10.4 %collective-permute-start.3 = (bf16[288,384]{1,0:T(8,128)(2,1)}, bf16[288,384]{1,0:T(8,128)(2,1)S(1)}, u32[]{:S(2)}, u32[]{:S(2)}) collective-permute-start(bf16[288,384]{1,0:T(8,128)(2,1)} %get-tuple-element.27), channel_id=1, source_target_pairs={{0,4},{4,0},{8,12},{12,8},{1,5},{5,1},{9,13},{13,9},{2,6},{6,2},{1... | collective-permute-start | bytes 663560 | tf_op jit(solution)/shard_map/ppermute | solution.py:337
  11.8 39.3 %copy-start.12 = (bf16[288,384]{1,0:T(8,128)(2,1)}, bf16[288,384]{1,0:T(8,128)(2,1)S(1)}, u32[]{:S(2)}) copy-start(bf16[288,384]{1,0:T(8,128)(2,1)S(1)} %collective-permute-done.4.refs_1_) | copy-start | bytes 663556
  11.8 19.0 %collective-permute-start.6 = (bf16[288,384]{1,0:T(8,128)(2,1)S(1)}, bf16[288,384]{1,0:T(8,128)(2,1)S(1)}, u32[]{:S(2)}, u32[]{:S(2)}) collective-permute-start(bf16[288,384]{1,0:T(8,128)(2,1)S(1)} %collective-permute-done.4.refs_1_), channel_id=1, source_target_pairs={{0,2},{1,3},{2,0},{3,1},{4,6},{5,7},{6,4},{7,5},{8,10},{9,11},{10,... | collective-permute-start | bytes 663560 | tf_op jit(solution)/shard_map/ppermute | solution.py:321
  15.7 35.4 %copy-start.13 = (bf16[288,384]{1,0:T(8,128)(2,1)}, bf16[288,384]{1,0:T(8,128)(2,1)S(1)}, u32[]{:S(2)}) copy-start(bf16[288,384]{1,0:T(8,128)(2,1)S(1)} %collective-permute-done.3.refs_0_) | copy-start | bytes 663556
  15.7 15.2 %collective-permute-start.5 = (bf16[288,384]{1,0:T(8,128)(2,1)S(1)}, bf16[288,384]{1,0:T(8,128)(2,1)S(1)}, u32[]{:S(2)}, u32[]{:S(2)}) collective-permute-start(bf16[288,384]{1,0:T(8,128)(2,1)S(1)} %collective-permute-done.3.refs_0_), channel_id=1, source_target_pairs={{0,2},{1,3},{2,0},{3,1},{4,6},{5,7},{6,4},{7,5},{8,10},{9,11},{10,... | collective-permute-start | bytes 663560 | tf_op jit(solution)/shard_map/ppermute | solution.py:321
  17.3 7.0 %collective-permute-start.14 = (bf16[32,1536]{1,0:T(8,128)(2,1)}, bf16[32,1536]{1,0:T(8,128)(2,1)S(1)}, u32[]{:S(2)}, u32[]{:S(2)}) collective-permute-start(bf16[32,1536]{1,0:T(8,128)(2,1)} %get-tuple-element.34), channel_id=1, source_target_pairs={{0,12},{4,0},{8,4},{12,8},{1,13},{5,1},{9,5},{13,9},{2,14},{6,2},{... | collective-permute-start | bytes 294920 | tf_op jit(solution)/shard_map/ppermute | solution.py:318
  20.9 9.3 %collective-permute-start.15 = (bf16[32,1536]{1,0:T(8,128)(2,1)}, bf16[32,1536]{1,0:T(8,128)(2,1)S(1)}, u32[]{:S(2)}, u32[]{:S(2)}) collective-permute-start(bf16[32,1536]{1,0:T(8,128)(2,1)} %get-tuple-element.33.refs_0_), channel_id=1, source_target_pairs={{0,8},{4,12},{8,0},{12,4},{1,9},{5,13},{9,1},{13,5},{2,10},{6,14},... | collective-permute-start | bytes 294920 | tf_op jit(solution)/shard_map/ppermute | solution.py:318
  20.9 9.3 %collective-permute-start.16 = (bf16[32,1536]{1,0:T(8,128)(2,1)}, bf16[32,1536]{1,0:T(8,128)(2,1)S(1)}, u32[]{:S(2)}, u32[]{:S(2)}) collective-permute-start(bf16[32,1536]{1,0:T(8,128)(2,1)} %get-tuple-element.34), channel_id=1, source_target_pairs={{0,4},{4,8},{8,12},{12,0},{1,5},{5,9},{9,13},{13,1},{2,6},{6,10},{... | collective-permute-start | bytes 294920 | tf_op jit(solution)/shard_map/ppermute | solution.py:318
  24.3 14.6 %copy-start = (bf16[32,1536]{1,0:T(8,128)(2,1)}, bf16[32,1536]{1,0:T(8,128)(2,1)S(1)}, u32[]{:S(2)}) copy-start(bf16[32,1536]{1,0:T(8,128)(2,1)S(1)} %collective-permute-done.14.refs_1_) | copy-start | bytes 294916
  24.3 7.0 %collective-permute-start = (bf16[32,1536]{1,0:T(8,128)(2,1)}, bf16[32,1536]{1,0:T(8,128)(2,1)S(1)}, u32[]{:S(2)}, u32[]{:S(2)}) collective-permute-start(bf16[32,1536]{1,0:T(8,128)(2,1)} %get-tuple-element.24), channel_id=1, source_target_pairs={{0,12},{4,0},{8,4},{12,8},{1,13},{5,1},{9,5},{13,9},{2,14},{6,2},{... | collective-permute-start | bytes 294920 | tf_op jit(solution)/shard_map/ppermute | solution.py:318
  30.2 20.7 %collective-permute-start.7 = (bf16[288,384]{1,0:T(8,128)(2,1)S(1)}, bf16[288,384]{1,0:T(8,128)(2,1)S(1)}, u32[]{:S(2)}, u32[]{:S(2)}) collective-permute-start(bf16[288,384]{1,0:T(8,128)(2,1)S(1)} %collective-permute-done.3.refs_0_), channel_id=1, source_target_pairs={{0,1},{1,0},{2,3},{3,2},{4,5},{5,4},{6,7},{7,6},{8,9},{9,8},{10,11... | collective-permute-start | bytes 663560 | tf_op jit(solution)/shard_map/ppermute | solution.py:321
  30.3 20.7 %collective-permute-start.8 = (bf16[288,384]{1,0:T(8,128)(2,1)S(1)}, bf16[288,384]{1,0:T(8,128)(2,1)S(1)}, u32[]{:S(2)}, u32[]{:S(2)}) collective-permute-start(bf16[288,384]{1,0:T(8,128)(2,1)S(1)} %collective-permute-done.4.refs_1_), channel_id=1, source_target_pairs={{0,1},{1,0},{2,3},{3,2},{4,5},{5,4},{6,7},{7,6},{8,9},{9,8},{10,11... | collective-permute-start | bytes 663560 | tf_op jit(solution)/shard_map/ppermute | solution.py:321
  30.8 13.1 %copy-start.14 = (bf16[288,384]{1,0:T(8,128)(2,1)}, bf16[288,384]{1,0:T(8,128)(2,1)S(1)}, u32[]{:S(2)}) copy-start(bf16[288,384]{1,0:T(8,128)(2,1)S(1)} %collective-permute-done.6.refs_3_) | copy-start | bytes 663556
  30.8 20.2 %collective-permute-start.10 = (bf16[288,384]{1,0:T(8,128)(2,1)S(1)}, bf16[288,384]{1,0:T(8,128)(2,1)S(1)}, u32[]{:S(2)}, u32[]{:S(2)}) collective-permute-start(bf16[288,384]{1,0:T(8,128)(2,1)S(1)} %collective-permute-done.6.refs_3_), channel_id=1, source_target_pairs={{0,1},{1,0},{2,3},{3,2},{4,5},{5,4},{6,7},{7,6},{8,9},{9,8},{10,11... | collective-permute-start | bytes 663560 | tf_op jit(solution)/shard_map/ppermute | solution.py:321
  30.9 20.2 %collective-permute-start.9 = (bf16[288,384]{1,0:T(8,128)(2,1)S(1)}, bf16[288,384]{1,0:T(8,128)(2,1)S(1)}, u32[]{:S(2)}, u32[]{:S(2)}) collective-permute-start(bf16[288,384]{1,0:T(8,128)(2,1)S(1)} %collective-permute-done.5.refs_2_), channel_id=1, source_target_pairs={{0,1},{1,0},{2,3},{3,2},{4,5},{5,4},{6,7},{7,6},{8,9},{9,8},{10,11... | collective-permute-start | bytes 663560 | tf_op jit(solution)/shard_map/ppermute | solution.py:321
  31.3 7.4 %collective-permute-start.1 = (bf16[32,1536]{1,0:T(8,128)(2,1)}, bf16[32,1536]{1,0:T(8,128)(2,1)S(1)}, u32[]{:S(2)}, u32[]{:S(2)}) collective-permute-start(bf16[32,1536]{1,0:T(8,128)(2,1)} %get-tuple-element.23.refs_0_), channel_id=1, source_target_pairs={{0,8},{4,12},{8,0},{12,4},{1,9},{5,13},{9,1},{13,5},{2,10},{6,14},... | collective-permute-start | bytes 294920 | tf_op jit(solution)/shard_map/ppermute | solution.py:318
  38.7 6.6 %collective-permute-start.2 = (bf16[32,1536]{1,0:T(8,128)(2,1)}, bf16[32,1536]{1,0:T(8,128)(2,1)S(1)}, u32[]{:S(2)}, u32[]{:S(2)}) collective-permute-start(bf16[32,1536]{1,0:T(8,128)(2,1)} %get-tuple-element.24), channel_id=1, source_target_pairs={{0,4},{4,8},{8,12},{12,0},{1,5},{5,9},{9,13},{13,1},{2,6},{6,10},{... | collective-permute-start | bytes 294920 | tf_op jit(solution)/shard_map/ppermute | solution.py:318
  60.0 22.8 %collective-permute-start.17 = (bf16[32,1152]{1,0:T(8,128)(2,1)}, bf16[32,1152]{1,0:T(8,128)(2,1)S(1)}, u32[]{:S(2)}, u32[]{:S(2)}) collective-permute-start(bf16[32,1152]{1,0:T(8,128)(2,1)} %get-tuple-element.38), channel_id=1, source_target_pairs={{0,12},{4,0},{8,4},{12,8},{1,13},{5,1},{9,5},{13,9},{2,14},{6,2},{... | collective-permute-start | bytes 221192 | tf_op jit(solution)/shard_map/ppermute | solution.py:318
  66.5 17.5 %collective-permute-start.18 = (bf16[32,1152]{1,0:T(8,128)(2,1)}, bf16[32,1152]{1,0:T(8,128)(2,1)S(1)}, u32[]{:S(2)}, u32[]{:S(2)}) collective-permute-start(bf16[32,1152]{1,0:T(8,128)(2,1)} %get-tuple-element.39), channel_id=1, source_target_pairs={{0,8},{4,12},{8,0},{12,4},{1,9},{5,13},{9,1},{13,5},{2,10},{6,14},... | collective-permute-start | bytes 221192 | tf_op jit(solution)/shard_map/ppermute | solution.py:318
  66.5 17.5 %collective-permute-start.19 = (bf16[32,1152]{1,0:T(8,128)(2,1)}, bf16[32,1152]{1,0:T(8,128)(2,1)S(1)}, u32[]{:S(2)}, u32[]{:S(2)}) collective-permute-start(bf16[32,1152]{1,0:T(8,128)(2,1)} %get-tuple-element.40), channel_id=1, source_target_pairs={{0,4},{4,8},{8,12},{12,0},{1,5},{5,9},{9,13},{13,1},{2,6},{6,10},{... | collective-permute-start | bytes 221192 | tf_op jit(solution)/shard_map/ppermute | solution.py:318
  75.7 9.3 %collective-permute-start.11 = (bf16[32,1152]{1,0:T(8,128)(2,1)}, bf16[32,1152]{1,0:T(8,128)(2,1)S(1)}, u32[]{:S(2)}, u32[]{:S(2)}) collective-permute-start(bf16[32,1152]{1,0:T(8,128)(2,1)} %get-tuple-element.30), channel_id=1, source_target_pairs={{0,12},{4,0},{8,4},{12,8},{1,13},{5,1},{9,5},{13,9},{2,14},{6,2},{... | collective-permute-start | bytes 221192 | tf_op jit(solution)/shard_map/ppermute | solution.py:318
  82.7 5.5 %collective-permute-start.12 = (bf16[32,1152]{1,0:T(8,128)(2,1)}, bf16[32,1152]{1,0:T(8,128)(2,1)S(1)}, u32[]{:S(2)}, u32[]{:S(2)}) collective-permute-start(bf16[32,1152]{1,0:T(8,128)(2,1)} %get-tuple-element.31), channel_id=1, source_target_pairs={{0,8},{4,12},{8,0},{12,4},{1,9},{5,13},{9,1},{13,5},{2,10},{6,14},... | collective-permute-start | bytes 221192 | tf_op jit(solution)/shard_map/ppermute | solution.py:318
  82.8 6.4 %collective-permute-start.13 = (bf16[32,1152]{1,0:T(8,128)(2,1)}, bf16[32,1152]{1,0:T(8,128)(2,1)S(1)}, u32[]{:S(2)}, u32[]{:S(2)}) collective-permute-start(bf16[32,1152]{1,0:T(8,128)(2,1)} %get-tuple-element.32), channel_id=1, source_target_pairs={{0,4},{4,8},{8,12},{12,0},{1,5},{5,9},{9,13},{13,1},{2,6},{6,10},{... | collective-permute-start | bytes 221192 | tf_op jit(solution)/shard_map/ppermute | solution.py:318
  (16 other events, 74.5 us)

commit v5 on v4

--- a/solution.py
+++ b/solution.py
@@ -12,9 +12,9 @@
 GROUP = 2
 LANES = 4
 BLOCK_PAGES = 8
-HEADS_STEP = 4
+HEADS_STEP = 8
 PIECES = 2
-CHUNKS = 2
+CHUNKS = 1
 
 
 FLOOR = -1e30
@@ -56,7 +56,7 @@
 
 def absorb_kernel(dims, tok_ref, off_ref, *refs):
     members, first, hc, hh, nope, rope, latent = dims
-    q_refs, keys_hbm, qs_ref, limit_ref, wk, sem = refs[:members], *refs[members:]
+    q_refs, keys_hbm, qs_ref, limit_ref, wk, turned, sem = refs[:members], *refs[members:]
     rows = limit_ref.shape[0]
     local_rows = rows // members
     member = lax.axis_index("pages")
@@ -72,18 +72,14 @@
     order = (jnp.broadcast_to(token, (rows, rows)) == wanted).astype(jnp.bfloat16)
     limit = jnp.max(jnp.where(across == wanted, off_ref[...], 0), axis=1, keepdims=True)
     limit_ref[...] = jnp.broadcast_to(limit, limit_ref.shape)
+    whole = jnp.concatenate([q[...] for q in q_refs], axis=0)
+    turned[...] = jnp.dot(order, whole, preferred_element_type=jnp.float32).astype(jnp.bfloat16)
     copy.wait()
     for h in range(hc):
-        query = jnp.concatenate([q[:, h * nope:(h + 1) * nope] for q in q_refs], axis=0)
-        query = jnp.dot(order, query, preferred_element_type=jnp.float32).astype(jnp.bfloat16)
-        lat = jnp.dot(query, wk[h], preferred_element_type=jnp.float32)
+        lat = jnp.dot(turned[:, h * nope:(h + 1) * nope], wk[h], preferred_element_type=jnp.float32)
         qs_ref[h * rows:(h + 1) * rows, :latent] = lat.astype(jnp.bfloat16)
-    for h in range(0, hc, 2):
         at = hc * nope + h * rope
-        both = jnp.concatenate([q[:, at:at + 2 * rope] for q in q_refs], axis=0)
-        both = jnp.dot(order, both, preferred_element_type=jnp.float32).astype(jnp.bfloat16)
-        for i in range(2):
-            qs_ref[(h + i) * rows:(h + i + 1) * rows, latent:] = both[:, i * rope:(i + 1) * rope]
+        qs_ref[h * rows:(h + 1) * rows, latent:] = turned[:, at:at + rope]
 
 
 def attend_kernel(dims, counts_ref, limit_ref, qs_hbm, *refs):
@@ -353,7 +349,11 @@
             ],
             in_specs=[vmem] * (2 + members) + [hbm],
             out_specs=[vmem] * 2,
-            scratch_shapes=[pltpu.VMEM((hc, nope, latent), bf16), pltpu.SemaphoreType.DMA(())],
+            scratch_shapes=[
+                pltpu.VMEM((hc, nope, latent), bf16),
+                pltpu.VMEM((rows, hc * (nope + rope)), bf16),
+                pltpu.SemaphoreType.DMA(()),
+            ],
         )(query_token[None, :], query_offsets[None, :], *blocks, absorb_keys))
 
     arrived = []

time: 92.9 us -> 82 us (0.88)
  starting transfers between devices: 34.1 us -> 21.2 us
  waiting for transfers between devices: 25 us -> 36.7 us
  Pallas kernels: 31 us -> 21.5 us
    ppermute x12 -> x6, starting transfers between devices: 26.3 us -> 13.8 us  [over_pages(): lax.ppermute(x, 'pages', [(i, (i - s) % members) for i in range(members)])]
    ppermute x12 -> x6, waiting for transfers between devices: 16.6 us -> 28.4 us  [over_pages(): lax.ppermute(x, 'pages', [(i, (i - s) % members) for i in range(members)])]
    pallas_call x2 -> x1, Pallas kernels: 10 us -> 5.04 us  [on_device(): pl.pallas_call(functools.partial(absorb_kernel, (members, c * hc, hc, hh,...]
    pallas_call x2 -> x1, Pallas kernels: 16.2 us -> 11.9 us  [on_device(): attend_call(members, c * hc, hc, hh, hb, nope, rope, latent, vhead, rows,...]
    unnamed x40 -> x28, local copies, waits for them, and re-layouts: 2.11 us -> 2.22 us
  transfers between devices with their start and end apart: 20 -> 14, of which waited for: 9 -> 7; matrix products, arithmetic and copies ran while one was open for 0% -> 0% of each run, Pallas kernels for 20% -> 6%
where the time goes in v5:
time: 82 us; the launch traced here: 81.8 us
  waiting for transfers between devices  36.7 us (45%)
  Pallas kernels  21.5 us (26%)
  starting transfers between devices  21.2 us (26%)
  local copies, waits for them, and re-layouts  2.22 us (3%)
    ppermute x6, waiting for transfers between devices, over_pages(): lax.ppermute(x, 'pages', [(i, (i - s) % members) for i in range(members)])  28.4 us
    ppermute x6, starting transfers between devices, over_pages(): lax.ppermute(x, 'pages', [(i, (i - s) % members) for i in range(members)])  13.8 us
    pallas_call x1, Pallas kernels, on_device(): attend_call(members, c * hc, hc, hh, hb, nope, rope, latent, vhead, rows,...  11.9 us
    ppermute x2, waiting for transfers between devices, on_device(): lax.ppermute(pieces[p], 'pages', [(i, i ^ 1) for i in range(members)])  8.36 us
    pallas_call x1, Pallas kernels, on_device(): pl.pallas_call(functools.partial(absorb_kernel, (members, c * hc, hc, hh,...  5.04 us
    ppermute x6, starting transfers between devices, over_heads(): return lax.ppermute(x, 'heads', [(i, i ^ bit) for i in range(devices)])  4.19 us
    ppermute x2, starting transfers between devices, on_device(): lax.ppermute(pieces[p], 'pages', [(i, i ^ 1) for i in range(members)])  3.2 us
    pallas_call x1, Pallas kernels, on_device(): pl.pallas_call(functools.partial(merge_kernel, (hc, vhead, members, chunk...  2.44 us
  transfers between devices with their start and end apart: 14, of which 7 were waited for; matrix products, arithmetic and copies ran while one was open for 0% of the time, Pallas kernels for 6%

profile of v5, /device:TPU:0, one launch (start us, length us, event | category | flops | bytes accessed | tf_op | source)
XLA Modules:
  0.0 81.8 jit_solution(14095872556318855479)
XLA Ops:
  0.0 2.1 %pack.1 = (bf16[288,384]{1,0:T(8,128)(2,1)}, bf16[288,384]{1,0:T(8,128)(2,1)}, bf16[32,3072]{1,0:T(8,128)(2,1)}, bf16[32,3072]{1,0:T(8,128)(2,1)}) custom-call(bf16[32,4096]{1,0:T(8,128)(2,1)} %nope_ref.1, bf16[32,2048]{1,0:T(8,128)(2,1)} %rope_ref.1, bf16[576,1536]{1,0:T(8,128)(2,1)} %bitcast.3), custom_call_target="tpu_custom_call" | custom-call | tf_op jit(solution)/shard_map/pack/pallas_call | solution.py:320
  2.2 3.1 %collective-permute-start.4 = (bf16[288,384]{1,0:T(8,128)(2,1)}, bf16[288,384]{1,0:T(8,128)(2,1)S(1)}, u32[]{:S(2)}, u32[]{:S(2)}) collective-permute-start(bf16[288,384]{1,0:T(8,128)(2,1)} %get-tuple-element.20), channel_id=1, source_target_pairs={{0,4},{4,0},{8,12},{12,8},{1,5},{5,1},{9,13},{13,9},{2,6},{6,2},{1... | collective-permute-start | bytes 663560 | tf_op jit(solution)/shard_map/ppermute | solution.py:333
  5.4 6.4 %collective-permute-done.4.refs_1_ = bf16[288,384]{1,0:T(8,128)(2,1)S(1)} collective-permute-done((bf16[288,384]{1,0:T(8,128)(2,1)}, bf16[288,384]{1,0:T(8,128)(2,1)S(1)}, u32[]{:S(2)}, u32[]{:S(2)}) %collective-permute-start.4) | collective-permute-done | bytes 221216 | tf_op jit(solution)/shard_map/ppermute | solution.py:333
  11.8 1.9 %collective-permute-start.6 = (bf16[288,384]{1,0:T(8,128)(2,1)S(1)}, bf16[288,384]{1,0:T(8,128)(2,1)S(1)}, u32[]{:S(2)}, u32[]{:S(2)}) collective-permute-start(bf16[288,384]{1,0:T(8,128)(2,1)S(1)} %collective-permute-done.4.refs_1_), channel_id=1, source_target_pairs={{0,2},{1,3},{2,0},{3,1},{4,6},{5,7},{6,4},{7,5},{8,10},{9,11},{10,... | collective-permute-start | bytes 663560 | tf_op jit(solution)/shard_map/ppermute | solution.py:317
  13.7 2.0 %collective-permute-done.3.refs_0_ = bf16[288,384]{1,0:T(8,128)(2,1)S(1)} collective-permute-done((bf16[288,384]{1,0:T(8,128)(2,1)}, bf16[288,384]{1,0:T(8,128)(2,1)S(1)}, u32[]{:S(2)}, u32[]{:S(2)}) %collective-permute-start.3) | collective-permute-done | bytes 221216 | tf_op jit(solution)/shard_map/ppermute | solution.py:333
  15.7 1.7 %collective-permute-start.5 = (bf16[288,384]{1,0:T(8,128)(2,1)S(1)}, bf16[288,384]{1,0:T(8,128)(2,1)S(1)}, u32[]{:S(2)}, u32[]{:S(2)}) collective-permute-start(bf16[288,384]{1,0:T(8,128)(2,1)S(1)} %collective-permute-done.3.refs_0_), channel_id=1, source_target_pairs={{0,2},{1,3},{2,0},{3,1},{4,6},{5,7},{6,4},{7,5},{8,10},{9,11},{10,... | collective-permute-start | bytes 663560 | tf_op jit(solution)/shard_map/ppermute | solution.py:317
  17.3 3.6 %collective-permute-start = (bf16[32,3072]{1,0:T(8,128)(2,1)}, bf16[32,3072]{1,0:T(8,128)(2,1)S(1)}, u32[]{:S(2)}, u32[]{:S(2)}) collective-permute-start(bf16[32,3072]{1,0:T(8,128)(2,1)} %get-tuple-element.16), channel_id=1, source_target_pairs={{0,12},{4,0},{8,4},{12,8},{1,13},{5,1},{9,5},{13,9},{2,14},{6,2},{... | collective-permute-start | bytes 589832 | tf_op jit(solution)/shard_map/ppermute | solution.py:314
  20.9 5.5 %collective-permute-done.refs_1_ = bf16[32,3072]{1,0:T(8,128)(2,1)S(1)} collective-permute-done((bf16[32,3072]{1,0:T(8,128)(2,1)}, bf16[32,3072]{1,0:T(8,128)(2,1)S(1)}, u32[]{:S(2)}, u32[]{:S(2)}) %collective-permute-start) | collective-permute-done | bytes 196640 | tf_op jit(solution)/shard_map/ppermute | solution.py:314
  26.4 0.5 collective-permute-start.10
  26.9 0.1 collective-permute-start.9
  27.0 5.6 %collective-permute-done.1.refs_2_ = bf16[32,3072]{1,0:T(8,128)(2,1)S(1)} collective-permute-done((bf16[32,3072]{1,0:T(8,128)(2,1)}, bf16[32,3072]{1,0:T(8,128)(2,1)S(1)}, u32[]{:S(2)}, u32[]{:S(2)}) %collective-permute-start.1) | collective-permute-done | bytes 196640 | tf_op jit(solution)/shard_map/ppermute | solution.py:314
  32.6 0.8 collective-permute-start.2
  33.4 7.3 %collective-permute-done.2.refs_3_ = bf16[32,3072]{1,0:T(8,128)(2,1)S(1)} collective-permute-done((bf16[32,3072]{1,0:T(8,128)(2,1)}, bf16[32,3072]{1,0:T(8,128)(2,1)S(1)}, u32[]{:S(2)}, u32[]{:S(2)}) %collective-permute-start.2) | collective-permute-done | bytes 196640 | tf_op jit(solution)/shard_map/ppermute | solution.py:314
  40.7 0.7 copy-done.2
  41.4 5.0 %shard_map.82 = (bf16[2048,576]{1,0:T(8,128)(2,1)}, s32[128,128]{1,0:T(8,128)}) custom-call(s32[1,128]{1,0:T(1,128)} %bitcast.5, s32[1,128]{1,0:T(1,128)} %bitcast.6, bf16[32,3072]{1,0:T(8,128)(2,1)} %get-tuple-element.15.refs_0_, bf16[32,3072]{1,0:T(8,128)(2,1)} %copy-done, bf16[32,3072]{1,0:T(8,128)(2,1)} %copy-done.1, bf16[32,3072]{1,0:T(8,128)(2,1)} %copy-done.2, ...), custom_call_target="tpu_custom_call" | custom-call | tf_op jit(solution)/shard_map/pallas_call | solution.py:344
  46.5 0.6 copy-done.10
  47.3 0.1 copy-done.13
  47.4 11.9 %shard_map.83 = (bf16[32,2176]{1,0:T(8,128)(2,1)}, bf16[32,2176]{1,0:T(8,128)(2,1)}, bf16[32,2176]{1,0:T(8,128)(2,1)}, bf16[32,2176]{1,0:T(8,128)(2,1)}) custom-call(s32[4]{0:T(128)} %counts_ref.1, s32[128,128]{1,0:T(8,128)} %get-tuple-element.17.limit_ref, bf16[2048,576]{1,0:T(8,128)(2,1)} %get-tuple-element.18.qs_hbm, bf16[288,384]{1,0:T(8,128)(2,1)} %copy-done.7, ...), custom_call_target="tpu_custom_call" | custom-call | flops 8000000000 | bytes 8000000 | tf_op jit(solution)/shard_map/pallas_call | solution.py:361
  59.2 8.8 %collective-permute-start.11 = (bf16[32,2176]{1,0:T(8,128)(2,1)}, bf16[32,2176]{1,0:T(8,128)(2,1)S(1)}, u32[]{:S(2)}, u32[]{:S(2)}) collective-permute-start(bf16[32,2176]{1,0:T(8,128)(2,1)} %get-tuple-element.22), channel_id=1, source_target_pairs={{0,12},{4,0},{8,4},{12,8},{1,13},{5,1},{9,5},{13,9},{2,14},{6,2},{... | collective-permute-start | bytes 417800 | tf_op jit(solution)/shard_map/ppermute | solution.py:314
  68.0 0.6 collective-permute-start.13
  68.6 3.7 %collective-permute-done.11.refs_1_ = bf16[32,2176]{1,0:T(8,128)(2,1)S(1)} collective-permute-done((bf16[32,2176]{1,0:T(8,128)(2,1)}, bf16[32,2176]{1,0:T(8,128)(2,1)S(1)}, u32[]{:S(2)}, u32[]{:S(2)}) %collective-permute-start.11) | collective-permute-done | bytes 139296 | tf_op jit(solution)/shard_map/ppermute | solution.py:314
  72.4 6.3 %collective-permute-done.12.refs_2_ = bf16[32,2176]{1,0:T(8,128)(2,1)S(1)} collective-permute-done((bf16[32,2176]{1,0:T(8,128)(2,1)}, bf16[32,2176]{1,0:T(8,128)(2,1)S(1)}, u32[]{:S(2)}, u32[]{:S(2)}) %collective-permute-start.12) | collective-permute-done | bytes 139296 | tf_op jit(solution)/shard_map/ppermute | solution.py:314
  78.6 0.6 copy-done.4
  79.3 2.4 %merge.1 = bf16[32,4096]{1,0:T(8,128)(2,1)} custom-call(bf16[32,2176]{1,0:T(8,128)(2,1)} %get-tuple-element.21.refs_0_, bf16[32,2176]{1,0:T(8,128)(2,1)} %copy-done.3, bf16[32,2176]{1,0:T(8,128)(2,1)} %copy-done.4, bf16[32,2176]{1,0:T(8,128)(2,1)} %copy-done.5), custom_call_target="tpu_custom_call" | custom-call | tf_op jit(solution)/shard_map/merge/pallas_call | solution.py:368
  (36 shorter events, 0.4 us)
Async XLA Ops:
  2.2 9.6 %collective-permute-start.4 = (bf16[288,384]{1,0:T(8,128)(2,1)}, bf16[288,384]{1,0:T(8,128)(2,1)S(1)}, u32[]{:S(2)}, u32[]{:S(2)}) collective-permute-start(bf16[288,384]{1,0:T(8,128)(2,1)} %get-tuple-element.20), channel_id=1, source_target_pairs={{0,4},{4,0},{8,12},{12,8},{1,5},{5,1},{9,13},{13,9},{2,6},{6,2},{1... | collective-permute-start | bytes 663560 | tf_op jit(solution)/shard_map/ppermute | solution.py:333
  5.3 10.4 %collective-permute-start.3 = (bf16[288,384]{1,0:T(8,128)(2,1)}, bf16[288,384]{1,0:T(8,128)(2,1)S(1)}, u32[]{:S(2)}, u32[]{:S(2)}) collective-permute-start(bf16[288,384]{1,0:T(8,128)(2,1)} %get-tuple-element.19), channel_id=1, source_target_pairs={{0,4},{4,0},{8,12},{12,8},{1,5},{5,1},{9,13},{13,9},{2,6},{6,2},{1... | collective-permute-start | bytes 663560 | tf_op jit(solution)/shard_map/ppermute | solution.py:333
  11.8 34.7 %copy-start.6 = (bf16[288,384]{1,0:T(8,128)(2,1)}, bf16[288,384]{1,0:T(8,128)(2,1)S(1)}, u32[]{:S(2)}) copy-start(bf16[288,384]{1,0:T(8,128)(2,1)S(1)} %collective-permute-done.4.refs_1_) | copy-start | bytes 663556
  11.8 14.6 %collective-permute-start.6 = (bf16[288,384]{1,0:T(8,128)(2,1)S(1)}, bf16[288,384]{1,0:T(8,128)(2,1)S(1)}, u32[]{:S(2)}, u32[]{:S(2)}) collective-permute-start(bf16[288,384]{1,0:T(8,128)(2,1)S(1)} %collective-permute-done.4.refs_1_), channel_id=1, source_target_pairs={{0,2},{1,3},{2,0},{3,1},{4,6},{5,7},{6,4},{7,5},{8,10},{9,11},{10,... | collective-permute-start | bytes 663560 | tf_op jit(solution)/shard_map/ppermute | solution.py:317
  15.7 30.9 %copy-start.7 = (bf16[288,384]{1,0:T(8,128)(2,1)}, bf16[288,384]{1,0:T(8,128)(2,1)S(1)}, u32[]{:S(2)}) copy-start(bf16[288,384]{1,0:T(8,128)(2,1)S(1)} %collective-permute-done.3.refs_0_) | copy-start | bytes 663556
  15.7 11.3 %collective-permute-start.5 = (bf16[288,384]{1,0:T(8,128)(2,1)S(1)}, bf16[288,384]{1,0:T(8,128)(2,1)S(1)}, u32[]{:S(2)}, u32[]{:S(2)}) collective-permute-start(bf16[288,384]{1,0:T(8,128)(2,1)S(1)} %collective-permute-done.3.refs_0_), channel_id=1, source_target_pairs={{0,2},{1,3},{2,0},{3,1},{4,6},{5,7},{6,4},{7,5},{8,10},{9,11},{10,... | collective-permute-start | bytes 663560 | tf_op jit(solution)/shard_map/ppermute | solution.py:317
  17.3 9.1 %collective-permute-start = (bf16[32,3072]{1,0:T(8,128)(2,1)}, bf16[32,3072]{1,0:T(8,128)(2,1)S(1)}, u32[]{:S(2)}, u32[]{:S(2)}) collective-permute-start(bf16[32,3072]{1,0:T(8,128)(2,1)} %get-tuple-element.16), channel_id=1, source_target_pairs={{0,12},{4,0},{8,4},{12,8},{1,13},{5,1},{9,5},{13,9},{2,14},{6,2},{... | collective-permute-start | bytes 589832 | tf_op jit(solution)/shard_map/ppermute | solution.py:314
  20.9 11.7 %collective-permute-start.1 = (bf16[32,3072]{1,0:T(8,128)(2,1)}, bf16[32,3072]{1,0:T(8,128)(2,1)S(1)}, u32[]{:S(2)}, u32[]{:S(2)}) collective-permute-start(bf16[32,3072]{1,0:T(8,128)(2,1)} %get-tuple-element.15.refs_0_), channel_id=1, source_target_pairs={{0,8},{4,12},{8,0},{12,4},{1,9},{5,13},{9,1},{13,5},{2,10},{6,14},... | collective-permute-start | bytes 589832 | tf_op jit(solution)/shard_map/ppermute | solution.py:314
  20.9 25.5 %collective-permute-start.7 = (bf16[288,384]{1,0:T(8,128)(2,1)S(1)}, bf16[288,384]{1,0:T(8,128)(2,1)S(1)}, u32[]{:S(2)}, u32[]{:S(2)}) collective-permute-start(bf16[288,384]{1,0:T(8,128)(2,1)S(1)} %collective-permute-done.3.refs_0_), channel_id=1, source_target_pairs={{0,1},{1,0},{2,3},{3,2},{4,5},{5,4},{6,7},{7,6},{8,9},{9,8},{10,11... | collective-permute-start | bytes 663560 | tf_op jit(solution)/shard_map/ppermute | solution.py:317
  26.4 14.3 %copy-start = (bf16[32,3072]{1,0:T(8,128)(2,1)}, bf16[32,3072]{1,0:T(8,128)(2,1)S(1)}, u32[]{:S(2)}) copy-start(bf16[32,3072]{1,0:T(8,128)(2,1)S(1)} %collective-permute-done.refs_1_) | copy-start | bytes 589828
  26.4 20.0 %collective-permute-start.8 = (bf16[288,384]{1,0:T(8,128)(2,1)S(1)}, bf16[288,384]{1,0:T(8,128)(2,1)S(1)}, u32[]{:S(2)}, u32[]{:S(2)}) collective-permute-start(bf16[288,384]{1,0:T(8,128)(2,1)S(1)} %collective-permute-done.4.refs_1_), channel_id=1, source_target_pairs={{0,1},{1,0},{2,3},{3,2},{4,5},{5,4},{6,7},{7,6},{8,9},{9,8},{10,11... | collective-permute-start | bytes 663560 | tf_op jit(solution)/shard_map/ppermute | solution.py:317
  26.4 20.1 %copy-start.8 = (bf16[288,384]{1,0:T(8,128)(2,1)}, bf16[288,384]{1,0:T(8,128)(2,1)S(1)}, u32[]{:S(2)}) copy-start(bf16[288,384]{1,0:T(8,128)(2,1)S(1)} %collective-permute-done.6.refs_3_) | copy-start | bytes 663556
  26.4 20.0 %collective-permute-start.10 = (bf16[288,384]{1,0:T(8,128)(2,1)S(1)}, bf16[288,384]{1,0:T(8,128)(2,1)S(1)}, u32[]{:S(2)}, u32[]{:S(2)}) collective-permute-start(bf16[288,384]{1,0:T(8,128)(2,1)S(1)} %collective-permute-done.6.refs_3_), channel_id=1, source_target_pairs={{0,1},{1,0},{2,3},{3,2},{4,5},{5,4},{6,7},{7,6},{8,9},{9,8},{10,11... | collective-permute-start | bytes 663560 | tf_op jit(solution)/shard_map/ppermute | solution.py:317
  26.9 19.6 %copy-start.9 = (bf16[288,384]{1,0:T(8,128)(2,1)}, bf16[288,384]{1,0:T(8,128)(2,1)S(1)}, u32[]{:S(2)}) copy-start(bf16[288,384]{1,0:T(8,128)(2,1)S(1)} %collective-permute-done.5.refs_2_) | copy-start | bytes 663556
  26.9 19.5 %collective-permute-start.9 = (bf16[288,384]{1,0:T(8,128)(2,1)S(1)}, bf16[288,384]{1,0:T(8,128)(2,1)S(1)}, u32[]{:S(2)}, u32[]{:S(2)}) collective-permute-start(bf16[288,384]{1,0:T(8,128)(2,1)S(1)} %collective-permute-done.5.refs_2_), channel_id=1, source_target_pairs={{0,1},{1,0},{2,3},{3,2},{4,5},{5,4},{6,7},{7,6},{8,9},{9,8},{10,11... | collective-permute-start | bytes 663560 | tf_op jit(solution)/shard_map/ppermute | solution.py:317
  32.6 8.1 %copy-start.1 = (bf16[32,3072]{1,0:T(8,128)(2,1)}, bf16[32,3072]{1,0:T(8,128)(2,1)S(1)}, u32[]{:S(2)}) copy-start(bf16[32,3072]{1,0:T(8,128)(2,1)S(1)} %collective-permute-done.1.refs_2_) | copy-start | bytes 589828
  32.6 8.1 %collective-permute-start.2 = (bf16[32,3072]{1,0:T(8,128)(2,1)}, bf16[32,3072]{1,0:T(8,128)(2,1)S(1)}, u32[]{:S(2)}, u32[]{:S(2)}) collective-permute-start(bf16[32,3072]{1,0:T(8,128)(2,1)} %get-tuple-element.16), channel_id=1, source_target_pairs={{0,4},{4,8},{8,12},{12,0},{1,5},{5,9},{9,13},{13,1},{2,6},{6,10},{... | collective-permute-start | bytes 589832 | tf_op jit(solution)/shard_map/ppermute | solution.py:314
  46.4 0.7 copy-start.11
  46.5 0.8 copy-start.12
  46.5 0.9 %copy-start.13 = (bf16[288,384]{1,0:T(8,128)(2,1)}, bf16[288,384]{1,0:T(8,128)(2,1)S(1)}, u32[]{:S(2)}) copy-start(bf16[288,384]{1,0:T(8,128)(2,1)S(1)} %collective-permute-done.9.refs_6_) | copy-start | bytes 663556
  59.2 13.1 %collective-permute-start.11 = (bf16[32,2176]{1,0:T(8,128)(2,1)}, bf16[32,2176]{1,0:T(8,128)(2,1)S(1)}, u32[]{:S(2)}, u32[]{:S(2)}) collective-permute-start(bf16[32,2176]{1,0:T(8,128)(2,1)} %get-tuple-element.22), channel_id=1, source_target_pairs={{0,12},{4,0},{8,4},{12,8},{1,13},{5,1},{9,5},{13,9},{2,14},{6,2},{... | collective-permute-start | bytes 417800 | tf_op jit(solution)/shard_map/ppermute | solution.py:314
  68.0 10.6 %collective-permute-start.12 = (bf16[32,2176]{1,0:T(8,128)(2,1)}, bf16[32,2176]{1,0:T(8,128)(2,1)S(1)}, u32[]{:S(2)}, u32[]{:S(2)}) collective-permute-start(bf16[32,2176]{1,0:T(8,128)(2,1)} %get-tuple-element.23), channel_id=1, source_target_pairs={{0,8},{4,12},{8,0},{12,4},{1,9},{5,13},{9,1},{13,5},{2,10},{6,14},... | collective-permute-start | bytes 417800 | tf_op jit(solution)/shard_map/ppermute | solution.py:314
  68.0 10.6 %collective-permute-start.13 = (bf16[32,2176]{1,0:T(8,128)(2,1)}, bf16[32,2176]{1,0:T(8,128)(2,1)S(1)}, u32[]{:S(2)}, u32[]{:S(2)}) collective-permute-start(bf16[32,2176]{1,0:T(8,128)(2,1)} %get-tuple-element.24), channel_id=1, source_target_pairs={{0,4},{4,8},{8,12},{12,0},{1,5},{5,9},{9,13},{13,1},{2,6},{6,10},{... | collective-permute-start | bytes 417800 | tf_op jit(solution)/shard_map/ppermute | solution.py:314
  72.4 6.3 %copy-start.3 = (bf16[32,2176]{1,0:T(8,128)(2,1)}, bf16[32,2176]{1,0:T(8,128)(2,1)S(1)}, u32[]{:S(2)}) copy-start(bf16[32,2176]{1,0:T(8,128)(2,1)S(1)} %collective-permute-done.11.refs_1_) | copy-start | bytes 417796
  (4 other events, 2.7 us)

commit v6 on v5

--- a/solution.py
+++ b/solution.py
@@ -22,21 +22,25 @@
 LOG2E = 1.4426950408889634
 
 
-def pack_kernel(dims, nope_ref, rope_ref, cache_ref, *refs):
-    nope_width, rope_width, quarter_cols, chunks = dims
+def pack_pages_kernel(quarter_cols, cache_ref, *refs):
+    outs, sems = refs[:-1], refs[-1]
+    lane = lax.axis_index("heads") % LANES
+    depth = cache_ref.shape[0] // PIECES
+    at = pl.ds(pl.multiple_of(lane * quarter_cols, 128), quarter_cols)
+    copies = [
+        pltpu.make_async_copy(cache_ref.at[pl.ds(p * depth, depth), at], outs[p], sems.at[p]) for p in range(PIECES)
+    ]
+    for c in copies:
+        c.start()
+    for c in copies:
+        c.wait()
+
+
+def pack_queries_kernel(dims, nope_ref, rope_ref, *refs):
+    nope_width, rope_width, chunks = dims
     outs, sems = refs[:-1], refs[-1]
     mine = lax.axis_index("pages") % GROUP
-    lane = lax.axis_index("heads") % LANES
-    depth = cache_ref.shape[0] // PIECES
     copies = []
-    for p in range(PIECES):
-        copies.append(
-            pltpu.make_async_copy(
-                cache_ref.at[pl.ds(p * depth, depth), pl.ds(pl.multiple_of(lane * quarter_cols, 128), quarter_cols)],
-                outs[p],
-                sems.at[p],
-            )
-        )
     for c in range(chunks):
         for e in range(GROUP):
             which = ((mine + e) % GROUP) * chunks + c
@@ -44,7 +48,7 @@
                 copies.append(
                     pltpu.make_async_copy(
                         ref.at[:, pl.ds(pl.multiple_of(which * width, 128), width)],
-                        outs[PIECES + c * GROUP + e].at[:, pl.ds(at, width)],
+                        outs[c * GROUP + e].at[:, pl.ds(at, width)],
                         sems.at[len(copies)],
                     )
                 )
@@ -54,40 +58,13 @@
         c.wait()
 
 
-def absorb_kernel(dims, tok_ref, off_ref, *refs):
-    members, first, hc, hh, nope, rope, latent = dims
-    q_refs, keys_hbm, qs_ref, limit_ref, wk, turned, sem = refs[:members], *refs[members:]
-    rows = limit_ref.shape[0]
-    local_rows = rows // members
-    member = lax.axis_index("pages")
-    mine = member % GROUP
-    copy = pltpu.make_async_copy(keys_hbm.at[pl.ds(mine * hh + first, hc)], wk, sem)
-    copy.start()
-    token = pltpu.roll(
-        jnp.broadcast_to(tok_ref[...], (8, rows)), lax.rem(rows - member * local_rows, rows), axis=1
-    )[:1]
-    across = lax.broadcasted_iota(jnp.int32, (rows, rows), 1)
-    down = lax.broadcasted_iota(jnp.int32, (rows, rows), 0)
-    wanted = lax.rem(member - down // local_rows + members, members) * local_rows + lax.rem(down, local_rows)
-    order = (jnp.broadcast_to(token, (rows, rows)) == wanted).astype(jnp.bfloat16)
-    limit = jnp.max(jnp.where(across == wanted, off_ref[...], 0), axis=1, keepdims=True)
-    limit_ref[...] = jnp.broadcast_to(limit, limit_ref.shape)
-    whole = jnp.concatenate([q[...] for q in q_refs], axis=0)
-    turned[...] = jnp.dot(order, whole, preferred_element_type=jnp.float32).astype(jnp.bfloat16)
-    copy.wait()
-    for h in range(hc):
-        lat = jnp.dot(turned[:, h * nope:(h + 1) * nope], wk[h], preferred_element_type=jnp.float32)
-        qs_ref[h * rows:(h + 1) * rows, :latent] = lat.astype(jnp.bfloat16)
-        at = hc * nope + h * rope
-        qs_ref[h * rows:(h + 1) * rows, latent:] = turned[:, at:at + rope]
-
-
-def attend_kernel(dims, counts_ref, limit_ref, qs_hbm, *refs):
+def attend_kernel(dims, counts_ref, tok_ref, off_ref, *refs):
     members, first, hc, hh, hb, nope, rope, latent, vhead, rows, slots = dims
+    q_refs, refs = refs[:members], refs[members:]
     part_refs, refs = refs[:LANES * PIECES], refs[LANES * PIECES:]
-    own_ref, values_hbm = refs[:2]
-    out_refs, refs = refs[2:2 + members], refs[2 + members:]
-    tiles, wv, bias, qs, sbuf, mx, den, acc, lse, sems, own_sems, part_sems = refs
+    own_ref, keys_hbm, values_hbm = refs[:3]
+    out_refs, refs = refs[3:3 + members], refs[3 + members:]
+    raw, turned, wk, wv, tiles, bias, qs, sbuf, mx, den, acc, lse, sems, own_sems, part_sems = refs
     local_rows = rows // members
     block = BLOCK_PAGES * PAGE
     cols = slots * PAGE
@@ -106,12 +83,11 @@
     blocks = own_blocks + part_blocks
 
     query_copies = [
-        pltpu.make_async_copy(
-            qs_hbm.at[pl.ds(g * group_rows, group_rows)], qs.at[pl.ds(g * group_rows, group_rows)], sems.at[g]
-        )
-        for g in range(steps)
+        pltpu.make_async_copy(q, raw.at[pl.ds(s * local_rows, local_rows)], sems.at[2 + s])
+        for s, q in enumerate(q_refs)
     ]
-    value_copy = pltpu.make_async_copy(values_hbm.at[pl.ds(mine * hh + first, hc)], wv, sems.at[steps])
+    key_copy = pltpu.make_async_copy(keys_hbm.at[pl.ds(mine * hh + first, hc)], wk, sems.at[0])
+    value_copy = pltpu.make_async_copy(values_hbm.at[pl.ds(mine * hh + first, hc)], wv, sems.at[1])
     tile_copies = []
     for b in range(-(-cols // block)):
         at = pl.ds(b * block, min(block, cols - b * block))
@@ -128,14 +104,22 @@
                     part_sems.at[i * PIECES + p],
                 ),
             ))
-    query_copies[0].start()
+    for copy in query_copies + [key_copy]:
+        copy.start()
     for used, copy in tile_copies:
         pl.when(used)(copy.start)
-    for copy in query_copies[1:] + [value_copy]:
-        copy.start()
+    value_copy.start()
+
+    token = pltpu.roll(
+        jnp.broadcast_to(tok_ref[...], (8, rows)), lax.rem(rows - member * local_rows, rows), axis=1
+    )[:1]
+    across = lax.broadcasted_iota(jnp.int32, (rows, rows), 1)
+    down = lax.broadcasted_iota(jnp.int32, (rows, rows), 0)
+    wanted = lax.rem(member - down // local_rows + members, members) * local_rows + lax.rem(down, local_rows)
+    order = (jnp.broadcast_to(token, (rows, rows)) == wanted).astype(jnp.bfloat16)
+    limit = jnp.max(jnp.where(across == wanted, off_ref[...], 0), axis=1, keepdims=True)
 
     before = lambda who: lax.fori_loop(0, who, lambda i, total: total + counts_ref[i], jnp.int32(0))
-    limit = limit_ref[:, :1]
     own_base, part_base = before(member) * PAGE, before(partner) * PAGE
 
     def column(b):
@@ -153,6 +137,18 @@
 
     lax.fori_loop(0, blocks, fill_bias, 0)
     lse[...] = jnp.zeros_like(lse)
+
+    for copy in query_copies:
+        copy.wait()
+    turned[...] = jnp.dot(order, raw[...], preferred_element_type=jnp.float32).astype(jnp.bfloat16)
+    key_copy.wait()
+
+    def absorb(g):
+        for h in range(g * hb, (g + 1) * hb):
+            lat = jnp.dot(turned[:, h * nope:(h + 1) * nope], wk[h], preferred_element_type=jnp.float32)
+            qs[h * rows:(h + 1) * rows, :latent] = lat.astype(jnp.bfloat16)
+            at = hc * nope + h * rope
+            qs[h * rows:(h + 1) * rows, latent:] = turned[:, at:at + rope]
 
     def score(g, b):
         slot = g % 2
@@ -203,7 +199,7 @@
     top = None
     for g in range(steps + 1):
         if g < steps:
-            query_copies[g].wait()
+            absorb(g)
             mx[g % 2] = jnp.full(mx.shape[1:], FLOOR, jnp.float32)
         if g == 0:
             for used, copy in tile_copies:
@@ -246,11 +242,14 @@
             attend_kernel, (members, first, hc, hh, hb, nope, rope, latent, vhead, rows, slots)
         ),
         out_shape=[jax.ShapeDtypeStruct((local_rows, packed), bf16)] * members,
-        in_specs=[pl.BlockSpec(memory_space=pltpu.SMEM), vmem] + [hbm] * (1 + LANES * PIECES + 2),
+        in_specs=[pl.BlockSpec(memory_space=pltpu.SMEM), vmem, vmem] + [hbm] * (members + LANES * PIECES + 3),
         out_specs=[vmem] * members,
         scratch_shapes=[
+            pltpu.VMEM((rows, hc * (nope + rope)), bf16),
+            pltpu.VMEM((rows, hc * (nope + rope)), bf16),
+            pltpu.VMEM((hc, nope, latent), bf16),
+            pltpu.VMEM((hc, latent, vhead), bf16),
             pltpu.VMEM((full, 2 * cols), bf16),
-            pltpu.VMEM((hc, latent, vhead), bf16),
             pltpu.VMEM((rows, most * block), jnp.float32),
             pltpu.VMEM((hc * rows, full), bf16),
             pltpu.VMEM((2, hb * rows, most * block), jnp.float32),
@@ -258,7 +257,7 @@
             pltpu.VMEM((hb * rows, 128), jnp.float32),
             pltpu.VMEM((hb * rows, latent), jnp.float32),
             pltpu.VMEM((rows, 128), jnp.float32),
-            pltpu.SemaphoreType.DMA((1 + hc // hb,)),
+            pltpu.SemaphoreType.DMA((2 + members,)),
             pltpu.SemaphoreType.DMA((most // 2,)),
             pltpu.SemaphoreType.DMA((LANES * PIECES,)),
         ],
@@ -317,16 +316,22 @@
         return lax.ppermute(x, "heads", [(i, i ^ bit) for i in range(devices)])
 
     turned = cache_tiles.T
-    packed = pl.pallas_call(
-        functools.partial(pack_kernel, (hc * nope, hc * rope, cols // LANES, chunks)),
-        out_shape=[jax.ShapeDtypeStruct((full // PIECES, cols // LANES), bf16)] * PIECES
-        + [jax.ShapeDtypeStruct((local_rows, hc * (nope + rope)), bf16)] * (GROUP * chunks),
-        in_specs=[hbm] * 3,
-        out_specs=[vmem] * (PIECES + GROUP * chunks),
-        scratch_shapes=[pltpu.SemaphoreType.DMA((PIECES + 2 * GROUP * chunks,))],
-        name="pack",
-    )(q_nope, q_rope, turned)
-    pieces, shares = packed[:PIECES], packed[PIECES:]
+    pieces = pl.pallas_call(
+        functools.partial(pack_pages_kernel, cols // LANES),
+        out_shape=[jax.ShapeDtypeStruct((full // PIECES, cols // LANES), bf16)] * PIECES,
+        in_specs=[hbm],
+        out_specs=[vmem] * PIECES,
+        scratch_shapes=[pltpu.SemaphoreType.DMA((PIECES,))],
+        name="pack_pages",
+    )(turned)
+    shares = pl.pallas_call(
+        functools.partial(pack_queries_kernel, (hc * nope, hc * rope, chunks)),
+        out_shape=[jax.ShapeDtypeStruct((local_rows, hc * (nope + rope)), bf16)] * (GROUP * chunks),
+        in_specs=[hbm] * 2,
+        out_specs=[vmem] * (GROUP * chunks),
+        scratch_shapes=[pltpu.SemaphoreType.DMA((2 * GROUP * chunks,))],
+        name="pack_queries",
+    )(q_nope, q_rope)
 
     parts = [[None] * PIECES for _ in range(LANES)]
     for p in range(PIECES):
@@ -335,32 +340,20 @@
         parts[2][p] = over_heads(parts[0][p], 1)
         parts[3][p] = over_heads(parts[1][p], 1)
     parts = [p for part in parts for p in part]
-    absorbed = []
+    queries = []
     for c in range(chunks):
         own, other = shares[c * GROUP:(c + 1) * GROUP]
         blocks = [own]
         for s in range(1, members):
             blocks.append(over_pages((own, other)[s % GROUP], s))
-        absorbed.append(pl.pallas_call(
-            functools.partial(absorb_kernel, (members, c * hc, hc, hh, nope, rope, latent)),
-            out_shape=[
-                jax.ShapeDtypeStruct((hc * rows, full), bf16),
-                jax.ShapeDtypeStruct((rows, 128), jnp.int32),
-            ],
-            in_specs=[vmem] * (2 + members) + [hbm],
-            out_specs=[vmem] * 2,
-            scratch_shapes=[
-                pltpu.VMEM((hc, nope, latent), bf16),
-                pltpu.VMEM((rows, hc * (nope + rope)), bf16),
-                pltpu.SemaphoreType.DMA(()),
-            ],
-        )(query_token[None, :], query_offsets[None, :], *blocks, absorb_keys))
+        queries.append(blocks)
 
     arrived = []
     for c in range(chunks):
         outs = attend_call(
             members, c * hc, hc, hh, hb, nope, rope, latent, vhead, rows, slots, chunks
-        )(page_counts, absorbed[c][1], absorbed[c][0], *parts, turned, absorb_values)
+        )(page_counts, query_token[None, :], query_offsets[None, :], *queries[c], *parts, turned, absorb_keys,
+          absorb_values)
         arrived.append(outs[0])
         for s in range(1, members):
             arrived.append(over_pages(outs[s], s))

time: 82 us -> 80.2 us (0.978)
  Pallas kernels: 21.5 us -> 19 us
    pallas_call x2, Pallas kernels: 7.18 us -> 3.59 us  [the longest x1 1.82 us: on_device(): pl.pallas_call(functools.partial(pack_pages_kernel, cols // LANES), out_s...]
    pallas_call x1, Pallas kernels: 11.9 us -> 13 us  [on_device(): attend_call(members, c * hc, hc, hh, hb, nope, rope, latent, vhead, rows,...]
  transfers between devices with their start and end apart: 14 -> 14, of which waited for: 7 -> 6; matrix products, arithmetic and copies ran while one was open for 0% -> 0% of each run, Pallas kernels for 6% -> 2%
where the time goes in v6:
time: 80.2 us; the launch traced here: 80 us
  waiting for transfers between devices  37.3 us (47%)
  starting transfers between devices  21.9 us (27%)
  Pallas kernels  19 us (24%)
  local copies, waits for them, and re-layouts  1.64 us (2%)
    ppermute x6, waiting for transfers between devices, over_pages(): lax.ppermute(x, 'pages', [(i, (i - s) % members) for i in range(members)])  28.9 us
    ppermute x6, starting transfers between devices, over_pages(): lax.ppermute(x, 'pages', [(i, (i - s) % members) for i in range(members)])  14.5 us
    pallas_call x1, Pallas kernels, on_device(): attend_call(members, c * hc, hc, hh, hb, nope, rope, latent, vhead, rows,...  13 us
    ppermute x2, waiting for transfers between devices, on_device(): lax.ppermute(pieces[p], 'pages', [(i, i ^ 1) for i in range(members)])  8.36 us
    ppermute x6, starting transfers between devices, over_heads(): return lax.ppermute(x, 'heads', [(i, i ^ bit) for i in range(devices)])  4.18 us
    ppermute x2, starting transfers between devices, on_device(): lax.ppermute(pieces[p], 'pages', [(i, i ^ 1) for i in range(members)])  3.2 us
    pallas_call x1, Pallas kernels, on_device(): pl.pallas_call(functools.partial(merge_kernel, (hc, vhead, members, chunk...  2.44 us
    pallas_call x1, Pallas kernels, on_device(): pl.pallas_call(functools.partial(pack_pages_kernel, cols // LANES), out_s...  1.82 us
  transfers between devices with their start and end apart: 14, of which 6 were waited for; matrix products, arithmetic and copies ran while one was open for 0% of the time, Pallas kernels for 2%

profile of v6, /device:TPU:0, one launch (start us, length us, event | category | flops | bytes accessed | tf_op | source)
XLA Modules:
  0.0 80.0 jit_solution(4316241125225943236)
XLA Ops:
  0.0 1.8 %pack_pages.1 = (bf16[288,384]{1,0:T(8,128)(2,1)}, bf16[288,384]{1,0:T(8,128)(2,1)}) custom-call(bf16[576,1536]{1,0:T(8,128)(2,1)} %bitcast.3), custom_call_target="tpu_custom_call" | custom-call | tf_op jit(solution)/shard_map/pack_pages/pallas_call | solution.py:319
  1.8 3.1 %collective-permute-start.3 = (bf16[288,384]{1,0:T(8,128)(2,1)}, bf16[288,384]{1,0:T(8,128)(2,1)S(1)}, u32[]{:S(2)}, u32[]{:S(2)}) collective-permute-start(bf16[288,384]{1,0:T(8,128)(2,1)} %get-tuple-element.15), channel_id=1, source_target_pairs={{0,4},{4,0},{8,12},{12,8},{1,5},{5,1},{9,13},{13,9},{2,6},{6,2},{1... | collective-permute-start | bytes 663560 | tf_op jit(solution)/shard_map/ppermute | solution.py:338
  4.9 0.1 collective-permute-start.4
  5.0 6.4 %collective-permute-done.3.refs_4_ = bf16[288,384]{1,0:T(8,128)(2,1)S(1)} collective-permute-done((bf16[288,384]{1,0:T(8,128)(2,1)}, bf16[288,384]{1,0:T(8,128)(2,1)S(1)}, u32[]{:S(2)}, u32[]{:S(2)}) %collective-permute-start.3) | collective-permute-done | bytes 221216 | tf_op jit(solution)/shard_map/ppermute | solution.py:338
  11.4 1.9 %collective-permute-start.5 = (bf16[288,384]{1,0:T(8,128)(2,1)S(1)}, bf16[288,384]{1,0:T(8,128)(2,1)S(1)}, u32[]{:S(2)}, u32[]{:S(2)}) collective-permute-start(bf16[288,384]{1,0:T(8,128)(2,1)S(1)} %collective-permute-done.3.refs_4_), channel_id=1, source_target_pairs={{0,2},{1,3},{2,0},{3,1},{4,6},{5,7},{6,4},{7,5},{8,10},{9,11},{10,... | collective-permute-start | bytes 663560 | tf_op jit(solution)/shard_map/ppermute | solution.py:316
  13.4 2.0 %collective-permute-done.4.refs_5_ = bf16[288,384]{1,0:T(8,128)(2,1)S(1)} collective-permute-done((bf16[288,384]{1,0:T(8,128)(2,1)}, bf16[288,384]{1,0:T(8,128)(2,1)S(1)}, u32[]{:S(2)}, u32[]{:S(2)}) %collective-permute-start.4) | collective-permute-done | bytes 221216 | tf_op jit(solution)/shard_map/ppermute | solution.py:338
  15.3 1.7 %collective-permute-start.6 = (bf16[288,384]{1,0:T(8,128)(2,1)S(1)}, bf16[288,384]{1,0:T(8,128)(2,1)S(1)}, u32[]{:S(2)}, u32[]{:S(2)}) collective-permute-start(bf16[288,384]{1,0:T(8,128)(2,1)S(1)} %collective-permute-done.4.refs_5_), channel_id=1, source_target_pairs={{0,2},{1,3},{2,0},{3,1},{4,6},{5,7},{6,4},{7,5},{8,10},{9,11},{10,... | collective-permute-start | bytes 663560 | tf_op jit(solution)/shard_map/ppermute | solution.py:316
  17.0 1.8 %pack_queries.1 = (bf16[32,3072]{1,0:T(8,128)(2,1)}, bf16[32,3072]{1,0:T(8,128)(2,1)}) custom-call(bf16[32,4096]{1,0:T(8,128)(2,1)} %nope_ref.1, bf16[32,2048]{1,0:T(8,128)(2,1)} %rope_ref.1), custom_call_target="tpu_custom_call" | custom-call | tf_op jit(solution)/shard_map/pack_queries/pallas_call | solution.py:327
  18.8 2.7 %collective-permute-start.1 = (bf16[32,3072]{1,0:T(8,128)(2,1)}, bf16[32,3072]{1,0:T(8,128)(2,1)S(1)}, u32[]{:S(2)}, u32[]{:S(2)}) collective-permute-start(bf16[32,3072]{1,0:T(8,128)(2,1)} %get-tuple-element.13.refs_0_), channel_id=1, source_target_pairs={{0,8},{4,12},{8,0},{12,4},{1,9},{5,13},{9,1},{13,5},{2,10},{6,14},... | collective-permute-start | bytes 589832 | tf_op jit(solution)/shard_map/ppermute | solution.py:313
  21.4 1.6 %collective-permute-start.2 = (bf16[32,3072]{1,0:T(8,128)(2,1)}, bf16[32,3072]{1,0:T(8,128)(2,1)S(1)}, u32[]{:S(2)}, u32[]{:S(2)}) collective-permute-start(bf16[32,3072]{1,0:T(8,128)(2,1)} %get-tuple-element.14), channel_id=1, source_target_pairs={{0,4},{4,8},{8,12},{12,0},{1,5},{5,9},{9,13},{13,1},{2,6},{6,10},{... | collective-permute-start | bytes 589832 | tf_op jit(solution)/shard_map/ppermute | solution.py:313
  23.0 10.9 %collective-permute-done.1.refs_2_ = bf16[32,3072]{1,0:T(8,128)(2,1)S(1)} collective-permute-done((bf16[32,3072]{1,0:T(8,128)(2,1)}, bf16[32,3072]{1,0:T(8,128)(2,1)S(1)}, u32[]{:S(2)}, u32[]{:S(2)}) %collective-permute-start.1) | collective-permute-done | bytes 196640 | tf_op jit(solution)/shard_map/ppermute | solution.py:313
  33.9 0.5 collective-permute-start.9
  34.4 0.1 collective-permute-start.10
  34.5 7.4 %collective-permute-done.refs_1_ = bf16[32,3072]{1,0:T(8,128)(2,1)S(1)} collective-permute-done((bf16[32,3072]{1,0:T(8,128)(2,1)}, bf16[32,3072]{1,0:T(8,128)(2,1)S(1)}, u32[]{:S(2)}, u32[]{:S(2)}) %collective-permute-start) | collective-permute-done | bytes 196640 | tf_op jit(solution)/shard_map/ppermute | solution.py:313
  42.1 0.6 copy-done.13
  42.6 0.1 copy-done.7
  42.9 0.1 copy-done.10
  43.0 13.0 %shard_map.82 = (bf16[32,2176]{1,0:T(8,128)(2,1)}, bf16[32,2176]{1,0:T(8,128)(2,1)}, bf16[32,2176]{1,0:T(8,128)(2,1)}, bf16[32,2176]{1,0:T(8,128)(2,1)}) custom-call(s32[4]{0:T(128)} %counts_ref.1, s32[1,128]{1,0:T(1,128)} %bitcast.5, s32[1,128]{1,0:T(1,128)} %bitcast.6, bf16[32,3072]{1,0:T(8,128)(2,1)} %get-tuple-element.13.refs_0_, ...), custom_call_target="tpu_custom_call" | custom-call | flops 8000000000 | bytes 8000000 | tf_op jit(solution)/shard_map/pallas_call | solution.py:353
  55.9 9.1 %collective-permute-start.11 = (bf16[32,2176]{1,0:T(8,128)(2,1)}, bf16[32,2176]{1,0:T(8,128)(2,1)S(1)}, u32[]{:S(2)}, u32[]{:S(2)}) collective-permute-start(bf16[32,2176]{1,0:T(8,128)(2,1)} %get-tuple-element.18), channel_id=1, source_target_pairs={{0,12},{4,0},{8,4},{12,8},{1,13},{5,1},{9,5},{13,9},{2,14},{6,2},{... | collective-permute-start | bytes 417800 | tf_op jit(solution)/shard_map/ppermute | solution.py:313
  65.0 1.2 %collective-permute-start.13 = (bf16[32,2176]{1,0:T(8,128)(2,1)}, bf16[32,2176]{1,0:T(8,128)(2,1)S(1)}, u32[]{:S(2)}, u32[]{:S(2)}) collective-permute-start(bf16[32,2176]{1,0:T(8,128)(2,1)} %get-tuple-element.20), channel_id=1, source_target_pairs={{0,4},{4,8},{8,12},{12,0},{1,5},{5,9},{9,13},{13,1},{2,6},{6,10},{... | collective-permute-start | bytes 417800 | tf_op jit(solution)/shard_map/ppermute | solution.py:313
  66.2 3.2 %collective-permute-done.11.refs_1_ = bf16[32,2176]{1,0:T(8,128)(2,1)S(1)} collective-permute-done((bf16[32,2176]{1,0:T(8,128)(2,1)}, bf16[32,2176]{1,0:T(8,128)(2,1)S(1)}, u32[]{:S(2)}, u32[]{:S(2)}) %collective-permute-start.11) | collective-permute-done | bytes 139296 | tf_op jit(solution)/shard_map/ppermute | solution.py:313
  69.5 7.4 %collective-permute-done.12.refs_2_ = bf16[32,2176]{1,0:T(8,128)(2,1)S(1)} collective-permute-done((bf16[32,2176]{1,0:T(8,128)(2,1)}, bf16[32,2176]{1,0:T(8,128)(2,1)S(1)}, u32[]{:S(2)}, u32[]{:S(2)}) %collective-permute-start.12) | collective-permute-done | bytes 139296 | tf_op jit(solution)/shard_map/ppermute | solution.py:313
  76.8 0.6 copy-done.1
  77.5 2.4 %merge.1 = bf16[32,4096]{1,0:T(8,128)(2,1)} custom-call(bf16[32,2176]{1,0:T(8,128)(2,1)} %get-tuple-element.17.refs_0_, bf16[32,2176]{1,0:T(8,128)(2,1)} %copy-done, bf16[32,2176]{1,0:T(8,128)(2,1)} %copy-done.1, bf16[32,2176]{1,0:T(8,128)(2,1)} %copy-done.2), custom_call_target="tpu_custom_call" | custom-call | tf_op jit(solution)/shard_map/merge/pallas_call | solution.py:361
  (36 shorter events, 0.3 us)
Async XLA Ops:
  1.8 9.6 %collective-permute-start.3 = (bf16[288,384]{1,0:T(8,128)(2,1)}, bf16[288,384]{1,0:T(8,128)(2,1)S(1)}, u32[]{:S(2)}, u32[]{:S(2)}) collective-permute-start(bf16[288,384]{1,0:T(8,128)(2,1)} %get-tuple-element.15), channel_id=1, source_target_pairs={{0,4},{4,0},{8,12},{12,8},{1,5},{5,1},{9,13},{13,9},{2,6},{6,2},{1... | collective-permute-start | bytes 663560 | tf_op jit(solution)/shard_map/ppermute | solution.py:338
  4.9 10.4 %collective-permute-start.4 = (bf16[288,384]{1,0:T(8,128)(2,1)}, bf16[288,384]{1,0:T(8,128)(2,1)S(1)}, u32[]{:S(2)}, u32[]{:S(2)}) collective-permute-start(bf16[288,384]{1,0:T(8,128)(2,1)} %get-tuple-element.16), channel_id=1, source_target_pairs={{0,4},{4,0},{8,12},{12,8},{1,5},{5,1},{9,13},{13,9},{2,6},{6,2},{1... | collective-permute-start | bytes 663560 | tf_op jit(solution)/shard_map/ppermute | solution.py:338
  11.4 30.6 %copy-start.3 = (bf16[288,384]{1,0:T(8,128)(2,1)}, bf16[288,384]{1,0:T(8,128)(2,1)S(1)}, u32[]{:S(2)}) copy-start(bf16[288,384]{1,0:T(8,128)(2,1)S(1)} %collective-permute-done.3.refs_4_) | copy-start | bytes 663556
  11.4 22.4 %collective-permute-start.5 = (bf16[288,384]{1,0:T(8,128)(2,1)S(1)}, bf16[288,384]{1,0:T(8,128)(2,1)S(1)}, u32[]{:S(2)}, u32[]{:S(2)}) collective-permute-start(bf16[288,384]{1,0:T(8,128)(2,1)S(1)} %collective-permute-done.3.refs_4_), channel_id=1, source_target_pairs={{0,2},{1,3},{2,0},{3,1},{4,6},{5,7},{6,4},{7,5},{8,10},{9,11},{10,... | collective-permute-start | bytes 663560 | tf_op jit(solution)/shard_map/ppermute | solution.py:316
  15.3 26.7 %copy-start.4 = (bf16[288,384]{1,0:T(8,128)(2,1)}, bf16[288,384]{1,0:T(8,128)(2,1)S(1)}, u32[]{:S(2)}) copy-start(bf16[288,384]{1,0:T(8,128)(2,1)S(1)} %collective-permute-done.4.refs_5_) | copy-start | bytes 663556
  15.3 19.1 %collective-permute-start.6 = (bf16[288,384]{1,0:T(8,128)(2,1)S(1)}, bf16[288,384]{1,0:T(8,128)(2,1)S(1)}, u32[]{:S(2)}, u32[]{:S(2)}) collective-permute-start(bf16[288,384]{1,0:T(8,128)(2,1)S(1)} %collective-permute-done.4.refs_5_), channel_id=1, source_target_pairs={{0,2},{1,3},{2,0},{3,1},{4,6},{5,7},{6,4},{7,5},{8,10},{9,11},{10,... | collective-permute-start | bytes 663560 | tf_op jit(solution)/shard_map/ppermute | solution.py:316
  18.8 15.1 %collective-permute-start.1 = (bf16[32,3072]{1,0:T(8,128)(2,1)}, bf16[32,3072]{1,0:T(8,128)(2,1)S(1)}, u32[]{:S(2)}, u32[]{:S(2)}) collective-permute-start(bf16[32,3072]{1,0:T(8,128)(2,1)} %get-tuple-element.13.refs_0_), channel_id=1, source_target_pairs={{0,8},{4,12},{8,0},{12,4},{1,9},{5,13},{9,1},{13,5},{2,10},{6,14},... | collective-permute-start | bytes 589832 | tf_op jit(solution)/shard_map/ppermute | solution.py:313
  21.4 13.1 %collective-permute-start.2 = (bf16[32,3072]{1,0:T(8,128)(2,1)}, bf16[32,3072]{1,0:T(8,128)(2,1)S(1)}, u32[]{:S(2)}, u32[]{:S(2)}) collective-permute-start(bf16[32,3072]{1,0:T(8,128)(2,1)} %get-tuple-element.14), channel_id=1, source_target_pairs={{0,4},{4,8},{8,12},{12,0},{1,5},{5,9},{9,13},{13,1},{2,6},{6,10},{... | collective-permute-start | bytes 589832 | tf_op jit(solution)/shard_map/ppermute | solution.py:313
  23.0 18.9 %collective-permute-start.7 = (bf16[288,384]{1,0:T(8,128)(2,1)S(1)}, bf16[288,384]{1,0:T(8,128)(2,1)S(1)}, u32[]{:S(2)}, u32[]{:S(2)}) collective-permute-start(bf16[288,384]{1,0:T(8,128)(2,1)S(1)} %collective-permute-done.3.refs_4_), channel_id=1, source_target_pairs={{0,1},{1,0},{2,3},{3,2},{4,5},{5,4},{6,7},{7,6},{8,9},{9,8},{10,11... | collective-permute-start | bytes 663560 | tf_op jit(solution)/shard_map/ppermute | solution.py:316
  33.9 8.1 %copy-start.11 = (bf16[32,3072]{1,0:T(8,128)(2,1)}, bf16[32,3072]{1,0:T(8,128)(2,1)S(1)}, u32[]{:S(2)}) copy-start(bf16[32,3072]{1,0:T(8,128)(2,1)S(1)} %collective-permute-done.1.refs_2_) | copy-start | bytes 589828
  33.9 8.1 %collective-permute-start.8 = (bf16[288,384]{1,0:T(8,128)(2,1)S(1)}, bf16[288,384]{1,0:T(8,128)(2,1)S(1)}, u32[]{:S(2)}, u32[]{:S(2)}) collective-permute-start(bf16[288,384]{1,0:T(8,128)(2,1)S(1)} %collective-permute-done.4.refs_5_), channel_id=1, source_target_pairs={{0,1},{1,0},{2,3},{3,2},{4,5},{5,4},{6,7},{7,6},{8,9},{9,8},{10,11... | collective-permute-start | bytes 663560 | tf_op jit(solution)/shard_map/ppermute | solution.py:316
  33.9 8.1 %copy-start.5 = (bf16[288,384]{1,0:T(8,128)(2,1)}, bf16[288,384]{1,0:T(8,128)(2,1)S(1)}, u32[]{:S(2)}) copy-start(bf16[288,384]{1,0:T(8,128)(2,1)S(1)} %collective-permute-done.5.refs_6_) | copy-start | bytes 663556
  33.9 8.1 %collective-permute-start.9 = (bf16[288,384]{1,0:T(8,128)(2,1)S(1)}, bf16[288,384]{1,0:T(8,128)(2,1)S(1)}, u32[]{:S(2)}, u32[]{:S(2)}) collective-permute-start(bf16[288,384]{1,0:T(8,128)(2,1)S(1)} %collective-permute-done.5.refs_6_), channel_id=1, source_target_pairs={{0,1},{1,0},{2,3},{3,2},{4,5},{5,4},{6,7},{7,6},{8,9},{9,8},{10,11... | collective-permute-start | bytes 663560 | tf_op jit(solution)/shard_map/ppermute | solution.py:316
  34.4 7.6 %copy-start.6 = (bf16[288,384]{1,0:T(8,128)(2,1)}, bf16[288,384]{1,0:T(8,128)(2,1)S(1)}, u32[]{:S(2)}) copy-start(bf16[288,384]{1,0:T(8,128)(2,1)S(1)} %collective-permute-done.6.refs_7_) | copy-start | bytes 663556
  34.4 7.6 %collective-permute-start.10 = (bf16[288,384]{1,0:T(8,128)(2,1)S(1)}, bf16[288,384]{1,0:T(8,128)(2,1)S(1)}, u32[]{:S(2)}, u32[]{:S(2)}) collective-permute-start(bf16[288,384]{1,0:T(8,128)(2,1)S(1)} %collective-permute-done.6.refs_7_), channel_id=1, source_target_pairs={{0,1},{1,0},{2,3},{3,2},{4,5},{5,4},{6,7},{7,6},{8,9},{9,8},{10,11... | collective-permute-start | bytes 663560 | tf_op jit(solution)/shard_map/ppermute | solution.py:316
  34.5 7.6 %copy-start.12 = (bf16[32,3072]{1,0:T(8,128)(2,1)}, bf16[32,3072]{1,0:T(8,128)(2,1)S(1)}, u32[]{:S(2)}) copy-start(bf16[32,3072]{1,0:T(8,128)(2,1)S(1)} %collective-permute-done.2.refs_3_) | copy-start | bytes 589828
  34.5 7.4 %collective-permute-start = (bf16[32,3072]{1,0:T(8,128)(2,1)}, bf16[32,3072]{1,0:T(8,128)(2,1)S(1)}, u32[]{:S(2)}, u32[]{:S(2)}) collective-permute-start(bf16[32,3072]{1,0:T(8,128)(2,1)} %get-tuple-element.14), channel_id=1, source_target_pairs={{0,12},{4,0},{8,4},{12,8},{1,13},{5,1},{9,5},{13,9},{2,14},{6,2},{... | collective-permute-start | bytes 589832 | tf_op jit(solution)/shard_map/ppermute | solution.py:313
  41.9 0.8 %copy-start.8 = (bf16[288,384]{1,0:T(8,128)(2,1)}, bf16[288,384]{1,0:T(8,128)(2,1)S(1)}, u32[]{:S(2)}) copy-start(bf16[288,384]{1,0:T(8,128)(2,1)S(1)} %collective-permute-done.8.refs_9_) | copy-start | bytes 663556
  42.0 0.9 %copy-start.9 = (bf16[288,384]{1,0:T(8,128)(2,1)}, bf16[288,384]{1,0:T(8,128)(2,1)S(1)}, u32[]{:S(2)}) copy-start(bf16[288,384]{1,0:T(8,128)(2,1)S(1)} %collective-permute-done.9.refs_10_) | copy-start | bytes 663556
  42.0 1.0 %copy-start.10 = (bf16[288,384]{1,0:T(8,128)(2,1)}, bf16[288,384]{1,0:T(8,128)(2,1)S(1)}, u32[]{:S(2)}) copy-start(bf16[288,384]{1,0:T(8,128)(2,1)S(1)} %collective-permute-done.10.refs_11_) | copy-start | bytes 663556
  55.9 13.5 %collective-permute-start.11 = (bf16[32,2176]{1,0:T(8,128)(2,1)}, bf16[32,2176]{1,0:T(8,128)(2,1)S(1)}, u32[]{:S(2)}, u32[]{:S(2)}) collective-permute-start(bf16[32,2176]{1,0:T(8,128)(2,1)} %get-tuple-element.18), channel_id=1, source_target_pairs={{0,12},{4,0},{8,4},{12,8},{1,13},{5,1},{9,5},{13,9},{2,14},{6,2},{... | collective-permute-start | bytes 417800 | tf_op jit(solution)/shard_map/ppermute | solution.py:313
  65.0 11.8 %collective-permute-start.12 = (bf16[32,2176]{1,0:T(8,128)(2,1)}, bf16[32,2176]{1,0:T(8,128)(2,1)S(1)}, u32[]{:S(2)}, u32[]{:S(2)}) collective-permute-start(bf16[32,2176]{1,0:T(8,128)(2,1)} %get-tuple-element.19), channel_id=1, source_target_pairs={{0,8},{4,12},{8,0},{12,4},{1,9},{5,13},{9,1},{13,5},{2,10},{6,14},... | collective-permute-start | bytes 417800 | tf_op jit(solution)/shard_map/ppermute | solution.py:313
  65.0 11.8 %collective-permute-start.13 = (bf16[32,2176]{1,0:T(8,128)(2,1)}, bf16[32,2176]{1,0:T(8,128)(2,1)S(1)}, u32[]{:S(2)}, u32[]{:S(2)}) collective-permute-start(bf16[32,2176]{1,0:T(8,128)(2,1)} %get-tuple-element.20), channel_id=1, source_target_pairs={{0,4},{4,8},{8,12},{12,0},{1,5},{5,9},{9,13},{13,1},{2,6},{6,10},{... | collective-permute-start | bytes 417800 | tf_op jit(solution)/shard_map/ppermute | solution.py:313
  69.5 7.4 %copy-start = (bf16[32,2176]{1,0:T(8,128)(2,1)}, bf16[32,2176]{1,0:T(8,128)(2,1)S(1)}, u32[]{:S(2)}) copy-start(bf16[32,2176]{1,0:T(8,128)(2,1)S(1)} %collective-permute-done.11.refs_1_) | copy-start | bytes 417796
  (4 other events, 2.8 us)

commit v7 on v6

v7 whole, which is shorter than its diff:
```python
import functools

import jax
import jax.numpy as jnp
from jax import lax
from jax.experimental import pallas as pl
from jax.experimental.pallas import tpu as pltpu
from jax.sharding import PartitionSpec as P


PAGE = 64
GROUP = 2
LANES = 4
BLOCK_PAGES = 4
PIECES = 2
HALVES = 2


FLOOR = -1e30
FAR = 2**30
LOG2E = 1.4426950408889634


def pack_pages_kernel(quarter_cols, cache_ref, *refs):
    outs, sems = refs[:-1], refs[-1]
    lane = lax.axis_index("heads") % LANES
    depth = cache_ref.shape[0] // PIECES
    at = pl.ds(pl.multiple_of(lane * quarter_cols, 128), quarter_cols)
    copies = [
        pltpu.make_async_copy(cache_ref.at[pl.ds(p * depth, depth), at], outs[p], sems.at[p]) for p in range(PIECES)
    ]
    for c in copies:
        c.start()
    for c in copies:
        c.wait()


def pack_queries_kernel(dims, nope_ref, rope_ref, *refs):
    nope_width, rope_width = dims
    outs, sems = refs[:-1], refs[-1]
    mine = lax.axis_index("pages") % GROUP
    copies = []
    for e in range(GROUP):
        which = (mine + e) % GROUP
        for ref, width, at in ((nope_ref, nope_width, 0), (rope_ref, rope_width, nope_width)):
            copies.append(
                pltpu.make_async_copy(
                    ref.at[:, pl.ds(pl.multiple_of(which * width, 128), width)],
                    outs[e].at[:, pl.ds(at, width)],
                    sems.at[len(copies)],
                )
            )
    for c in copies:
        c.start()
    for c in copies:
        c.wait()


def attend_kernel(dims, counts_ref, tok_ref, off_ref, *refs):
    members, hh, nope, rope, latent, vhead, rows, slots = dims
    q_refs, refs = refs[:members], refs[members:]
    part_refs, refs = refs[:LANES * PIECES], refs[LANES * PIECES:]
    own_ref, keys_hbm, values_hbm = refs[:3]
    out_refs, refs = refs[3:3 + members], refs[3 + members:]
    raw, turned, wk, wv, tiles, bias, qs, sbuf, mx, den, acc, sums, flat, sems, own_sems, part_sems = refs
    local_rows = rows // members
    block = BLOCK_PAGES * PAGE
    cols = slots * PAGE
    quarter_cols = cols // LANES
    depth = (latent + rope) // PIECES
    scale2 = (nope + rope) ** (-0.5) * LOG2E
    half = rows // HALVES
    group_rows = hh * half
    member = lax.axis_index("pages")
    lane_id = lax.axis_index("heads") % LANES
    partner = member ^ 1
    mine = member % GROUP
    own_live, part_live = counts_ref[member], counts_ref[partner]
    own_blocks = (own_live + BLOCK_PAGES - 1) // BLOCK_PAGES
    part_blocks = (part_live + BLOCK_PAGES - 1) // BLOCK_PAGES

    query_copies = [
        pltpu.make_async_copy(q, raw.at[pl.ds(s * local_rows, local_rows)], sems.at[2 + s])
        for s, q in enumerate(q_refs)
    ]
    key_copy = pltpu.make_async_copy(keys_hbm.at[pl.ds(mine * hh, hh)], wk, sems.at[0])
    value_copy = pltpu.make_async_copy(values_hbm.at[pl.ds(mine * hh, hh)], wv, sems.at[1])
    tile_copies = []
    for b in range(-(-cols // block)):
        at = pl.ds(b * block, min(block, cols - b * block))
        tile_copies.append((b < own_blocks, pltpu.make_async_copy(own_ref.at[:, at], tiles.at[:, at], own_sems.at[b])))
    for i, flip in enumerate((0, 2, 1, 3)):
        quarter = lane_id ^ flip
        at = pl.multiple_of(cols + quarter * quarter_cols, 128)
        for p in range(PIECES):
            tile_copies.append((
                quarter * quarter_cols < part_blocks * block,
                pltpu.make_async_copy(
                    part_refs[i * PIECES + p],
                    tiles.at[pl.ds(p * depth, depth), pl.ds(at, quarter_cols)],
                    part_sems.at[i * PIECES + p],
                ),
            ))
    for copy in query_copies + [key_copy]:
        copy.start()
    for used, copy in tile_copies:
        pl.when(used)(copy.start)
    value_copy.start()

    across = lax.broadcasted_iota(jnp.int32, (rows, rows), 1)
    down = lax.broadcasted_iota(jnp.int32, (rows, rows), 0)
    off = jnp.broadcast_to(off_ref[...], (rows, rows))
    off_down = jnp.max(jnp.where(across == down, off, 0), axis=1, keepdims=True)
    rank = jnp.sum(
        jnp.where((off_down < off) | ((off_down == off) & (down < across)), 1.0, 0.0), axis=0, keepdims=True
    ).astype(jnp.int32)
    rank_down = jnp.max(jnp.where(across == down, rank, 0), axis=1, keepdims=True)
    token = pltpu.roll(
        jnp.broadcast_to(tok_ref[...], (8, rows)), lax.rem(rows - member * local_rows, rows), axis=1
    )[:1]
    row_rank = jnp.max(jnp.where(down == token, rank_down, 0), axis=0, keepdims=True)
    order = (row_rank == down).astype(jnp.bfloat16)
    limit = jnp.max(jnp.where(rank == down, off, 0), axis=1, keepdims=True)
    wanted = lax.rem(member - down // local_rows + members, members) * local_rows + lax.rem(down, local_rows)
    leave = (jnp.max(jnp.where(across == wanted, rank, 0), axis=1, keepdims=True) == across).astype(jnp.bfloat16)

    before = lambda who: lax.fori_loop(0, who, lambda i, total: total + counts_ref[i], jnp.int32(0))
    own_base, part_base = before(member) * PAGE, before(partner) * PAGE

    def in_reach(g):
        last = jnp.max(limit[g * half:(g + 1) * half])
        own = jnp.clip((last - own_base + block - 1) // block, 0, own_blocks)
        return own, own + jnp.clip((last - part_base + block - 1) // block, 0, part_blocks)

    reach = [in_reach(g) for g in range(HALVES)]

    def place(g, b):
        own, _ = reach[g]
        return pl.multiple_of(jnp.where(b < own, b * block, cols + (b - own) * block), 128)

    spot = lax.broadcasted_iota(jnp.int32, (1, block), 1)

    def fill_bias(b, carry):
        at = place(HALVES - 1, b)
        own = at < cols
        inside = jnp.where(own, at, at - cols) + spot
        live = jnp.where(own, own_live, part_live) * PAGE
        positions = jnp.where(inside < live, jnp.where(own, own_base, part_base) + inside, FAR)
        bias[:, pl.ds(at, block)] = jnp.where(positions < limit, 0.0, FLOOR)
        return carry

    lax.fori_loop(0, reach[-1][1], fill_bias, 0)
    for copy in query_copies:
        copy.wait()
    turned[...] = jnp.dot(order, raw[...], preferred_element_type=jnp.float32).astype(jnp.bfloat16)
    key_copy.wait()
    for h in range(hh):
        lat = jnp.dot(turned[:, h * nope:(h + 1) * nope], wk[h], preferred_element_type=jnp.float32)
        lat = lat.astype(jnp.bfloat16)
        at = hh * nope + h * rope
        for g in range(HALVES):
            to = slice(g * group_rows + h * half, g * group_rows + (h + 1) * half)
            qs[to, :latent] = lat[g * half:(g + 1) * half]
            qs[to, latent:] = turned[g * half:(g + 1) * half, at:at + rope]
    mx[...] = jnp.full(mx.shape, FLOOR, jnp.float32)
    for used, copy in tile_copies:
        pl.when(used)(copy.wait)

    def score(g, b):
        at = place(g, b)
        scores = jnp.dot(
            qs[g * group_rows:(g + 1) * group_rows], tiles[:, pl.ds(at, block)], preferred_element_type=jnp.float32
        )
        shut = bias[g * half:(g + 1) * half, pl.ds(at, block)]
        for h in range(hh):
            part = slice(h * half, (h + 1) * half)
            value = scores[part] + shut
            sbuf[g, part, pl.ds(pl.multiple_of(b * block, 128), block)] = value
            top = functools.reduce(jnp.maximum, [value[:, i:i + 128] for i in range(0, block, 128)])
            mx[g, part] = jnp.maximum(mx[g, part], top)

    def gather(g, b, top):
        weights = jnp.exp2((sbuf[g, :, pl.ds(pl.multiple_of(b * block, 128), block)] - top) * scale2)
        den[...] += functools.reduce(jnp.add, [weights[:, i:i + 128] for i in range(0, block, 128)])
        acc[...] += lax.dot_general(
            weights.astype(jnp.bfloat16),
            tiles[:latent, pl.ds(place(g, b), block)],
            (((1,), (1,)), ((), ())),
            preferred_element_type=jnp.float32,
        )

    stats = []

    def close(g, top):
        total = jnp.sum(den[...], axis=1, keepdims=True)
        seen = top > 0.5 * FLOOR
        total = jnp.where(seen, total, 1.0)
        stats.append((jnp.where(seen, 1.0 / total, 0.0), jnp.where(seen, top * scale2 + jnp.log2(total), FLOOR)))
        for h in range(hh):
            sums[h, g * half:(g + 1) * half] = acc[h * half:(h + 1) * half].astype(jnp.bfloat16)

    def each(low, high, *steps):
        def body(b, carry):
            for step in steps:
                step(b)
            return carry

        lax.fori_loop(low, high, body, 0)

    each(0, reach[0][1], lambda b: score(0, b))
    for g in range(HALVES):
        top = jnp.max(mx[g], axis=1, keepdims=True)
        den[...] = jnp.zeros_like(den)
        acc[...] = jnp.zeros_like(acc)
        if g + 1 < HALVES:
            each(0, reach[g][1], lambda b: score(g + 1, b), lambda b: gather(g, b, top))
            each(reach[g][1], reach[g + 1][1], lambda b: score(g + 1, b))
        else:
            each(0, reach[g][1], lambda b: gather(g, b, top))
        close(g, top)

    value_copy.wait()
    lane = lax.broadcasted_iota(jnp.int32, (rows, 128), 1)
    logs = jnp.zeros((rows, 128), jnp.float32)
    for h in range(hh):
        part = slice(h * half, (h + 1) * half)
        value = jnp.dot(sums[h], wv[h], preferred_element_type=jnp.float32)
        value = value * jnp.concatenate([share[part] for share, _ in stats], axis=0)
        flat[:, h * vhead:(h + 1) * vhead] = value.astype(jnp.bfloat16)
        full = jnp.concatenate([log[part] for _, log in stats], axis=0)
        high = full.astype(jnp.bfloat16).astype(jnp.float32)
        middle = (full - high).astype(jnp.bfloat16).astype(jnp.float32)
        low = full - high - middle
        logs = jnp.where(lane == h, high, jnp.where(lane == hh + h, middle, jnp.where(lane == 2 * hh + h, low, logs)))
    flat[:, hh * vhead:] = logs.astype(jnp.bfloat16)
    ordered = jnp.dot(leave, flat[...], preferred_element_type=jnp.float32).astype(jnp.bfloat16)
    for s in range(members):
        out_refs[s][...] = ordered[s * local_rows:(s + 1) * local_rows]


def attend_call(members, hh, nope, rope, latent, vhead, rows, slots):
    hbm = pl.BlockSpec(memory_space=pltpu.HBM)
    vmem = pl.BlockSpec(memory_space=pltpu.VMEM)
    bf16, f32 = jnp.bfloat16, jnp.float32
    full = latent + rope
    cols = slots * PAGE
    local_rows = rows // members
    packed = hh * vhead + 128
    block = BLOCK_PAGES * PAGE
    own_blocks = -(-cols // block)
    group_rows = hh * (rows // HALVES)
    return pl.pallas_call(
        functools.partial(attend_kernel, (members, hh, nope, rope, latent, vhead, rows, slots)),
        out_shape=[jax.ShapeDtypeStruct((local_rows, packed), bf16)] * members,
        in_specs=[pl.BlockSpec(memory_space=pltpu.SMEM), vmem, vmem] + [hbm] * (members + LANES * PIECES + 3),
        out_specs=[vmem] * members,
        scratch_shapes=[
            pltpu.VMEM((rows, hh * (nope + rope)), bf16),
            pltpu.VMEM((rows, hh * (nope + rope)), bf16),
            pltpu.VMEM((hh, nope, latent), bf16),
            pltpu.VMEM((hh, latent, vhead), bf16),
            pltpu.VMEM((full, 2 * cols), bf16),
            pltpu.VMEM((rows, 2 * cols), f32),
            pltpu.VMEM((HALVES * group_rows, full), bf16),
            pltpu.VMEM((HALVES, group_rows, 2 * own_blocks * block), f32),
            pltpu.VMEM((HALVES, group_rows, 128), f32),
            pltpu.VMEM((group_rows, 128), f32),
            pltpu.VMEM((group_rows, latent), f32),
            pltpu.VMEM((hh, rows, latent), bf16),
            pltpu.VMEM((rows, packed), bf16),
            pltpu.SemaphoreType.DMA((2 + members,)),
            pltpu.SemaphoreType.DMA((own_blocks,)),
            pltpu.SemaphoreType.DMA((LANES * PIECES,)),
        ],
        compiler_params=pltpu.CompilerParams(vmem_limit_bytes=58 << 20),
        cost_estimate=pl.CostEstimate(flops=8 * 10**9, bytes_accessed=8 * 10**6, transcendentals=0),
        name="attend",
    )


def merge_kernel(dims, *refs):
    hh, vhead, members = dims
    out_ref = refs[-1]
    mine = lax.axis_index("pages") % GROUP
    for parity in range(GROUP):
        parts = [refs[s] for s in range(members) if s % GROUP == parity]
        logs = []
        for b in parts:
            packed = b[:, hh * vhead:].astype(jnp.float32)
            logs.append(packed[:, :hh] + packed[:, hh:2 * hh] + packed[:, 2 * hh:3 * hh])
        top = functools.reduce(jnp.maximum, logs)
        weights = [jnp.exp2(v - top) for v in logs]
        total = functools.reduce(jnp.add, weights)
        weights = [w / total for w in weights]
        base = lax.rem(mine + parity, GROUP) * (hh * vhead)
        for h in range(hh):
            cols = slice(h * vhead, (h + 1) * vhead)
            value = functools.reduce(
                jnp.add, [w[:, h:h + 1] * b[:, cols].astype(jnp.float32) for w, b in zip(weights, parts)]
            )
            out_ref[:, pl.ds(pl.multiple_of(base + h * vhead, 128), vhead)] = value.astype(jnp.bfloat16)


def on_device(
    q_nope, q_rope, cache_tiles, absorb_keys, absorb_values, page_counts, query_token, query_offsets, members, devices
):
    heads_here, nope, latent = absorb_keys.shape
    vhead = absorb_values.shape[2]
    local_rows = q_nope.shape[0]
    rope = q_rope.shape[1] // heads_here
    full = cache_tiles.shape[1]
    slots = cache_tiles.shape[0] // PAGE
    cols = slots * PAGE
    rows = local_rows * members
    hh = heads_here // GROUP
    hbm = pl.BlockSpec(memory_space=pltpu.HBM)
    vmem = pl.BlockSpec(memory_space=pltpu.VMEM)
    bf16 = jnp.bfloat16

    def over_pages(x, s):
        return lax.ppermute(x, "pages", [(i, (i - s) % members) for i in range(members)])

    def over_heads(x, bit):
        return lax.ppermute(x, "heads", [(i, i ^ bit) for i in range(devices)])

    turned = cache_tiles.T
    pieces = pl.pallas_call(
        functools.partial(pack_pages_kernel, cols // LANES),
        out_shape=[jax.ShapeDtypeStruct((full // PIECES, cols // LANES), bf16)] * PIECES,
        in_specs=[hbm],
        out_specs=[vmem] * PIECES,
        scratch_shapes=[pltpu.SemaphoreType.DMA((PIECES,))],
        name="pack_pages",
    )(turned)
    shares = pl.pallas_call(
        functools.partial(pack_queries_kernel, (hh * nope, hh * rope)),
        out_shape=[jax.ShapeDtypeStruct((local_rows, hh * (nope + rope)), bf16)] * GROUP,
        in_specs=[hbm] * 2,
        out_specs=[vmem] * GROUP,
        scratch_shapes=[pltpu.SemaphoreType.DMA((2 * GROUP,))],
        name="pack_queries",
    )(q_nope, q_rope)

    parts = [[None] * PIECES for _ in range(LANES)]
    for p in range(PIECES):
        parts[0][p] = lax.ppermute(pieces[p], "pages", [(i, i ^ 1) for i in range(members)])
        parts[1][p] = over_heads(parts[0][p], 2)
        parts[2][p] = over_heads(parts[0][p], 1)
        parts[3][p] = over_heads(parts[1][p], 1)
    parts = [p for part in parts for p in part]
    queries = [shares[0]]
    for s in range(1, members):
        queries.append(over_pages(shares[s % GROUP], s))
    outs = attend_call(members, hh, nope, rope, latent, vhead, rows, slots)(
        page_counts, query_token[None, :], query_offsets[None, :], *queries, *parts, turned, absorb_keys, absorb_values
    )
    arrived = [outs[0]]
    for s in range(1, members):
        arrived.append(over_pages(outs[s], s))

    return pl.pallas_call(
        functools.partial(merge_kernel, (hh, vhead, members)),
        out_shape=jax.ShapeDtypeStruct((local_rows, heads_here * vhead), bf16),
        in_specs=[vmem] * members,
        out_specs=vmem,
        name="merge",
    )(*arrived)


def solution(mesh):
    in_specs = (
        P(("groups", "pages"), "heads"),
        P(("groups", "pages"), "heads"),
        P(("groups", "pages"), None),
        P("heads", None, None),
        P("heads", None, None),
        P("groups"),
        P("groups"),
        P("groups"),
    )
    body = functools.partial(on_device, members=mesh.shape["pages"], devices=mesh.shape["heads"])
    return jax.shard_map(
        body, mesh=mesh, in_specs=in_specs, out_specs=P(("groups", "pages"), "heads"), check_vma=False
    )
```

time: 80.2 us -> 78.8 us (0.983)
  Pallas kernels: 19 us -> 16.8 us
    pallas_call x3, Pallas kernels: 17.2 us -> 15 us  [the longest x1 10.7 us: on_device(): attend_call(members, hh, nope, rope, latent, vhead, rows, slots)]
where the time goes in v7:
time: 78.8 us; the launch traced here: 78.4 us
  waiting for transfers between devices  37.2 us (47%)
  starting transfers between devices  22.6 us (29%)
  Pallas kernels  16.8 us (21%)
  local copies, waits for them, and re-layouts  1.64 us (2%)
    ppermute x6, waiting for transfers between devices, over_pages(): lax.ppermute(x, 'pages', [(i, (i - s) % members) for i in range(members)])  28.8 us
    ppermute x6, starting transfers between devices, over_pages(): lax.ppermute(x, 'pages', [(i, (i - s) % members) for i in range(members)])  15.2 us
    pallas_call x1, Pallas kernels, on_device(): attend_call(members, hh, nope, rope, latent, vhead, rows, slots)  10.7 us
    ppermute x2, waiting for transfers between devices, on_device(): lax.ppermute(pieces[p], 'pages', [(i, i ^ 1) for i in range(members)])  8.36 us
    ppermute x6, starting transfers between devices, over_heads(): return lax.ppermute(x, 'heads', [(i, i ^ bit) for i in range(devices)])  4.18 us
    ppermute x2, starting transfers between devices, on_device(): lax.ppermute(pieces[p], 'pages', [(i, i ^ 1) for i in range(members)])  3.2 us
    pallas_call x1, Pallas kernels, on_device(): pl.pallas_call(functools.partial(merge_kernel, (hh, vhead, members)), out...  2.44 us
    pallas_call x1, Pallas kernels, on_device(): pl.pallas_call(functools.partial(pack_pages_kernel, cols // LANES), out_s...  1.82 us
  transfers between devices with their start and end apart: 14, of which 6 were waited for; matrix products, arithmetic and copies ran while one was open for 0% of the time, Pallas kernels for 2%

profile of v7, /device:TPU:0, one launch (start us, length us, event | category | flops | bytes accessed | tf_op | source)
XLA Modules:
  0.0 78.4 jit_solution(8586762975703526936)
XLA Ops:
  0.0 1.8 %pack_pages.1 = (bf16[288,384]{1,0:T(8,128)(2,1)}, bf16[288,384]{1,0:T(8,128)(2,1)}) custom-call(bf16[576,1536]{1,0:T(8,128)(2,1)} %bitcast.3), custom_call_target="tpu_custom_call" | custom-call | tf_op jit(solution)/shard_map/pack_pages/pallas_call | solution.py:327
  1.8 3.1 %collective-permute-start.3 = (bf16[288,384]{1,0:T(8,128)(2,1)}, bf16[288,384]{1,0:T(8,128)(2,1)S(1)}, u32[]{:S(2)}, u32[]{:S(2)}) collective-permute-start(bf16[288,384]{1,0:T(8,128)(2,1)} %get-tuple-element.15), channel_id=1, source_target_pairs={{0,4},{4,0},{8,12},{12,8},{1,5},{5,1},{9,13},{13,9},{2,6},{6,2},{1... | collective-permute-start | bytes 663560 | tf_op jit(solution)/shard_map/ppermute | solution.py:346
  4.9 0.1 collective-permute-start.4
  5.0 6.4 %collective-permute-done.3.refs_4_ = bf16[288,384]{1,0:T(8,128)(2,1)S(1)} collective-permute-done((bf16[288,384]{1,0:T(8,128)(2,1)}, bf16[288,384]{1,0:T(8,128)(2,1)S(1)}, u32[]{:S(2)}, u32[]{:S(2)}) %collective-permute-start.3) | collective-permute-done | bytes 221216 | tf_op jit(solution)/shard_map/ppermute | solution.py:346
  11.4 1.9 %collective-permute-start.5 = (bf16[288,384]{1,0:T(8,128)(2,1)S(1)}, bf16[288,384]{1,0:T(8,128)(2,1)S(1)}, u32[]{:S(2)}, u32[]{:S(2)}) collective-permute-start(bf16[288,384]{1,0:T(8,128)(2,1)S(1)} %collective-permute-done.3.refs_4_), channel_id=1, source_target_pairs={{0,2},{1,3},{2,0},{3,1},{4,6},{5,7},{6,4},{7,5},{8,10},{9,11},{10,... | collective-permute-start | bytes 663560 | tf_op jit(solution)/shard_map/ppermute | solution.py:324
  13.4 2.0 %collective-permute-done.4.refs_5_ = bf16[288,384]{1,0:T(8,128)(2,1)S(1)} collective-permute-done((bf16[288,384]{1,0:T(8,128)(2,1)}, bf16[288,384]{1,0:T(8,128)(2,1)S(1)}, u32[]{:S(2)}, u32[]{:S(2)}) %collective-permute-start.4) | collective-permute-done | bytes 221216 | tf_op jit(solution)/shard_map/ppermute | solution.py:346
  15.3 1.7 %collective-permute-start.6 = (bf16[288,384]{1,0:T(8,128)(2,1)S(1)}, bf16[288,384]{1,0:T(8,128)(2,1)S(1)}, u32[]{:S(2)}, u32[]{:S(2)}) collective-permute-start(bf16[288,384]{1,0:T(8,128)(2,1)S(1)} %collective-permute-done.4.refs_5_), channel_id=1, source_target_pairs={{0,2},{1,3},{2,0},{3,1},{4,6},{5,7},{6,4},{7,5},{8,10},{9,11},{10,... | collective-permute-start | bytes 663560 | tf_op jit(solution)/shard_map/ppermute | solution.py:324
  17.0 1.8 %pack_queries.1 = (bf16[32,3072]{1,0:T(8,128)(2,1)}, bf16[32,3072]{1,0:T(8,128)(2,1)}) custom-call(bf16[32,4096]{1,0:T(8,128)(2,1)} %nope_ref.1, bf16[32,2048]{1,0:T(8,128)(2,1)} %rope_ref.1), custom_call_target="tpu_custom_call" | custom-call | tf_op jit(solution)/shard_map/pack_queries/pallas_call | solution.py:335
  18.8 2.7 %collective-permute-start.1 = (bf16[32,3072]{1,0:T(8,128)(2,1)}, bf16[32,3072]{1,0:T(8,128)(2,1)S(1)}, u32[]{:S(2)}, u32[]{:S(2)}) collective-permute-start(bf16[32,3072]{1,0:T(8,128)(2,1)} %get-tuple-element.13.refs_0_), channel_id=1, source_target_pairs={{0,8},{4,12},{8,0},{12,4},{1,9},{5,13},{9,1},{13,5},{2,10},{6,14},... | collective-permute-start | bytes 589832 | tf_op jit(solution)/shard_map/ppermute | solution.py:321
  21.4 1.6 %collective-permute-start.2 = (bf16[32,3072]{1,0:T(8,128)(2,1)}, bf16[32,3072]{1,0:T(8,128)(2,1)S(1)}, u32[]{:S(2)}, u32[]{:S(2)}) collective-permute-start(bf16[32,3072]{1,0:T(8,128)(2,1)} %get-tuple-element.14), channel_id=1, source_target_pairs={{0,4},{4,8},{8,12},{12,0},{1,5},{5,9},{9,13},{13,1},{2,6},{6,10},{... | collective-permute-start | bytes 589832 | tf_op jit(solution)/shard_map/ppermute | solution.py:321
  23.0 10.9 %collective-permute-done.1.refs_2_ = bf16[32,3072]{1,0:T(8,128)(2,1)S(1)} collective-permute-done((bf16[32,3072]{1,0:T(8,128)(2,1)}, bf16[32,3072]{1,0:T(8,128)(2,1)S(1)}, u32[]{:S(2)}, u32[]{:S(2)}) %collective-permute-start.1) | collective-permute-done | bytes 196640 | tf_op jit(solution)/shard_map/ppermute | solution.py:321
  33.9 0.5 collective-permute-start.9
  34.4 0.1 collective-permute-start.10
  34.5 7.4 %collective-permute-done.refs_1_ = bf16[32,3072]{1,0:T(8,128)(2,1)S(1)} collective-permute-done((bf16[32,3072]{1,0:T(8,128)(2,1)}, bf16[32,3072]{1,0:T(8,128)(2,1)S(1)}, u32[]{:S(2)}, u32[]{:S(2)}) %collective-permute-start) | collective-permute-done | bytes 196640 | tf_op jit(solution)/shard_map/ppermute | solution.py:321
  42.1 0.6 copy-done.13
  42.6 0.1 copy-done.7
  42.9 0.1 copy-done.10
  43.0 10.7 %attend.1 = (bf16[32,2176]{1,0:T(8,128)(2,1)}, bf16[32,2176]{1,0:T(8,128)(2,1)}, bf16[32,2176]{1,0:T(8,128)(2,1)}, bf16[32,2176]{1,0:T(8,128)(2,1)}) custom-call(s32[4]{0:T(128)} %counts_ref.1, s32[1,128]{1,0:T(1,128)} %bitcast.5, s32[1,128]{1,0:T(1,128)} %bitcast.6, bf16[32,3072]{1,0:T(8,128)(2,1)} %get-tuple-element.13.refs_0_, ...), custom_call_target="tpu_custom_call" | custom-call | flops 8000000000 | bytes 8000000 | tf_op jit(solution)/shard_map/attend/pallas_call | solution.py:354
  53.7 9.7 %collective-permute-start.11 = (bf16[32,2176]{1,0:T(8,128)(2,1)}, bf16[32,2176]{1,0:T(8,128)(2,1)S(1)}, u32[]{:S(2)}, u32[]{:S(2)}) collective-permute-start(bf16[32,2176]{1,0:T(8,128)(2,1)} %get-tuple-element.18), channel_id=1, source_target_pairs={{0,12},{4,0},{8,4},{12,8},{1,13},{5,1},{9,5},{13,9},{2,14},{6,2},{... | collective-permute-start | bytes 417800 | tf_op jit(solution)/shard_map/ppermute | solution.py:321
  63.5 1.3 %collective-permute-start.13 = (bf16[32,2176]{1,0:T(8,128)(2,1)}, bf16[32,2176]{1,0:T(8,128)(2,1)S(1)}, u32[]{:S(2)}, u32[]{:S(2)}) collective-permute-start(bf16[32,2176]{1,0:T(8,128)(2,1)} %get-tuple-element.20), channel_id=1, source_target_pairs={{0,4},{4,8},{8,12},{12,0},{1,5},{5,9},{9,13},{13,1},{2,6},{6,10},{... | collective-permute-start | bytes 417800 | tf_op jit(solution)/shard_map/ppermute | solution.py:321
  64.7 3.1 %collective-permute-done.11.refs_1_ = bf16[32,2176]{1,0:T(8,128)(2,1)S(1)} collective-permute-done((bf16[32,2176]{1,0:T(8,128)(2,1)}, bf16[32,2176]{1,0:T(8,128)(2,1)S(1)}, u32[]{:S(2)}, u32[]{:S(2)}) %collective-permute-start.11) | collective-permute-done | bytes 139296 | tf_op jit(solution)/shard_map/ppermute | solution.py:321
  67.9 7.4 %collective-permute-done.12.refs_2_ = bf16[32,2176]{1,0:T(8,128)(2,1)S(1)} collective-permute-done((bf16[32,2176]{1,0:T(8,128)(2,1)}, bf16[32,2176]{1,0:T(8,128)(2,1)S(1)}, u32[]{:S(2)}, u32[]{:S(2)}) %collective-permute-start.12) | collective-permute-done | bytes 139296 | tf_op jit(solution)/shard_map/ppermute | solution.py:321
  75.2 0.6 copy-done.1
  75.9 2.4 %merge.1 = bf16[32,4096]{1,0:T(8,128)(2,1)} custom-call(bf16[32,2176]{1,0:T(8,128)(2,1)} %get-tuple-element.17.refs_0_, bf16[32,2176]{1,0:T(8,128)(2,1)} %copy-done, bf16[32,2176]{1,0:T(8,128)(2,1)} %copy-done.1, bf16[32,2176]{1,0:T(8,128)(2,1)} %copy-done.2), custom_call_target="tpu_custom_call" | custom-call | tf_op jit(solution)/shard_map/merge/pallas_call | solution.py:361
  (36 shorter events, 0.3 us)
Async XLA Ops:
  1.8 9.6 %collective-permute-start.3 = (bf16[288,384]{1,0:T(8,128)(2,1)}, bf16[288,384]{1,0:T(8,128)(2,1)S(1)}, u32[]{:S(2)}, u32[]{:S(2)}) collective-permute-start(bf16[288,384]{1,0:T(8,128)(2,1)} %get-tuple-element.15), channel_id=1, source_target_pairs={{0,4},{4,0},{8,12},{12,8},{1,5},{5,1},{9,13},{13,9},{2,6},{6,2},{1... | collective-permute-start | bytes 663560 | tf_op jit(solution)/shard_map/ppermute | solution.py:346
  4.9 10.4 %collective-permute-start.4 = (bf16[288,384]{1,0:T(8,128)(2,1)}, bf16[288,384]{1,0:T(8,128)(2,1)S(1)}, u32[]{:S(2)}, u32[]{:S(2)}) collective-permute-start(bf16[288,384]{1,0:T(8,128)(2,1)} %get-tuple-element.16), channel_id=1, source_target_pairs={{0,4},{4,0},{8,12},{12,8},{1,5},{5,1},{9,13},{13,9},{2,6},{6,2},{1... | collective-permute-start | bytes 663560 | tf_op jit(solution)/shard_map/ppermute | solution.py:346
  11.4 30.6 %copy-start.3 = (bf16[288,384]{1,0:T(8,128)(2,1)}, bf16[288,384]{1,0:T(8,128)(2,1)S(1)}, u32[]{:S(2)}) copy-start(bf16[288,384]{1,0:T(8,128)(2,1)S(1)} %collective-permute-done.3.refs_4_) | copy-start | bytes 663556
  11.4 22.4 %collective-permute-start.5 = (bf16[288,384]{1,0:T(8,128)(2,1)S(1)}, bf16[288,384]{1,0:T(8,128)(2,1)S(1)}, u32[]{:S(2)}, u32[]{:S(2)}) collective-permute-start(bf16[288,384]{1,0:T(8,128)(2,1)S(1)} %collective-permute-done.3.refs_4_), channel_id=1, source_target_pairs={{0,2},{1,3},{2,0},{3,1},{4,6},{5,7},{6,4},{7,5},{8,10},{9,11},{10,... | collective-permute-start | bytes 663560 | tf_op jit(solution)/shard_map/ppermute | solution.py:324
  15.3 26.7 %copy-start.4 = (bf16[288,384]{1,0:T(8,128)(2,1)}, bf16[288,384]{1,0:T(8,128)(2,1)S(1)}, u32[]{:S(2)}) copy-start(bf16[288,384]{1,0:T(8,128)(2,1)S(1)} %collective-permute-done.4.refs_5_) | copy-start | bytes 663556
  15.3 19.1 %collective-permute-start.6 = (bf16[288,384]{1,0:T(8,128)(2,1)S(1)}, bf16[288,384]{1,0:T(8,128)(2,1)S(1)}, u32[]{:S(2)}, u32[]{:S(2)}) collective-permute-start(bf16[288,384]{1,0:T(8,128)(2,1)S(1)} %collective-permute-done.4.refs_5_), channel_id=1, source_target_pairs={{0,2},{1,3},{2,0},{3,1},{4,6},{5,7},{6,4},{7,5},{8,10},{9,11},{10,... | collective-permute-start | bytes 663560 | tf_op jit(solution)/shard_map/ppermute | solution.py:324
  18.8 15.1 %collective-permute-start.1 = (bf16[32,3072]{1,0:T(8,128)(2,1)}, bf16[32,3072]{1,0:T(8,128)(2,1)S(1)}, u32[]{:S(2)}, u32[]{:S(2)}) collective-permute-start(bf16[32,3072]{1,0:T(8,128)(2,1)} %get-tuple-element.13.refs_0_), channel_id=1, source_target_pairs={{0,8},{4,12},{8,0},{12,4},{1,9},{5,13},{9,1},{13,5},{2,10},{6,14},... | collective-permute-start | bytes 589832 | tf_op jit(solution)/shard_map/ppermute | solution.py:321
  21.4 13.1 %collective-permute-start.2 = (bf16[32,3072]{1,0:T(8,128)(2,1)}, bf16[32,3072]{1,0:T(8,128)(2,1)S(1)}, u32[]{:S(2)}, u32[]{:S(2)}) collective-permute-start(bf16[32,3072]{1,0:T(8,128)(2,1)} %get-tuple-element.14), channel_id=1, source_target_pairs={{0,4},{4,8},{8,12},{12,0},{1,5},{5,9},{9,13},{13,1},{2,6},{6,10},{... | collective-permute-start | bytes 589832 | tf_op jit(solution)/shard_map/ppermute | solution.py:321
  23.0 18.9 %collective-permute-start.7 = (bf16[288,384]{1,0:T(8,128)(2,1)S(1)}, bf16[288,384]{1,0:T(8,128)(2,1)S(1)}, u32[]{:S(2)}, u32[]{:S(2)}) collective-permute-start(bf16[288,384]{1,0:T(8,128)(2,1)S(1)} %collective-permute-done.3.refs_4_), channel_id=1, source_target_pairs={{0,1},{1,0},{2,3},{3,2},{4,5},{5,4},{6,7},{7,6},{8,9},{9,8},{10,11... | collective-permute-start | bytes 663560 | tf_op jit(solution)/shard_map/ppermute | solution.py:324
  33.9 8.1 %copy-start.11 = (bf16[32,3072]{1,0:T(8,128)(2,1)}, bf16[32,3072]{1,0:T(8,128)(2,1)S(1)}, u32[]{:S(2)}) copy-start(bf16[32,3072]{1,0:T(8,128)(2,1)S(1)} %collective-permute-done.1.refs_2_) | copy-start | bytes 589828
  33.9 8.1 %collective-permute-start.8 = (bf16[288,384]{1,0:T(8,128)(2,1)S(1)}, bf16[288,384]{1,0:T(8,128)(2,1)S(1)}, u32[]{:S(2)}, u32[]{:S(2)}) collective-permute-start(bf16[288,384]{1,0:T(8,128)(2,1)S(1)} %collective-permute-done.4.refs_5_), channel_id=1, source_target_pairs={{0,1},{1,0},{2,3},{3,2},{4,5},{5,4},{6,7},{7,6},{8,9},{9,8},{10,11... | collective-permute-start | bytes 663560 | tf_op jit(solution)/shard_map/ppermute | solution.py:324
  33.9 8.1 %copy-start.5 = (bf16[288,384]{1,0:T(8,128)(2,1)}, bf16[288,384]{1,0:T(8,128)(2,1)S(1)}, u32[]{:S(2)}) copy-start(bf16[288,384]{1,0:T(8,128)(2,1)S(1)} %collective-permute-done.5.refs_6_) | copy-start | bytes 663556
  33.9 8.1 %collective-permute-start.9 = (bf16[288,384]{1,0:T(8,128)(2,1)S(1)}, bf16[288,384]{1,0:T(8,128)(2,1)S(1)}, u32[]{:S(2)}, u32[]{:S(2)}) collective-permute-start(bf16[288,384]{1,0:T(8,128)(2,1)S(1)} %collective-permute-done.5.refs_6_), channel_id=1, source_target_pairs={{0,1},{1,0},{2,3},{3,2},{4,5},{5,4},{6,7},{7,6},{8,9},{9,8},{10,11... | collective-permute-start | bytes 663560 | tf_op jit(solution)/shard_map/ppermute | solution.py:324
  34.4 7.6 %copy-start.6 = (bf16[288,384]{1,0:T(8,128)(2,1)}, bf16[288,384]{1,0:T(8,128)(2,1)S(1)}, u32[]{:S(2)}) copy-start(bf16[288,384]{1,0:T(8,128)(2,1)S(1)} %collective-permute-done.6.refs_7_) | copy-start | bytes 663556
  34.4 7.6 %collective-permute-start.10 = (bf16[288,384]{1,0:T(8,128)(2,1)S(1)}, bf16[288,384]{1,0:T(8,128)(2,1)S(1)}, u32[]{:S(2)}, u32[]{:S(2)}) collective-permute-start(bf16[288,384]{1,0:T(8,128)(2,1)S(1)} %collective-permute-done.6.refs_7_), channel_id=1, source_target_pairs={{0,1},{1,0},{2,3},{3,2},{4,5},{5,4},{6,7},{7,6},{8,9},{9,8},{10,11... | collective-permute-start | bytes 663560 | tf_op jit(solution)/shard_map/ppermute | solution.py:324
  34.5 7.6 %copy-start.12 = (bf16[32,3072]{1,0:T(8,128)(2,1)}, bf16[32,3072]{1,0:T(8,128)(2,1)S(1)}, u32[]{:S(2)}) copy-start(bf16[32,3072]{1,0:T(8,128)(2,1)S(1)} %collective-permute-done.2.refs_3_) | copy-start | bytes 589828
  34.5 7.4 %collective-permute-start = (bf16[32,3072]{1,0:T(8,128)(2,1)}, bf16[32,3072]{1,0:T(8,128)(2,1)S(1)}, u32[]{:S(2)}, u32[]{:S(2)}) collective-permute-start(bf16[32,3072]{1,0:T(8,128)(2,1)} %get-tuple-element.14), channel_id=1, source_target_pairs={{0,12},{4,0},{8,4},{12,8},{1,13},{5,1},{9,5},{13,9},{2,14},{6,2},{... | collective-permute-start | bytes 589832 | tf_op jit(solution)/shard_map/ppermute | solution.py:321
  41.9 0.8 %copy-start.8 = (bf16[288,384]{1,0:T(8,128)(2,1)}, bf16[288,384]{1,0:T(8,128)(2,1)S(1)}, u32[]{:S(2)}) copy-start(bf16[288,384]{1,0:T(8,128)(2,1)S(1)} %collective-permute-done.8.refs_9_) | copy-start | bytes 663556
  42.0 0.9 %copy-start.9 = (bf16[288,384]{1,0:T(8,128)(2,1)}, bf16[288,384]{1,0:T(8,128)(2,1)S(1)}, u32[]{:S(2)}) copy-start(bf16[288,384]{1,0:T(8,128)(2,1)S(1)} %collective-permute-done.9.refs_10_) | copy-start | bytes 663556
  42.0 1.0 %copy-start.10 = (bf16[288,384]{1,0:T(8,128)(2,1)}, bf16[288,384]{1,0:T(8,128)(2,1)S(1)}, u32[]{:S(2)}) copy-start(bf16[288,384]{1,0:T(8,128)(2,1)S(1)} %collective-permute-done.10.refs_11_) | copy-start | bytes 663556
  53.7 14.1 %collective-permute-start.11 = (bf16[32,2176]{1,0:T(8,128)(2,1)}, bf16[32,2176]{1,0:T(8,128)(2,1)S(1)}, u32[]{:S(2)}, u32[]{:S(2)}) collective-permute-start(bf16[32,2176]{1,0:T(8,128)(2,1)} %get-tuple-element.18), channel_id=1, source_target_pairs={{0,12},{4,0},{8,4},{12,8},{1,13},{5,1},{9,5},{13,9},{2,14},{6,2},{... | collective-permute-start | bytes 417800 | tf_op jit(solution)/shard_map/ppermute | solution.py:321
  63.5 11.8 %collective-permute-start.12 = (bf16[32,2176]{1,0:T(8,128)(2,1)}, bf16[32,2176]{1,0:T(8,128)(2,1)S(1)}, u32[]{:S(2)}, u32[]{:S(2)}) collective-permute-start(bf16[32,2176]{1,0:T(8,128)(2,1)} %get-tuple-element.19), channel_id=1, source_target_pairs={{0,8},{4,12},{8,0},{12,4},{1,9},{5,13},{9,1},{13,5},{2,10},{6,14},... | collective-permute-start | bytes 417800 | tf_op jit(solution)/shard_map/ppermute | solution.py:321
  63.5 11.8 %collective-permute-start.13 = (bf16[32,2176]{1,0:T(8,128)(2,1)}, bf16[32,2176]{1,0:T(8,128)(2,1)S(1)}, u32[]{:S(2)}, u32[]{:S(2)}) collective-permute-start(bf16[32,2176]{1,0:T(8,128)(2,1)} %get-tuple-element.20), channel_id=1, source_target_pairs={{0,4},{4,8},{8,12},{12,0},{1,5},{5,9},{9,13},{13,1},{2,6},{6,10},{... | collective-permute-start | bytes 417800 | tf_op jit(solution)/shard_map/ppermute | solution.py:321
  67.9 7.4 %copy-start = (bf16[32,2176]{1,0:T(8,128)(2,1)}, bf16[32,2176]{1,0:T(8,128)(2,1)S(1)}, u32[]{:S(2)}) copy-start(bf16[32,2176]{1,0:T(8,128)(2,1)S(1)} %collective-permute-done.11.refs_1_) | copy-start | bytes 417796
  (4 other events, 2.8 us)

commit v8 on v7

--- a/solution.py
+++ b/solution.py
@@ -11,7 +11,7 @@
 PAGE = 64
 GROUP = 2
 LANES = 4
-BLOCK_PAGES = 4
+BLOCK_PAGES = 8
 PIECES = 2
 HALVES = 2
 
@@ -62,7 +62,7 @@
     part_refs, refs = refs[:LANES * PIECES], refs[LANES * PIECES:]
     own_ref, keys_hbm, values_hbm = refs[:3]
     out_refs, refs = refs[3:3 + members], refs[3 + members:]
-    raw, turned, wk, wv, tiles, bias, qs, sbuf, mx, den, acc, sums, flat, sems, own_sems, part_sems = refs
+    turned, wk, wv, tiles, bias, qs, sbuf, mx, den, acc, sums, flat, sems, own_sems = refs
     local_rows = rows // members
     block = BLOCK_PAGES * PAGE
     cols = slots * PAGE
@@ -79,33 +79,27 @@
     own_blocks = (own_live + BLOCK_PAGES - 1) // BLOCK_PAGES
     part_blocks = (part_live + BLOCK_PAGES - 1) // BLOCK_PAGES
 
-    query_copies = [
-        pltpu.make_async_copy(q, raw.at[pl.ds(s * local_rows, local_rows)], sems.at[2 + s])
-        for s, q in enumerate(q_refs)
-    ]
-    key_copy = pltpu.make_async_copy(keys_hbm.at[pl.ds(mine * hh, hh)], wk, sems.at[0])
-    value_copy = pltpu.make_async_copy(values_hbm.at[pl.ds(mine * hh, hh)], wv, sems.at[1])
     tile_copies = []
     for b in range(-(-cols // block)):
         at = pl.ds(b * block, min(block, cols - b * block))
         tile_copies.append((b < own_blocks, pltpu.make_async_copy(own_ref.at[:, at], tiles.at[:, at], own_sems.at[b])))
+    key_copy = pltpu.make_async_copy(keys_hbm.at[pl.ds(mine * hh, hh)], wk, sems.at[0])
+    value_copy = pltpu.make_async_copy(values_hbm.at[pl.ds(mine * hh, hh)], wv, sems.at[1])
+    key_copy.start()
+    for used, copy in tile_copies:
+        pl.when(used)(copy.start)
     for i, flip in enumerate((0, 2, 1, 3)):
         quarter = lane_id ^ flip
         at = pl.multiple_of(cols + quarter * quarter_cols, 128)
-        for p in range(PIECES):
-            tile_copies.append((
-                quarter * quarter_cols < part_blocks * block,
-                pltpu.make_async_copy(
-                    part_refs[i * PIECES + p],
-                    tiles.at[pl.ds(p * depth, depth), pl.ds(at, quarter_cols)],
-                    part_sems.at[i * PIECES + p],
-                ),
-            ))
-    for copy in query_copies + [key_copy]:
-        copy.start()
-    for used, copy in tile_copies:
-        pl.when(used)(copy.start)
-    value_copy.start()
+
+        @pl.when(quarter * quarter_cols < part_blocks * block)
+        def _(i=i, at=at):
+            for p in range(PIECES):
+                tiles[p * depth:(p + 1) * depth, pl.ds(at, quarter_cols)] = part_refs[i * PIECES + p][...]
+
+    mx[...] = jnp.full(mx.shape, FLOOR, jnp.float32)
+    den[...] = jnp.zeros_like(den)
+    acc[...] = jnp.zeros_like(acc)
 
     across = lax.broadcasted_iota(jnp.int32, (rows, rows), 1)
     down = lax.broadcasted_iota(jnp.int32, (rows, rows), 0)
@@ -150,9 +144,8 @@
         return carry
 
     lax.fori_loop(0, reach[-1][1], fill_bias, 0)
-    for copy in query_copies:
-        copy.wait()
-    turned[...] = jnp.dot(order, raw[...], preferred_element_type=jnp.float32).astype(jnp.bfloat16)
+    whole = jnp.concatenate([q[...] for q in q_refs], axis=0)
+    turned[...] = jnp.dot(order, whole, preferred_element_type=jnp.float32).astype(jnp.bfloat16)
     key_copy.wait()
     for h in range(hh):
         lat = jnp.dot(turned[:, h * nope:(h + 1) * nope], wk[h], preferred_element_type=jnp.float32)
@@ -162,7 +155,7 @@
             to = slice(g * group_rows + h * half, g * group_rows + (h + 1) * half)
             qs[to, :latent] = lat[g * half:(g + 1) * half]
             qs[to, latent:] = turned[g * half:(g + 1) * half, at:at + rope]
-    mx[...] = jnp.full(mx.shape, FLOOR, jnp.float32)
+    value_copy.start()
     for used, copy in tile_copies:
         pl.when(used)(copy.wait)
 
@@ -175,14 +168,14 @@
         for h in range(hh):
             part = slice(h * half, (h + 1) * half)
             value = scores[part] + shut
-            sbuf[g, part, pl.ds(pl.multiple_of(b * block, 128), block)] = value
+            sbuf[part, pl.ds(pl.multiple_of(b * block, 128), block)] = value
             top = functools.reduce(jnp.maximum, [value[:, i:i + 128] for i in range(0, block, 128)])
             mx[g, part] = jnp.maximum(mx[g, part], top)
 
     def gather(g, b, top):
-        weights = jnp.exp2((sbuf[g, :, pl.ds(pl.multiple_of(b * block, 128), block)] - top) * scale2)
-        den[...] += functools.reduce(jnp.add, [weights[:, i:i + 128] for i in range(0, block, 128)])
-        acc[...] += lax.dot_general(
+        weights = jnp.exp2((sbuf[:, pl.ds(pl.multiple_of(b * block, 128), block)] - top) * scale2)
+        den[g] += functools.reduce(jnp.add, [weights[:, i:i + 128] for i in range(0, block, 128)])
+        acc[g] += lax.dot_general(
             weights.astype(jnp.bfloat16),
             tiles[:latent, pl.ds(place(g, b), block)],
             (((1,), (1,)), ((), ())),
@@ -192,12 +185,12 @@
     stats = []
 
     def close(g, top):
-        total = jnp.sum(den[...], axis=1, keepdims=True)
+        total = jnp.sum(den[g], axis=1, keepdims=True)
         seen = top > 0.5 * FLOOR
         total = jnp.where(seen, total, 1.0)
         stats.append((jnp.where(seen, 1.0 / total, 0.0), jnp.where(seen, top * scale2 + jnp.log2(total), FLOOR)))
         for h in range(hh):
-            sums[h, g * half:(g + 1) * half] = acc[h * half:(h + 1) * half].astype(jnp.bfloat16)
+            sums[h, g * half:(g + 1) * half] = acc[g, h * half:(h + 1) * half].astype(jnp.bfloat16)
 
     def each(low, high, *steps):
         def body(b, carry):
@@ -210,10 +203,8 @@
     each(0, reach[0][1], lambda b: score(0, b))
     for g in range(HALVES):
         top = jnp.max(mx[g], axis=1, keepdims=True)
-        den[...] = jnp.zeros_like(den)
-        acc[...] = jnp.zeros_like(acc)
         if g + 1 < HALVES:
-            each(0, reach[g][1], lambda b: score(g + 1, b), lambda b: gather(g, b, top))
+            each(0, reach[g][1], lambda b: gather(g, b, top), lambda b: score(g + 1, b))
             each(reach[g][1], reach[g + 1][1], lambda b: score(g + 1, b))
         else:
             each(0, reach[g][1], lambda b: gather(g, b, top))
@@ -252,27 +243,25 @@
     return pl.pallas_call(
         functools.partial(attend_kernel, (members, hh, nope, rope, latent, vhead, rows, slots)),
         out_shape=[jax.ShapeDtypeStruct((local_rows, packed), bf16)] * members,
-        in_specs=[pl.BlockSpec(memory_space=pltpu.SMEM), vmem, vmem] + [hbm] * (members + LANES * PIECES + 3),
+        in_specs=[pl.BlockSpec(memory_space=pltpu.SMEM)] + [vmem] * (2 + members + LANES * PIECES) + [hbm] * 3,
         out_specs=[vmem] * members,
         scratch_shapes=[
-            pltpu.VMEM((rows, hh * (nope + rope)), bf16),
             pltpu.VMEM((rows, hh * (nope + rope)), bf16),
             pltpu.VMEM((hh, nope, latent), bf16),
             pltpu.VMEM((hh, latent, vhead), bf16),
             pltpu.VMEM((full, 2 * cols), bf16),
             pltpu.VMEM((rows, 2 * cols), f32),
             pltpu.VMEM((HALVES * group_rows, full), bf16),
-            pltpu.VMEM((HALVES, group_rows, 2 * own_blocks * block), f32),
+            pltpu.VMEM((group_rows, 2 * own_blocks * block), f32),
             pltpu.VMEM((HALVES, group_rows, 128), f32),
-            pltpu.VMEM((group_rows, 128), f32),
-            pltpu.VMEM((group_rows, latent), f32),
+            pltpu.VMEM((HALVES, group_rows, 128), f32),
+            pltpu.VMEM((HALVES, group_rows, latent), f32),
             pltpu.VMEM((hh, rows, latent), bf16),
             pltpu.VMEM((rows, packed), bf16),
-            pltpu.SemaphoreType.DMA((2 + members,)),
+            pltpu.SemaphoreType.DMA((2,)),
             pltpu.SemaphoreType.DMA((own_blocks,)),
-            pltpu.SemaphoreType.DMA((LANES * PIECES,)),
         ],
-        compiler_params=pltpu.CompilerParams(vmem_limit_bytes=58 << 20),
+        compiler_params=pltpu.CompilerParams(vmem_limit_bytes=48 << 20),
         cost_estimate=pl.CostEstimate(flops=8 * 10**9, bytes_accessed=8 * 10**6, transcendentals=0),
         name="attend",
     )
@@ -330,6 +319,7 @@
         in_specs=[hbm],
         out_specs=[vmem] * PIECES,
         scratch_shapes=[pltpu.SemaphoreType.DMA((PIECES,))],
+        compiler_params=pltpu.CompilerParams(vmem_limit_bytes=8 << 20),
         name="pack_pages",
     )(turned)
     shares = pl.pallas_call(
@@ -338,6 +328,8 @@
         in_specs=[hbm] * 2,
         out_specs=[vmem] * GROUP,
         scratch_shapes=[pltpu.SemaphoreType.DMA((2 * GROUP,))],
+        cost_estimate=pl.CostEstimate(flops=3 * 10**10, bytes_accessed=10**6, transcendentals=0),
+        compiler_params=pltpu.CompilerParams(vmem_limit_bytes=8 << 20),
         name="pack_queries",
     )(q_nope, q_rope)
 
@@ -363,6 +355,7 @@
         out_shape=jax.ShapeDtypeStruct((local_rows, heads_here * vhead), bf16),
         in_specs=[vmem] * members,
         out_specs=vmem,
+        compiler_params=pltpu.CompilerParams(vmem_limit_bytes=16 << 20),
         name="merge",
     )(*arrived)
 

time: 78.8 us -> 73.2 us (0.929)
  Pallas kernels: 16.8 us -> 13.1 us
  starting transfers between devices: 22.6 us -> 20.2 us
  local copies, waits for them, and re-layouts: 1.64 us -> 3.34 us
  waiting for transfers between devices: 37.2 us -> 36.2 us
    ppermute x6, starting transfers between devices: 15.2 us -> 12.8 us  [over_pages(): lax.ppermute(x, 'pages', [(i, (i - s) % members) for i in range(members)])]
    pallas_call x1, Pallas kernels: 1.82 us -> 0.07 us  [on_device(): pl.pallas_call(functools.partial(pack_pages_kernel, cols // LANES), out_s...]
    unnamed x28 -> x14, local copies, waits for them, and re-layouts: 1.64 us -> 3.34 us
    pallas_call x1, Pallas kernels: 1.78 us -> 0.16 us  [on_device(): pl.pallas_call(functools.partial(pack_queries_kernel, (hh * nope, hh * ro...]
    pallas_call x1, Pallas kernels: 2.44 us -> 1.33 us  [on_device(): pl.pallas_call(functools.partial(merge_kernel, (hh, vhead, members)), out...]
  transfers between devices with their start and end apart: 14 -> 14, of which waited for: 6 -> 6; matrix products, arithmetic and copies ran while one was open for 0% -> 0% of each run, Pallas kernels for 2% -> 0%
where the time goes in v8:
time: 73.2 us; the launch traced here: 72.9 us
  waiting for transfers between devices  36.2 us (49%)
  starting transfers between devices  20.2 us (28%)
  Pallas kernels  13.1 us (18%)
  local copies, waits for them, and re-layouts  3.34 us (5%)
    ppermute x6, waiting for transfers between devices, over_pages(): lax.ppermute(x, 'pages', [(i, (i - s) % members) for i in range(members)])  28.1 us
    ppermute x6, starting transfers between devices, over_pages(): lax.ppermute(x, 'pages', [(i, (i - s) % members) for i in range(members)])  12.8 us
    pallas_call x1, Pallas kernels, on_device(): attend_call(members, hh, nope, rope, latent, vhead, rows, slots)  11.5 us
    ppermute x2, waiting for transfers between devices, on_device(): lax.ppermute(pieces[p], 'pages', [(i, i ^ 1) for i in range(members)])  8.1 us
    ppermute x6, starting transfers between devices, over_heads(): return lax.ppermute(x, 'heads', [(i, i ^ bit) for i in range(devices)])  4.17 us
    unnamed x14, local copies, waits for them, and re-layouts  3.34 us
    ppermute x2, starting transfers between devices, on_device(): lax.ppermute(pieces[p], 'pages', [(i, i ^ 1) for i in range(members)])  3.23 us
  transfers between devices with their start and end apart: 14, of which 6 were waited for; matrix products, arithmetic and copies ran while one was open for 0% of the time, Pallas kernels for 0%

profile of v8, /device:TPU:0, one launch (start us, length us, event | category | flops | bytes accessed | tf_op | source)
XLA Modules:
  0.0 72.9 jit_solution(10659733852555579297)
XLA Ops:
  0.0 1.5 %copy-done = bf16[1536,576]{0,1:T(8,128)(2,1)S(1)} copy-done((bf16[1536,576]{0,1:T(8,128)(2,1)S(1)}, bf16[1536,576]{0,1:T(8,128)(2,1)}, u32[]{:S(2)}) %copy-start) | copy-done | bytes 1769496
  1.5 0.1 pack_pages.1
  1.6 3.1 %collective-permute-start.3 = (bf16[288,384]{1,0:T(8,128)(2,1)S(1)}, bf16[288,384]{1,0:T(8,128)(2,1)S(1)}, u32[]{:S(2)}, u32[]{:S(2)}) collective-permute-start(bf16[288,384]{1,0:T(8,128)(2,1)S(1)} %get-tuple-element.15), channel_id=1, source_target_pairs={{0,4},{4,0},{8,12},{12,8},{1,5},{5,1},{9,13},{13,9},{2,6},{6,2},{1... | collective-permute-start | bytes 663560 | tf_op jit(solution)/shard_map/ppermute | solution.py:338
  4.7 0.1 collective-permute-start.4
  4.8 6.2 %collective-permute-done.3.refs_4_ = bf16[288,384]{1,0:T(8,128)(2,1)S(1)} collective-permute-done((bf16[288,384]{1,0:T(8,128)(2,1)S(1)}, bf16[288,384]{1,0:T(8,128)(2,1)S(1)}, u32[]{:S(2)}, u32[]{:S(2)}) %collective-permute-start.3) | collective-permute-done | bytes 221216 | tf_op jit(solution)/shard_map/ppermute | solution.py:338
  10.9 1.9 %collective-permute-start.5 = (bf16[288,384]{1,0:T(8,128)(2,1)S(1)}, bf16[288,384]{1,0:T(8,128)(2,1)S(1)}, u32[]{:S(2)}, u32[]{:S(2)}) collective-permute-start(bf16[288,384]{1,0:T(8,128)(2,1)S(1)} %collective-permute-done.3.refs_4_), channel_id=1, source_target_pairs={{0,2},{1,3},{2,0},{3,1},{4,6},{5,7},{6,4},{7,5},{8,10},{9,11},{10,... | collective-permute-start | bytes 663560 | tf_op jit(solution)/shard_map/ppermute | solution.py:313
  12.9 2.0 %collective-permute-done.4.refs_5_ = bf16[288,384]{1,0:T(8,128)(2,1)S(1)} collective-permute-done((bf16[288,384]{1,0:T(8,128)(2,1)S(1)}, bf16[288,384]{1,0:T(8,128)(2,1)S(1)}, u32[]{:S(2)}, u32[]{:S(2)}) %collective-permute-start.4) | collective-permute-done | bytes 221216 | tf_op jit(solution)/shard_map/ppermute | solution.py:338
  14.8 1.7 %collective-permute-start.6 = (bf16[288,384]{1,0:T(8,128)(2,1)S(1)}, bf16[288,384]{1,0:T(8,128)(2,1)S(1)}, u32[]{:S(2)}, u32[]{:S(2)}) collective-permute-start(bf16[288,384]{1,0:T(8,128)(2,1)S(1)} %collective-permute-done.4.refs_5_), channel_id=1, source_target_pairs={{0,2},{1,3},{2,0},{3,1},{4,6},{5,7},{6,4},{7,5},{8,10},{9,11},{10,... | collective-permute-start | bytes 663560 | tf_op jit(solution)/shard_map/ppermute | solution.py:313
  16.5 0.9 %copy-done.2 = bf16[32,4096]{1,0:T(8,128)(2,1)S(1)} copy-done((bf16[32,4096]{1,0:T(8,128)(2,1)S(1)}, bf16[32,4096]{1,0:T(8,128)(2,1)}, u32[]{:S(2)}) %copy-start.2) | copy-done | bytes 262168
  17.4 0.9 %copy-done.3 = bf16[32,2048]{1,0:T(8,128)(2,1)S(1)} copy-done((bf16[32,2048]{1,0:T(8,128)(2,1)S(1)}, bf16[32,2048]{1,0:T(8,128)(2,1)}, u32[]{:S(2)}) %copy-start.3) | copy-done | bytes 131096
  18.3 0.2 pack_queries.1
  18.5 2.7 %collective-permute-start.1 = (bf16[32,3072]{1,0:T(8,128)(2,1)S(1)}, bf16[32,3072]{1,0:T(8,128)(2,1)S(1)}, u32[]{:S(2)}, u32[]{:S(2)}) collective-permute-start(bf16[32,3072]{1,0:T(8,128)(2,1)S(1)} %get-tuple-element.13.refs_0_), channel_id=1, source_target_pairs={{0,8},{4,12},{8,0},{12,4},{1,9},{5,13},{9,1},{13,5},{2,10},{6,14},... | collective-permute-start | bytes 589832 | tf_op jit(solution)/shard_map/ppermute | solution.py:310
  21.2 1.6 %collective-permute-start.2 = (bf16[32,3072]{1,0:T(8,128)(2,1)S(1)}, bf16[32,3072]{1,0:T(8,128)(2,1)S(1)}, u32[]{:S(2)}, u32[]{:S(2)}) collective-permute-start(bf16[32,3072]{1,0:T(8,128)(2,1)S(1)} %get-tuple-element.14), channel_id=1, source_target_pairs={{0,4},{4,8},{8,12},{12,0},{1,5},{5,9},{9,13},{13,1},{2,6},{6,10},{... | collective-permute-start | bytes 589832 | tf_op jit(solution)/shard_map/ppermute | solution.py:310
  22.8 10.7 %collective-permute-done.1.refs_2_ = bf16[32,3072]{1,0:T(8,128)(2,1)S(1)} collective-permute-done((bf16[32,3072]{1,0:T(8,128)(2,1)S(1)}, bf16[32,3072]{1,0:T(8,128)(2,1)S(1)}, u32[]{:S(2)}, u32[]{:S(2)}) %collective-permute-start.1) | collective-permute-done | bytes 196640 | tf_op jit(solution)/shard_map/ppermute | solution.py:310
  33.4 0.0 collective-permute-start.8
  33.4 0.5 collective-permute-start.9
  33.9 0.1 collective-permute-start.10
  34.0 7.2 %collective-permute-done.refs_1_ = bf16[32,3072]{1,0:T(8,128)(2,1)S(1)} collective-permute-done((bf16[32,3072]{1,0:T(8,128)(2,1)S(1)}, bf16[32,3072]{1,0:T(8,128)(2,1)S(1)}, u32[]{:S(2)}, u32[]{:S(2)}) %collective-permute-start) | collective-permute-done | bytes 196640 | tf_op jit(solution)/shard_map/ppermute | solution.py:310
  41.3 11.5 %attend.1 = (bf16[32,2176]{1,0:T(8,128)(2,1)S(1)}, bf16[32,2176]{1,0:T(8,128)(2,1)S(1)}, bf16[32,2176]{1,0:T(8,128)(2,1)S(1)}, bf16[32,2176]{1,0:T(8,128)(2,1)S(1)}) custom-call(s32[4]{0:T(128)S(1)} %copy-done.4, s32[1,128]{1,0:T(1,128)S(1)} %bitcast.5, s32[1,128]{1,0:T(1,128)S(1)} %bitcast.6, bf16[32,3072]{1,0:T(8,128)(2,1)S(1)} %get-tuple-element.13.refs_0_, ...), custom_call_target="tpu_custom_call" | custom-call | flops 8000000000 | bytes 8000000 | tf_op jit(solution)/shard_map/attend/pallas_call | solution.py:346
  52.8 7.3 %collective-permute-start.11 = (bf16[32,2176]{1,0:T(8,128)(2,1)S(1)}, bf16[32,2176]{1,0:T(8,128)(2,1)S(1)}, u32[]{:S(2)}, u32[]{:S(2)}) collective-permute-start(bf16[32,2176]{1,0:T(8,128)(2,1)S(1)} %get-tuple-element.18), channel_id=1, source_target_pairs={{0,12},{4,0},{8,4},{12,8},{1,13},{5,1},{9,5},{13,9},{2,14},{6,2},{... | collective-permute-start | bytes 417800 | tf_op jit(solution)/shard_map/ppermute | solution.py:310
  60.1 1.3 %collective-permute-start.13 = (bf16[32,2176]{1,0:T(8,128)(2,1)S(1)}, bf16[32,2176]{1,0:T(8,128)(2,1)S(1)}, u32[]{:S(2)}, u32[]{:S(2)}) collective-permute-start(bf16[32,2176]{1,0:T(8,128)(2,1)S(1)} %get-tuple-element.20), channel_id=1, source_target_pairs={{0,4},{4,8},{8,12},{12,0},{1,5},{5,9},{9,13},{13,1},{2,6},{6,10},{... | collective-permute-start | bytes 417800 | tf_op jit(solution)/shard_map/ppermute | solution.py:310
  61.4 2.8 %collective-permute-done.11.refs_1_ = bf16[32,2176]{1,0:T(8,128)(2,1)S(1)} collective-permute-done((bf16[32,2176]{1,0:T(8,128)(2,1)S(1)}, bf16[32,2176]{1,0:T(8,128)(2,1)S(1)}, u32[]{:S(2)}, u32[]{:S(2)}) %collective-permute-start.11) | collective-permute-done | bytes 139296 | tf_op jit(solution)/shard_map/ppermute | solution.py:310
  64.2 7.4 %collective-permute-done.12.refs_2_ = bf16[32,2176]{1,0:T(8,128)(2,1)S(1)} collective-permute-done((bf16[32,2176]{1,0:T(8,128)(2,1)S(1)}, bf16[32,2176]{1,0:T(8,128)(2,1)S(1)}, u32[]{:S(2)}, u32[]{:S(2)}) %collective-permute-start.12) | collective-permute-done | bytes 139296 | tf_op jit(solution)/shard_map/ppermute | solution.py:310
  71.6 1.3 %merge.1 = bf16[32,4096]{1,0:T(8,128)(2,1)} custom-call(bf16[32,2176]{1,0:T(8,128)(2,1)S(1)} %get-tuple-element.17.refs_0_, bf16[32,2176]{1,0:T(8,128)(2,1)S(1)} %collective-permute-done.11.refs_1_, bf16[32,2176]{1,0:T(8,128)(2,1)S(1)} %collective-permute-done.12.refs_2_, bf16[32,2176]{1,0:T(8,128)(2,1)S(1)} %collective-permute-done.13.refs_3_), custom_call_target="tpu_custom_call" | custom-call | tf_op jit(solution)/shard_map/merge/pallas_call | solution.py:353
  (22 shorter events, 0.0 us)
Async XLA Ops:
  0.0 1.5 %copy-start = (bf16[1536,576]{0,1:T(8,128)(2,1)S(1)}, bf16[1536,576]{0,1:T(8,128)(2,1)}, u32[]{:S(2)}) copy-start(bf16[1536,576]{0,1:T(8,128)(2,1)} %param.10) | copy-start | bytes 5308420
  1.6 9.4 %collective-permute-start.3 = (bf16[288,384]{1,0:T(8,128)(2,1)S(1)}, bf16[288,384]{1,0:T(8,128)(2,1)S(1)}, u32[]{:S(2)}, u32[]{:S(2)}) collective-permute-start(bf16[288,384]{1,0:T(8,128)(2,1)S(1)} %get-tuple-element.15), channel_id=1, source_target_pairs={{0,4},{4,0},{8,12},{12,8},{1,5},{5,1},{9,13},{13,9},{2,6},{6,2},{1... | collective-permute-start | bytes 663560 | tf_op jit(solution)/shard_map/ppermute | solution.py:338
  4.7 36.6 %copy-start.4 = (s32[4]{0:T(128)S(1)}, s32[4]{0:T(128)}, u32[]{:S(2)}) copy-start(s32[4]{0:T(128)} %counts_ref.1) | copy-start | bytes 52
  4.7 36.6 %copy-start.5 = (s32[128]{0:T(128)S(1)}, s32[128]{0:T(128)}, u32[]{:S(2)}) copy-start(s32[128]{0:T(128)} %param.14) | copy-start | bytes 1540
  4.7 36.6 %copy-start.6 = (s32[128]{0:T(128)S(1)}, s32[128]{0:T(128)}, u32[]{:S(2)}) copy-start(s32[128]{0:T(128)} %param.15) | copy-start | bytes 1540
  4.7 36.6 %copy-start.1 = (bf16[1536,576]{0,1:T(8,128)(2,1)S(1)}, bf16[1536,576]{0,1:T(8,128)(2,1)}, u32[]{:S(2)}) copy-start(bf16[1536,576]{0,1:T(8,128)(2,1)} %param.10) | copy-start | bytes 5308420
  4.7 10.2 %collective-permute-start.4 = (bf16[288,384]{1,0:T(8,128)(2,1)S(1)}, bf16[288,384]{1,0:T(8,128)(2,1)S(1)}, u32[]{:S(2)}, u32[]{:S(2)}) collective-permute-start(bf16[288,384]{1,0:T(8,128)(2,1)S(1)} %get-tuple-element.16), channel_id=1, source_target_pairs={{0,4},{4,0},{8,12},{12,8},{1,5},{5,1},{9,13},{13,9},{2,6},{6,2},{1... | collective-permute-start | bytes 663560 | tf_op jit(solution)/shard_map/ppermute | solution.py:338
  10.9 22.5 %collective-permute-start.5 = (bf16[288,384]{1,0:T(8,128)(2,1)S(1)}, bf16[288,384]{1,0:T(8,128)(2,1)S(1)}, u32[]{:S(2)}, u32[]{:S(2)}) collective-permute-start(bf16[288,384]{1,0:T(8,128)(2,1)S(1)} %collective-permute-done.3.refs_4_), channel_id=1, source_target_pairs={{0,2},{1,3},{2,0},{3,1},{4,6},{5,7},{6,4},{7,5},{8,10},{9,11},{10,... | collective-permute-start | bytes 663560 | tf_op jit(solution)/shard_map/ppermute | solution.py:313
  14.8 19.1 %collective-permute-start.6 = (bf16[288,384]{1,0:T(8,128)(2,1)S(1)}, bf16[288,384]{1,0:T(8,128)(2,1)S(1)}, u32[]{:S(2)}, u32[]{:S(2)}) collective-permute-start(bf16[288,384]{1,0:T(8,128)(2,1)S(1)} %collective-permute-done.4.refs_5_), channel_id=1, source_target_pairs={{0,2},{1,3},{2,0},{3,1},{4,6},{5,7},{6,4},{7,5},{8,10},{9,11},{10,... | collective-permute-start | bytes 663560 | tf_op jit(solution)/shard_map/ppermute | solution.py:313
  16.5 0.9 %copy-start.2 = (bf16[32,4096]{1,0:T(8,128)(2,1)S(1)}, bf16[32,4096]{1,0:T(8,128)(2,1)}, u32[]{:S(2)}) copy-start(bf16[32,4096]{1,0:T(8,128)(2,1)} %nope_ref.1) | copy-start | bytes 786436
  17.4 0.9 %copy-start.3 = (bf16[32,2048]{1,0:T(8,128)(2,1)S(1)}, bf16[32,2048]{1,0:T(8,128)(2,1)}, u32[]{:S(2)}) copy-start(bf16[32,2048]{1,0:T(8,128)(2,1)} %rope_ref.1) | copy-start | bytes 393220
  18.5 14.9 %collective-permute-start.1 = (bf16[32,3072]{1,0:T(8,128)(2,1)S(1)}, bf16[32,3072]{1,0:T(8,128)(2,1)S(1)}, u32[]{:S(2)}, u32[]{:S(2)}) collective-permute-start(bf16[32,3072]{1,0:T(8,128)(2,1)S(1)} %get-tuple-element.13.refs_0_), channel_id=1, source_target_pairs={{0,8},{4,12},{8,0},{12,4},{1,9},{5,13},{9,1},{13,5},{2,10},{6,14},... | collective-permute-start | bytes 589832 | tf_op jit(solution)/shard_map/ppermute | solution.py:310
  21.2 12.8 %collective-permute-start.2 = (bf16[32,3072]{1,0:T(8,128)(2,1)S(1)}, bf16[32,3072]{1,0:T(8,128)(2,1)S(1)}, u32[]{:S(2)}, u32[]{:S(2)}) collective-permute-start(bf16[32,3072]{1,0:T(8,128)(2,1)S(1)} %get-tuple-element.14), channel_id=1, source_target_pairs={{0,4},{4,8},{8,12},{12,0},{1,5},{5,9},{9,13},{13,1},{2,6},{6,10},{... | collective-permute-start | bytes 589832 | tf_op jit(solution)/shard_map/ppermute | solution.py:310
  22.7 18.5 %collective-permute-start.7 = (bf16[288,384]{1,0:T(8,128)(2,1)S(1)}, bf16[288,384]{1,0:T(8,128)(2,1)S(1)}, u32[]{:S(2)}, u32[]{:S(2)}) collective-permute-start(bf16[288,384]{1,0:T(8,128)(2,1)S(1)} %collective-permute-done.3.refs_4_), channel_id=1, source_target_pairs={{0,1},{1,0},{2,3},{3,2},{4,5},{5,4},{6,7},{7,6},{8,9},{9,8},{10,11... | collective-permute-start | bytes 663560 | tf_op jit(solution)/shard_map/ppermute | solution.py:313
  33.4 7.8 %collective-permute-start.8 = (bf16[288,384]{1,0:T(8,128)(2,1)S(1)}, bf16[288,384]{1,0:T(8,128)(2,1)S(1)}, u32[]{:S(2)}, u32[]{:S(2)}) collective-permute-start(bf16[288,384]{1,0:T(8,128)(2,1)S(1)} %collective-permute-done.4.refs_5_), channel_id=1, source_target_pairs={{0,1},{1,0},{2,3},{3,2},{4,5},{5,4},{6,7},{7,6},{8,9},{9,8},{10,11... | collective-permute-start | bytes 663560 | tf_op jit(solution)/shard_map/ppermute | solution.py:313
  33.4 7.8 %collective-permute-start.9 = (bf16[288,384]{1,0:T(8,128)(2,1)S(1)}, bf16[288,384]{1,0:T(8,128)(2,1)S(1)}, u32[]{:S(2)}, u32[]{:S(2)}) collective-permute-start(bf16[288,384]{1,0:T(8,128)(2,1)S(1)} %collective-permute-done.5.refs_6_), channel_id=1, source_target_pairs={{0,1},{1,0},{2,3},{3,2},{4,5},{5,4},{6,7},{7,6},{8,9},{9,8},{10,11... | collective-permute-start | bytes 663560 | tf_op jit(solution)/shard_map/ppermute | solution.py:313
  33.9 7.3 %collective-permute-start.10 = (bf16[288,384]{1,0:T(8,128)(2,1)S(1)}, bf16[288,384]{1,0:T(8,128)(2,1)S(1)}, u32[]{:S(2)}, u32[]{:S(2)}) collective-permute-start(bf16[288,384]{1,0:T(8,128)(2,1)S(1)} %collective-permute-done.6.refs_7_), channel_id=1, source_target_pairs={{0,1},{1,0},{2,3},{3,2},{4,5},{5,4},{6,7},{7,6},{8,9},{9,8},{10,11... | collective-permute-start | bytes 663560 | tf_op jit(solution)/shard_map/ppermute | solution.py:313
  34.0 7.2 %collective-permute-start = (bf16[32,3072]{1,0:T(8,128)(2,1)S(1)}, bf16[32,3072]{1,0:T(8,128)(2,1)S(1)}, u32[]{:S(2)}, u32[]{:S(2)}) collective-permute-start(bf16[32,3072]{1,0:T(8,128)(2,1)S(1)} %get-tuple-element.14), channel_id=1, source_target_pairs={{0,12},{4,0},{8,4},{12,8},{1,13},{5,1},{9,5},{13,9},{2,14},{6,2},{... | collective-permute-start | bytes 589832 | tf_op jit(solution)/shard_map/ppermute | solution.py:310
  52.8 11.3 %collective-permute-start.11 = (bf16[32,2176]{1,0:T(8,128)(2,1)S(1)}, bf16[32,2176]{1,0:T(8,128)(2,1)S(1)}, u32[]{:S(2)}, u32[]{:S(2)}) collective-permute-start(bf16[32,2176]{1,0:T(8,128)(2,1)S(1)} %get-tuple-element.18), channel_id=1, source_target_pairs={{0,12},{4,0},{8,4},{12,8},{1,13},{5,1},{9,5},{13,9},{2,14},{6,2},{... | collective-permute-start | bytes 417800 | tf_op jit(solution)/shard_map/ppermute | solution.py:310
  60.1 11.5 %collective-permute-start.12 = (bf16[32,2176]{1,0:T(8,128)(2,1)S(1)}, bf16[32,2176]{1,0:T(8,128)(2,1)S(1)}, u32[]{:S(2)}, u32[]{:S(2)}) collective-permute-start(bf16[32,2176]{1,0:T(8,128)(2,1)S(1)} %get-tuple-element.19), channel_id=1, source_target_pairs={{0,8},{4,12},{8,0},{12,4},{1,9},{5,13},{9,1},{13,5},{2,10},{6,14},... | collective-permute-start | bytes 417800 | tf_op jit(solution)/shard_map/ppermute | solution.py:310
  60.1 11.5 %collective-permute-start.13 = (bf16[32,2176]{1,0:T(8,128)(2,1)S(1)}, bf16[32,2176]{1,0:T(8,128)(2,1)S(1)}, u32[]{:S(2)}, u32[]{:S(2)}) collective-permute-start(bf16[32,2176]{1,0:T(8,128)(2,1)S(1)} %get-tuple-element.20), channel_id=1, source_target_pairs={{0,4},{4,8},{8,12},{12,0},{1,5},{5,9},{9,13},{13,1},{2,6},{6,10},{... | collective-permute-start | bytes 417800 | tf_op jit(solution)/shard_map/ppermute | solution.py:310
